TPU v7x, 16 devices: a whole 2x2x2 slice. The times are simulated.
16 devices in a mesh: dp: 16 (over z, y, x, core).
Axes of the slice: x: 2, y: 2, z: 2, core: 2. Of those that a mesh axis runs over, the one named last changes fastest.
Arguments:
- w_in0: float32 [1024, 512], replicated
- w_short: float32 [1024, 2048], replicated
- w_in: float32 [1, 2048, 512], replicated
- w_mid: float32 [2, 3, 3, 512, 512], replicated
- w_out: float32 [2, 512, 2048], replicated
- w_fc: float32 [2048, 1000], replicated
- w_bn: float32 [16384], replicated
- w_bias: float32 [1000], replicated
- g_in0: float32 [16, 1024, 512], P('dp')
- g_short: float32 [16, 1024, 2048], P('dp')
- g_in: float32 [16, 1, 2048, 512], P('dp')
- g_mid: float32 [16, 2, 3, 3, 512, 512], P('dp')
- g_out: float32 [16, 2, 512, 2048], P('dp')
- g_bn: float32 [16, 16384], P('dp')
- pooled: bfloat16 [16384, 2048], P('dp')
- dlogits: bfloat16 [16384, 1000], P('dp')
- v_in0: float32 [524288], P('dp')
- v_short: float32 [2097152], P('dp')
- v_in: float32 [1, 1048576], P(None, 'dp')
- v_mid: float32 [2, 2359296], P(None, 'dp')
- v_out: float32 [2, 1048576], P(None, 'dp')
- v_fc: float32 [2048000], P('dp')
- v_bn: float32 [16384], P('dp')
- v_bias: float32 [1008], P('dp')
- learn_rate: float32 [], replicated
Outputs:
- output 1: float32 [1024, 512], replicated
- output 2: float32 [1024, 2048], replicated
- output 3: float32 [1, 2048, 512], replicated
- output 4: float32 [2, 3, 3, 512, 512], replicated
- output 5: float32 [2, 512, 2048], replicated
- output 6: float32 [2048, 1000], replicated
- output 7: float32 [16384], replicated
- output 8: float32 [1000], replicated
- output 9: bfloat16 [1024, 512], replicated
- output 10: bfloat16 [1024, 2048], replicated
- output 11: bfloat16 [1, 2048, 512], replicated
- output 12: bfloat16 [2, 3, 3, 512, 512], replicated
- output 13: bfloat16 [2, 512, 2048], replicated
- output 14: bfloat16 [2048, 1000], replicated
- output 15: float32 [524288], P('dp')
- output 16: float32 [2097152], P('dp')
- output 17: float32 [1, 1048576], P(None, 'dp')
- output 18: float32 [2, 2359296], P(None, 'dp')
- output 19: float32 [2, 1048576], P(None, 'dp')
- output 20: float32 [2048000], P('dp')
- output 21: float32 [16384], P('dp')
- output 22: float32 [1008], P('dp')
All inputs are finite; a program needn't handle non-finite values.
Results may differ from a plain program's by a relative error of at most 0.001.
Values sent between devices are 32-bit elements.
A program may use at most 1 GiB of HBM per device.

v0:
```python
import jax
import jax.numpy as jnp
from jax import lax
from jax.sharding import PartitionSpec as P

MOMENTUM = 0.9
TRUST_COEF = 0.001
DECAY = 0.0001


def trust_factor(sq_w, sq_g):
    w_norm = jnp.sqrt(sq_w)
    g_norm = jnp.sqrt(sq_g)
    return jnp.where((w_norm > 0) & (g_norm > 0), TRUST_COEF * w_norm / (g_norm + DECAY * w_norm), 1.0)


def solution(mesh):
    n_dev = mesh.shape['dp']
    spec_full = P()
    spec_lead = P('dp')
    spec_cols = P(None, 'dp')
    moment_specs = (spec_lead, spec_lead, spec_cols, spec_cols, spec_cols, spec_lead, spec_lead, spec_lead)
    in_specs = (spec_full,) * 8 + (spec_lead,) * 8 + moment_specs + (spec_full,)
    out_specs = (spec_full,) * 14 + moment_specs

    def body(w_in0, w_short, w_in, w_mid, w_out, w_fc, w_bn, w_bias,
             g_in0, g_short, g_in, g_mid, g_out, g_bn, pooled, dlogits,
             v_in0, v_short, v_in, v_mid, v_out, v_fc, v_bn, v_bias, learn_rate):
        rank = lax.axis_index('dp')
        rows = pooled.shape[0] * n_dev
        classes = w_bias.shape[0]
        bias_width = v_bias.shape[0]
        bias_pad = bias_width * n_dev
        bn_width = v_bn.shape[0]
        fc_local = lax.dot_general(pooled, dlogits, (((0,), (0,)), ((), ())),
                                   preferred_element_type=jnp.float32)
        bias_local = jnp.sum(dlogits, axis=0, dtype=jnp.float32)
        weights = [w_in0, w_short, w_in, w_mid, w_out, w_fc]
        moments = [v_in0, v_short, v_in, v_mid, v_out, v_fc]
        local_grads = [g_in0, g_short, g_in, g_mid, g_out, fc_local]
        divisors = [n_dev] * 5 + [rows]
        w_parts = []
        g_parts = []
        squares = []
        for weight, moment, gradient, divisor in zip(weights, moments, local_grads, divisors):
            moment_2d = moment.reshape(-1, moment.shape[-1])
            count, width = moment_2d.shape
            w_flat = weight.reshape(count, -1)
            w_part = lax.dynamic_slice_in_dim(w_flat, rank * width, width, axis=1)
            g_part = lax.psum_scatter(gradient.reshape(count, -1), 'dp', scatter_dimension=1, tiled=True) / divisor
            w_parts.append(w_part)
            g_parts.append(g_part)
            squares.append(jnp.sum(w_part * w_part, axis=1))
            squares.append(jnp.sum(g_part * g_part, axis=1))
        bn_grad = lax.psum_scatter(g_bn.reshape(-1), 'dp', scatter_dimension=0, tiled=True) / n_dev
        bias_grad = lax.psum_scatter(jnp.pad(bias_local, (0, bias_pad - classes)), 'dp',
                                     scatter_dimension=0, tiled=True) / rows
        sq_total = lax.psum(jnp.concatenate(squares), 'dp')
        offset = 0
        kernels_new = []
        kernels_bf = []
        moments_new = []
        for weight, moment, w_part, g_part in zip(weights, moments, w_parts, g_parts):
            count = w_part.shape[0]
            trust = trust_factor(sq_total[offset:offset + count], sq_total[offset + count:offset + 2 * count])[:, None]
            offset += 2 * count
            moment_next = MOMENTUM * moment.reshape(w_part.shape) + learn_rate * trust * (g_part + DECAY * w_part)
            w_full = lax.all_gather(w_part - moment_next, 'dp', axis=1, tiled=True).reshape(weight.shape)
            kernels_new.append(w_full)
            kernels_bf.append(w_full.astype(jnp.bfloat16))
            moments_new.append(moment_next.reshape(moment.shape))
        bn_moment = MOMENTUM * v_bn + learn_rate * bn_grad
        bn_part = lax.dynamic_slice_in_dim(w_bn, rank * bn_width, bn_width) - bn_moment
        bn_full = lax.all_gather(bn_part, 'dp', axis=0, tiled=True)
        bias_moment = MOMENTUM * v_bias + learn_rate * bias_grad
        w_bias_pad = jnp.pad(w_bias, (0, bias_pad - classes))
        bias_part = lax.dynamic_slice_in_dim(w_bias_pad, rank * bias_width, bias_width) - bias_moment
        bias_full = lax.all_gather(bias_part, 'dp', axis=0, tiled=True)[:classes]
        return (tuple(kernels_new) + (bn_full, bias_full) + tuple(kernels_bf)
                + tuple(moments_new) + (bn_moment, bias_moment))

    return jax.shard_map(body, mesh=mesh, in_specs=in_specs, out_specs=out_specs, check_vma=False)
```

profile of v0, /device:TPU:1, one launch (start us, length us, event | category | flops | bytes accessed | tf_op | source)
XLA Modules:
  0.0 981.3 jit_solution(17551254751860089256)
XLA Ops:
  7.2 10.8 %fusion.10 = f32[2048,1000]{1,0:T(8,128)} fusion(bf16[1024,2048]{1,0:T(8,128)(2,1)} %param.39, bf16[1024,1000]{0,1:T(8,128)(2,1)} %param.40), kind=kOutput, calls=%fused_computation.50 | convolution fusion | flops 4194304000 | bytes 14434304 | tf_op jit(solution)/shard_map/dot_general | solution.py:35
  18.1 22.2 %reshape.159 = f32[1,2048000]{1,0:T(1,128)} reshape(f32[2048,1000]{1,0:T(8,128)} %fusion.10) | data formatting | bytes 16384000 | tf_op jit(solution)/shard_map/reshape | solution.py:50
  41.9 3.5 copy.69
  45.3 11.0 %copy.71 = f32[1,1,1024,2048]{3,1,2,0:T(1,128)} copy(f32[1,1,1024,2048]{3,2,1,0:T(8,128)} %bitcast.97) | data formatting | bytes 16777216
  56.3 11.7 %copy.73 = f32[1,1,2048,512]{3,1,2,0:T(1,128)} copy(f32[1,1,2048,512]{3,2,1,0:T(8,128)S(1)} %copy-done.3) | data formatting | bytes 8388608
  68.5 32.9 %reshape.155 = f32[2,2359296]{1,0:T(2,128)} reshape(f32[1,2,3,3,512,512]{5,4,3,2,1,0:T(8,128)} %param.36) | data formatting | bytes 37748736 | tf_op jit(solution)/shard_map/reshape | solution.py:50
  101.4 15.4 %copy.76 = f32[1,2,512,2048]{3,1,2,0:T(2,128)} copy(f32[1,2,512,2048]{3,2,1,0:T(8,128)} %param.37) | data formatting | bytes 16777216
  116.8 3.8 copy.68
  121.2 10.8 %copy.70 = f32[1,1,1024,2048]{3,1,2,0:T(1,128)} copy(f32[1,1,1024,2048]{3,2,1,0:T(8,128)} %bitcast.98) | data formatting | bytes 16777216
  132.1 8.4 copy.72
  140.5 31.9 %copy.74 = f32[1,2,4608,512]{3,1,2,0:T(2,128)} copy(f32[1,2,4608,512]{3,2,1,0:T(8,128)} %bitcast.87) | data formatting | bytes 37748736
  172.4 15.4 %copy.75 = f32[1,2,512,2048]{3,1,2,0:T(2,128)} copy(f32[1,2,512,2048]{3,2,1,0:T(8,128)} %bitcast.99) | data formatting | bytes 16777216
  187.7 9.6 copy.51
  197.4 22.3 %reshape.158 = f32[1,2048000]{1,0:T(1,128)} reshape(f32[2048,1000]{1,0:T(8,128)} %copy.51) | data formatting | bytes 16384000 | tf_op jit(solution)/shard_map/reshape | solution.py:48
  221.6 34.2 %all-reduce.10 = f32[1008]{0:T(1024)S(1)} all-reduce(f32[1008]{0:T(1024)S(1)} %pad.8), channel_id=9, replica_groups=mesh['dp'=16] {'dp'}, use_global_device_ids=true, to_apply=%region_21.22.clone | all-reduce | flops 1008 | bytes 8064
  256.7 2.1 multiply_reduce_fusion.9
  260.5 2.7 multiply_reduce_fusion.7
  263.2 2.7 multiply_reduce_fusion.5
  266.0 2.4 multiply_reduce_fusion.1
  270.2 2.7 multiply_reduce_fusion.6
  272.9 52.6 %all-reduce.20.cloned.1.call-done = (f32[1,524288]{1,0:T(1,128)}, f32[1,2097152]{1,0:T(1,128)}, f32[1,1048576]{1,0:T(1,128)}, f32[16384]{0:T(1024)}) async-done(((f32[1,524288]{1,0:T(1,128)}, f32[1,2097152]{1,0:T(1,128)}, f32[1,1048576]{1,0:T(1,128)}, f32[16384]{0:T(1024)}), (f32[1,524288]{1,0:T(1,128)}, f32[1,2097152]{1,0:T(1,128)}, f32[1,1048576]{1,0:T(1,128)}, ...) | async-done | bytes 14745616
  329.4 2.7 multiply_reduce_fusion.4
  332.1 265.1 %all-reduce.22.cloned.1.call-done = (f32[2,2359296]{1,0:T(2,128)}, f32[2,1048576]{1,0:T(2,128)}) async-done(((f32[2,2359296]{1,0:T(2,128)}, f32[2,1048576]{1,0:T(2,128)}), (f32[2,2359296]{1,0:T(2,128)}, f32[2,1048576]{1,0:T(2,128)})) %all-reduce.22.cloned.1.call-update) | async-done | bytes 27262992
  598.9 2.4 multiply_reduce_fusion
  601.3 5.3 concatenate.3
  606.6 31.9 %all-reduce.11 = (f32[16]{0:T(128)S(1)}, f32[1008]{0:T(1024)}) all-reduce(f32[16]{0:T(128)S(1)} %concatenate.3, f32[1008]{0:T(1024)S(1)} %get-tuple-element.90), channel_id=1, replica_groups=mesh['dp'=16] {'dp'}, use_global_device_ids=true, to_apply=%region_18.0 | all-reduce | flops 1024 | bytes 8192 | tf_op jit(solution)/shard_map/psum | solution.py:58
  644.0 2.5 dynamic-slice_subtract_fusion.4
  648.1 3.5 dynamic-slice_subtract_fusion.3
  653.1 3.4 dynamic-slice_subtract_fusion.2
  656.7 2.9 dynamic-slice_subtract_fusion.1
  659.7 4.0 dynamic-slice_subtract_fusion
  665.1 14.9 %all_gather.30 = f32[16384]{0:T(1024)S(1)} all-gather(f32[1024]{0:T(1024)S(1)} %get-tuple-element.76), channel_id=1, replica_groups=mesh['dp'=16] {'dp'}, dimensions={0}, use_global_device_ids=true | all-gather | bytes 69632 | tf_op jit(solution)/shard_map/all_gather | solution.py:74
  680.5 18.6 %reduce.20 = f32[524288]{0:T(1024)} reduce(f32[1,524288]{1,0:T(1,128)} %all-gather.7.cloned.1.call-done, f32[]{:T(128)} %broadcast.56), dimensions={0}, to_apply=%all_gather.24.reduce_sub_computation.3 | reduce | bytes 4194308 | tf_op jit(solution)/shard_map/all_gather | solution.py:68
  702.2 9.4 all-gather.11.cloned.1.call-done
  711.6 4.8 copy.85
  718.0 44.3 %all-gather.17.cloned.1.call-done = f32[1,2048000]{1,0:T(1,128)} async-done(((f32[1,128000]{1,0:T(1,128)}), f32[1,2048000]{1,0:T(1,128)}) %all-gather.17.cloned.1.call-update) | async-done | bytes 8192016 | tf_op jit(solution)/shard_map/all_gather | solution.py:68
  762.3 64.7 %reduce.22 = f32[2048000]{0:T(1024)} reduce(f32[1,2048000]{1,0:T(1,128)} %all-gather.17.cloned.1.call-done, f32[]{:T(128)} %broadcast.56), dimensions={0}, to_apply=%all_gather.29.reduce_sub_computation.3 | reduce | bytes 16384004 | tf_op jit(solution)/shard_map/all_gather | solution.py:68
  826.9 10.4 %reshape.165 = f32[2048,1000]{1,0:T(8,128)} reshape(f32[2048000]{0:T(1024)} %reduce.22) | data formatting | bytes 16384000 | tf_op jit(solution)/shard_map/reshape | solution.py:68
  837.3 9.1 copy.53
  846.5 6.1 convert_element_type.38
  852.5 6.6 copy.54
  859.2 66.2 %reduce.21 = f32[2097152]{0:T(1024)} reduce(f32[1,2097152]{1,0:T(1,128)} %all-gather.9.cloned.1.call-done, f32[]{:T(128)} %broadcast.56), dimensions={0}, to_apply=%all_gather.25.reduce_sub_computation.3 | reduce | bytes 16777220 | tf_op jit(solution)/shard_map/all_gather | solution.py:68
  925.3 9.2 reshape.161
  934.6 6.1 convert_element_type.34
  940.7 13.2 %fusion.6 = (bf16[2,512,2048]{2,1,0:T(8,128)(2,1)}, f32[2,512,2048]{2,1,0:T(8,128)}) fusion(f32[1,2,512,2048]{3,1,2,0:T(2,128)} %bitcast.100), kind=kLoop, calls=%fused_computation.47 | loop fusion | flops 2097152 | bytes 20971520 | tf_op jit(solution)/shard_map/convert_element_type | solution.py:70
  954.0 10.3 %copy.77 = f32[1,2,4608,512]{3,2,1,0:T(8,128)S(1)} copy(f32[1,2,4608,512]{3,1,2,0:T(2,128)} %bitcast.88) | data formatting | bytes 37748736
  964.3 6.2 convert_element_type.36
  970.5 3.5 copy-done
  (69 shorter events, 24.0 us)
Async XLA Ops:
  7.2 263.0 %all-reduce.18.cloned.1.call-start = ((), (), s32[]{:S(2)}) async-start(), calls=%async_computation.6 | async-start | bytes 16384000
  40.3 1.6 copy-start.4
  40.3 285.2 %all-reduce.20.cloned.1.call-start = ((), (), s32[]{:S(2)}) async-start(), calls=%async_computation.7 | async-start | bytes 29491200
  45.3 11.0 %copy-start.3 = (f32[1,1,2048,512]{3,2,1,0:T(8,128)S(1)}, f32[1,1,2048,512]{3,2,1,0:T(8,128)}, u32[]{:S(2)}) copy-start(f32[1,1,2048,512]{3,2,1,0:T(8,128)} %param.35) | copy-start | bytes 12582916
  68.0 529.2 %all-reduce.22.cloned.1.call-start = ((), (), s32[]{:S(2)}) async-start(), calls=%async_computation.8 | async-start | bytes 54525952
  116.8 563.3 %all-gather.7.cloned.1.call-start = ((), (), s32[]{:S(2)}) async-start(), calls=%async_computation | async-start | bytes 2228224 | tf_op jit(solution)/shard_map/all_gather | solution.py:68
  219.6 48.7 %copy-start.10 = (f32[1000]{0:T(1024)S(1)}, f32[1000]{0:T(1024)}, u32[]{:S(2)}) copy-start(f32[1000]{0:T(1024)} %param.32) | copy-start | bytes 12004
  219.6 48.7 %copy-start.12 = (f32[63]{0:T(128)S(1)}, f32[63]{0:T(128)}, u32[]{:S(2)}) copy-start(f32[63]{0:T(128)} %param.48) | copy-start | bytes 760
  219.6 49.4 %copy-start.9 = (f32[32768]{0:T(1024)S(1)}, f32[32768]{0:T(1024)}, u32[]{:S(2)}) copy-start(f32[32768]{0:T(1024)} %param.41) | copy-start | bytes 393220
  219.6 49.4 %copy-start.6 = (f32[131072]{0:T(1024)S(1)}, f32[131072]{0:T(1024)}, u32[]{:S(2)}) copy-start(f32[131072]{0:T(1024)} %param.42) | copy-start | bytes 1572868
  260.5 383.6 %copy-start.8 = (f32[1,65536]{1,0:T(1,128)S(1)}, f32[1,65536]{1,0:T(1,128)}, u32[]{:S(2)}) copy-start(f32[1,65536]{1,0:T(1,128)} %param.43) | copy-start | bytes 786436
  643.2 13.5 %copy-start.7 = (f32[2,65536]{1,0:T(2,128)S(1)}, f32[2,65536]{1,0:T(2,128)}, u32[]{:S(2)}) copy-start(f32[2,65536]{1,0:T(2,128)} %param.45) | copy-start | bytes 1572868
  643.2 68.3 %all-gather.11.cloned.1.call-start = ((), (), s32[]{:S(2)}) async-start(), calls=%async_computation.2 | async-start | bytes 4456448 | tf_op jit(solution)/shard_map/all_gather | solution.py:68
  648.0 114.2 %all-gather.17.cloned.1.call-start = ((), (), s32[]{:S(2)}) async-start(), calls=%async_computation.5 | async-start | bytes 8704000 | tf_op jit(solution)/shard_map/all_gather | solution.py:68
  648.1 11.6 %copy-start.5 = (f32[2,147456]{1,0:T(2,128)S(1)}, f32[2,147456]{1,0:T(2,128)}, u32[]{:S(2)}) copy-start(f32[2,147456]{1,0:T(2,128)} %param.44) | copy-start | bytes 3538948
  653.1 206.1 %all-gather.9.cloned.1.call-start = ((), (), s32[]{:S(2)}) async-start(), calls=%async_computation.1 | async-start | bytes 8912896 | tf_op jit(solution)/shard_map/all_gather | solution.py:68
  656.6 284.2 %all-gather.15.cloned.1.call-start = ((), (), s32[]{:S(2)}) async-start(), calls=%async_computation.4 | async-start | bytes 8912896 | tf_op jit(solution)/shard_map/all_gather | solution.py:68
  659.7 4.1 copy-start.11
  659.7 294.3 %all-gather.13.cloned.1.call-start = ((), (), s32[]{:S(2)}) async-start(), calls=%async_computation.3 | async-start | bytes 20054016 | tf_op jit(solution)/shard_map/all_gather | solution.py:68
  700.9 15.4 %copy-start.2 = (f32[1024,512]{1,0:T(8,128)}, f32[1024,512]{1,0:T(8,128)S(1)}, u32[]{:S(2)}) copy-start(f32[1024,512]{1,0:T(8,128)S(1)} %reshape.160) | copy-start | bytes 6291460
  711.5 4.8 copy-start.1
  964.3 9.7 copy-start
Sparse Core Ops, SparseCore 0:
  40.4 113.8 all-reduce.17
  161.5 163.9 all-reduce.19
  332.0 265.2 all-reduce.21
  643.3 30.4 all-gather.6
  676.5 35.0 all-gather.10
  714.2 47.9 all-gather.16
  765.1 48.6 all-gather.8
  816.0 48.6 all-gather.14
  867.5 82.7 all-gather.12
where the time goes:
time: 993 us; the launch traced here: 981 us
  waiting for transfers between devices  372 us (37%)
  local copies, waits for them, and re-layouts  263 us (26%)
  other arithmetic  233 us (23%)
  blocking collectives  81 us (8%)
  between operations  20.7 us (2%)
  matrix products  10.8 us (1%)
    unnamed x12, waiting for transfers between devices  318 us
    unnamed x42, local copies, waits for them, and re-layouts  158 us
    all_gather x3, other arithmetic, body(): lax.all_gather(w_part - moment_next, 'dp', axis=1, tiled=True)  149 us
    reshape x2, local copies, waits for them, and re-layouts, body(): gradient.reshape(count, -1)  55.1 us
    all_gather x6, waiting for transfers between devices, body(): lax.all_gather(w_part - moment_next, 'dp', axis=1, tiled=True)  53.7 us
    convert_element_type x6, other arithmetic, body(): kernels_bf.append(w_full.astype(jnp.bfloat16))  34.4 us
    unnamed x1, blocking collectives  34.2 us
    psum x1, blocking collectives, body(): sq_total = lax.psum(jnp.concatenate(squares), 'dp')  31.9 us
  transfers between devices with their start and end apart: 9, of which 4 were waited for; matrix products, arithmetic and copies ran while one was open for 45% of the time, Pallas kernels for 0%

commit v1 on v0

v1 whole, which is shorter than its diff:
```python
import functools
import jax
import jax.numpy as jnp
from jax import lax
from jax.experimental import pallas as pl
from jax.experimental.pallas import tpu as pltpu
from jax.sharding import PartitionSpec as P

MOMENTUM = 0.9
TRUST_COEF = 0.001
DECAY = 0.0001

MESH = pl.DeviceIdType.MESH
F32 = jnp.float32
DEV = 16
U = 32
CW = 512
NCH = 48
NSLOT = 12
FC0 = 40
STARTS = (0, 9, 18, 26, 30, 34, 38, 40)
MID, SHORT, OUT = (2, DEV, 288, CW), (DEV, 64, 2048), (2, DEV, U, 2048)
INN, IN0 = (DEV, 128, CW), (DEV, 64, CW)
LANES = 128
SPLIT = 34
L1, L2, L3, L4 = 2, 5, 8, 10
AG0 = 48
M0, M1, M2, M3, M4 = 1, 3, 6, 10, 14
NSEND = 16


def tensor_of(c):
    t = 0
    for first in STARTS[1:]:
        t = t + jnp.where(c >= first, 1, 0)
    return t


def chunk_views(c, refs, fn):
    mid, short, out, inn, in0, fc = refs

    def rows(x):
        return pl.ds(pl.multiple_of(x * U, U), U)

    def cols(x):
        return pl.ds(pl.multiple_of(x * CW, CW), CW)

    def whole(ref):
        return [(ref, lambda dst: dst)]

    def strip(i):
        return lambda dst: dst.at[:, pl.ds(128 * i, 128)]

    @pl.when(c < 18)
    def _():
        fn(lambda p: whole(mid.at[c // 9, p, rows(c % 9), :]))

    @pl.when((c >= 18) & (c < 26))
    def _():
        fn(lambda p: whole(short.at[p, rows((c - 18) // 4), cols((c - 18) % 4)]))

    @pl.when((c >= 26) & (c < 34))
    def _():
        fn(lambda p: whole(out.at[(c - 26) // 4, p, :, cols((c - 26) % 4)]))

    @pl.when((c >= 34) & (c < 38))
    def _():
        fn(lambda p: whole(inn.at[p, rows(c - 34), :]))

    @pl.when((c >= 38) & (c < 40))
    def _():
        fn(lambda p: whole(in0.at[p, rows(c - 38), :]))

    if fc is not None:
        @pl.when(c >= FC0)
        def _():
            fn(lambda p: [(fc.at[rows(4 * (c - FC0) + i), pl.ds(pl.multiple_of(p * 128, 128), 128)], strip(i))
                          for i in range(4)])


def comm_kernel(lr_ref, gm, gs, go, gi, g0, gf, wm, ws, wo, wi, w0, wf, vm, vs, vo, vi, v0, vf,
                small_g, small_w, small_v,
                o_ref, vn_ref, so_ref, sv_ref,
                acc, rd, r1, r2, r3, grad, wbuf, vbuf, wnew, vnew, sums, nb, tr, sb, snew, svnew,
                load_sem, ds_sem, dr_sem, s1_sem, p1_sem, s2_sem, p2_sem, s3_sem, p3_sem,
                w_sem, v_sem, sm_send, sm_recv, so_send, so_recv, nb_send, nb_recv, loc_sem, vn_sem, misc_sem,
                a1_sem, a2_sem, a3_sem, ad_sem, as_sem,
                cd_sem, c1_sem, c2_sem, c3_sem):
    me = lax.axis_index('dp')
    core = me % 2
    chip = me // 2
    partner = me + 1 - 2 * core

    send_sems = (ds_sem, s1_sem, s2_sem, s3_sem)
    recv_sems = (dr_sem, p1_sem, p2_sem, p3_sem)
    ag_sems = (a1_sem, a2_sem, a3_sem)
    credits = (None, c1_sem, c2_sem, c3_sem)

    def order(c):
        steps = []
        for i in range(3):
            d = (c + i) % 3
            weight = 1 + d + (d * (d - 1)) // 2
            steps.append(weight * (1 - 2 * ((chip // weight) % 2)))
        return steps

    def remote(src, dst, send, recv, dev):
        return pltpu.make_async_remote_copy(src_ref=src, dst_ref=dst, send_sem=send, recv_sem=recv,
                                            device_id=(dev,), device_id_type=MESH)

    def local(src, dst, sem):
        return pltpu.make_async_copy(src, dst, sem)

    def units(n):
        return o_ref.at[0, pl.ds(0, n)]

    def drain(n, sem):
        local(units(n), units(n), sem).wait()

    def signal(sem, dev):
        pl.semaphore_signal(sem, inc=1, device_id=(dev,), device_id_type=MESH)

    barrier = pltpu.get_barrier_semaphore()

    def ring(d, _):
        signal(barrier, (me + d) % DEV)
        return 0
    lax.fori_loop(1, DEV, ring, 0)
    pl.semaphore_wait(barrier, DEV - 1)

    def small_out(d, _):
        dev = (me + d) % DEV
        remote(small_g.at[dev], sb.at[me], sm_send, sm_recv, dev).start()
        return 0

    def load_state(c, _):
        def weight(view):
            for src, part in view(me):
                local(src, part(wbuf.at[c]), w_sem).start()

        def moment(view):
            for src, part in view(0):
                local(src, part(vbuf.at[c]), v_sem).start()
        chunk_views(c, (wm, ws, wo, wi, w0, None), weight)
        chunk_views(c, (vm, vs, vo, vi, v0, vf), moment)
        return 0

    def fc_weights():
        lane = pl.ds(pl.multiple_of(me * 128, 128), 128)
        for b in range(31):
            local(wf.at[pl.ds(b * U, U), lane], wbuf.at[FC0 + b // 4, :, pl.ds(b % 4 * 128, 128)], w_sem).start()
        local(wf.at[pl.ds(992, 8), lane], wbuf.at[NCH - 1, pl.ds(0, 8), pl.ds(384, 128)], w_sem).start()
        wbuf[NCH - 1, 8:32, 384:512] = jnp.zeros((24, 128), F32)

    def weights_wait():
        first = pl.ds(0, NCH - 1)
        local(wbuf.at[first], wbuf.at[first], w_sem).wait()
        for part in (wbuf.at[NCH - 1, :, pl.ds(0, 384)], wbuf.at[NCH - 1, pl.ds(0, 8), pl.ds(384, 128)]):
            local(part, part, w_sem).wait()

    def sent(slot):
        for level in range(4):
            drain(8 >> level, send_sems[level].at[slot])

    def rs_start(c):
        slot = c % NSLOT

        @pl.when(c >= NSLOT)
        def _():
            sent(slot)
            pl.semaphore_wait(cd_sem, 1)
        x1, x2, x3 = order(c)
        chips = [chip + (q // 4) * x1 + ((q // 2) % 2) * x2 + (q % 2) * x3 for q in range(8)]

        def go_all(view):
            for q in (4, 5, 6, 7, 0, 1, 2, 3):
                for src, part in view(2 * chips[q] + 1 - core):
                    remote(src, part(rd.at[slot, q]), ds_sem.at[slot], dr_sem.at[slot], partner).start()
                for src, part in view(2 * chips[q] + core):
                    local(src, part(acc.at[slot, q]), load_sem.at[slot]).start()
        chunk_views(c, (gm, gs, go, gi, g0, gf), go_all)

    def rs_fold(c, level):
        slot, half = c % NSLOT, 4 >> level
        came, going = (rd, r1, r2, r3)[level:level + 2]
        dev = 2 * (chip + order(c)[level]) + core
        if level == 0:
            drain(8, load_sem.at[slot])
        drain(2 * half, recv_sems[level].at[slot])
        acc[slot, half:2 * half] = acc[slot, half:2 * half] + came[slot, half:2 * half]

        @pl.when(c >= NSLOT)
        def _():
            pl.semaphore_wait(credits[level + 1].at[c % 3], 1)
        remote(acc.at[slot, pl.ds(half, half)], going.at[slot], send_sems[level + 1].at[slot],
               recv_sems[level + 1].at[slot], dev).start()
        acc[slot, 0:half] = acc[slot, 0:half] + came[slot, 0:half]
        give_credit(c, level)

    def give_credit(c, level):
        @pl.when(c + NSLOT < NCH)
        def _():
            if level == 0:
                signal(cd_sem, partner)
            else:
                signal(credits[level].at[c % 3], 2 * (chip + order(c)[level - 1]) + core)

    def fold(x):
        y = jnp.sum(x * x, axis=0, keepdims=True)
        return sum(y[:, i:i + LANES] for i in range(0, CW, LANES))

    def rs_end(c):
        slot = c % NSLOT
        drain(1, p3_sem.at[slot])
        scale = jnp.where(c >= FC0, 1.0 / 16384.0, 1.0 / 16.0).astype(F32)
        g = (acc[slot, 0] + r3[slot, 0]) * scale
        grad[c] = g
        t = tensor_of(c)
        sums[pl.ds(t, 1), :] = sums[pl.ds(t, 1), :] + fold(g)
        give_credit(c, 3)

    def weight_sums(c, _):
        t = tensor_of(c)
        sums[pl.ds(8 + t, 1), :] = sums[pl.ds(8 + t, 1), :] + fold(wbuf[c])
        return 0

    def norms_out(n):
        nb[n, me] = sums[...]

        def send(d, _):
            dev = (me + d) % DEV
            remote(nb.at[n, me], nb.at[n, me], nb_send.at[n], nb_recv.at[n], dev).start()
            return 0
        lax.fori_loop(1, DEV, send, 0)

    def norms_in(n):
        local(nb.at[n, pl.ds(0, DEV - 1)], nb.at[n, pl.ds(0, DEV - 1)], nb_recv.at[n]).wait()
        local(nb.at[n, pl.ds(0, DEV - 1)], nb.at[n, pl.ds(0, DEV - 1)], nb_send.at[n]).wait()
        total = jnp.sum(nb[n], axis=0)
        norm = jnp.sqrt(jnp.broadcast_to(jnp.sum(total, axis=1, keepdims=True), (16, 128)))
        g_norm, w_norm = norm[0:8], norm[8:16]
        ratio = jnp.where((w_norm > 0) & (g_norm > 0), TRUST_COEF * w_norm / (g_norm + DECAY * w_norm), 1.0)
        tr[...] = lr_ref[0, 0] * ratio

    def update(a):
        rate = tr[pl.ds(tensor_of(a), 1), :]
        for i in range(4):
            s = slice(128 * i, 128 * i + 128)
            w = wbuf[a, :, s]
            v = MOMENTUM * vbuf[a, :, s] + rate * (grad[a, :, s] + DECAY * w)
            vnew[a, :, s] = v
            wnew[a, :, s] = w - v

    def ag_send(src, a, p, recv, dev):
        remote(src, o_ref.at[a, p], as_sem.at[a % NSEND], recv.at[a], dev).start()

    def ids(a):
        x1, x2, x3 = order(a)
        return [me + 2 * ((q % 2) * x1 + ((q // 2) % 2) * x2 + (q // 4) * x3) for q in range(8)]

    def ag_pass(a, n):
        e = ids(a)
        level = n.bit_length() - 1
        held = [wnew.at[a]] + [o_ref.at[a, p] for p in e[1:n]]
        if n > 1:
            drain(n // 2, ag_sems[level - 1].at[a])
        if n < 8:
            for q in range(n):
                ag_send(held[q], a, e[q], ag_sems[level], e[n])
        for q in range(n // 2, n):
            ag_send(held[q], a, e[q], ad_sem, partner)

    def ag_first(a):
        @pl.when(a >= NSEND)
        def _():
            drain(15, as_sem.at[a % NSEND])
        ag_pass(a, 1)
        local(wnew.at[a], o_ref.at[a, me], loc_sem).start()
        local(vnew.at[a], vn_ref.at[a], vn_sem).start()

    def ag_end(a):
        drain(8, ad_sem.at[a])

    def stage(s, lag, fn):
        c = s - lag

        @pl.when((c >= 0) & (c < NCH))
        def _():
            fn(c)

    def rs_rest(s):
        stage(s, L4, rs_end)
        for level, lag in ((2, L3), (1, L2), (0, L1)):
            stage(s, lag, functools.partial(rs_fold, level=level))

    def rs_step(s, _):
        rs_rest(s)
        stage(s, 0, rs_start)
        return 0

    def ag_step(s):
        stage(s, AG0 + M4, ag_end)
        for n, lag in ((8, M3), (4, M2), (2, M1)):
            stage(s, AG0 + lag, functools.partial(ag_pass, n=n))
        stage(s, AG0 + M0, ag_first)
        stage(s, AG0, update)

    def both_step(s, _):
        rs_rest(s)
        ag_step(s)
        return 0

    def last_step(s, _):
        ag_step(s)
        return 0

    lax.fori_loop(0, 2, rs_step, 0)
    lax.fori_loop(1, DEV, small_out, 0)
    sums[...] = jnp.zeros_like(sums)
    own = local(small_g.at[me], sb.at[me], misc_sem)
    own.start()
    lax.fori_loop(0, NCH, load_state, 0)
    fc_weights()
    lax.fori_loop(2, 10, rs_step, 0)

    own.wait()
    local(sb.at[pl.ds(0, DEV - 1)], sb.at[pl.ds(0, DEV - 1)], sm_recv).wait()
    local(sb.at[pl.ds(0, DEV - 1)], sb.at[pl.ds(0, DEV - 1)], sm_send).wait()
    row = lax.broadcasted_iota(jnp.int32, (16, 128), 0)
    small = jnp.sum(sb[...], axis=0) * jnp.where(row < 8, 1.0 / 16.0, 1.0 / 16384.0)
    sv = MOMENTUM * small_v[...] + lr_ref[0, 0] * small
    svnew[...] = sv
    snew[...] = small_w[...] - sv

    lax.fori_loop(10, 14, rs_step, 0)

    def small_back(d, _):
        dev = (me + d) % DEV
        remote(snew, so_ref.at[me], so_send, so_recv, dev).start()
        return 0
    lax.fori_loop(1, DEV, small_back, 0)
    own_s = local(snew, so_ref.at[me], misc_sem)
    own_s.start()
    own_v = local(svnew, sv_ref, w_sem)

    weights_wait()
    local(vbuf, vbuf, v_sem).wait()
    own_v.start()
    lax.fori_loop(0, NCH, weight_sums, 0)

    lax.fori_loop(14, SPLIT + L4, rs_step, 0)
    norms_out(0)
    lax.fori_loop(SPLIT + L4, AG0, rs_step, 0)
    norms_in(0)
    lax.fori_loop(AG0, NCH + L4, both_step, 0)
    norms_out(1)
    lax.fori_loop(NCH + L4, NCH + L4 + 4, last_step, 0)
    norms_in(1)
    lax.fori_loop(NCH + L4 + 4, AG0 + M4 + NCH, last_step, 0)

    def rest(c, _):
        sent(c % NSLOT)
        return 0
    lax.fori_loop(NCH - NSLOT, NCH, rest, 0)

    def rest_ag(a, _):
        drain(15, as_sem.at[a % NSEND])
        return 0
    lax.fori_loop(NCH - NSEND, NCH, rest_ag, 0)
    own_s.wait()
    own_v.wait()
    local(so_ref.at[pl.ds(0, DEV - 1)], so_ref.at[pl.ds(0, DEV - 1)], so_recv).wait()
    local(so_ref.at[pl.ds(0, DEV - 1)], so_ref.at[pl.ds(0, DEV - 1)], so_send).wait()
    local(wnew, wnew, loc_sem).wait()
    local(vnew, vn_ref, vn_sem).wait()


def run_comm(lr, grads, weights, moments, small_g, small_w, small_v):
    unit = (U, CW)
    anyspec = pl.BlockSpec(memory_space=pl.ANY)
    vspec = pl.BlockSpec(memory_space=pltpu.VMEM)
    dma = pltpu.SemaphoreType.DMA
    reg = pltpu.SemaphoreType.REGULAR
    slots = [dma((NSLOT,))] * 9
    return pl.pallas_call(
        comm_kernel,
        out_shape=[jax.ShapeDtypeStruct((NCH, DEV) + unit, F32), jax.ShapeDtypeStruct((NCH,) + unit, F32),
                   jax.ShapeDtypeStruct((DEV, 16, 128), F32), jax.ShapeDtypeStruct((16, 128), F32)],
        in_specs=[pl.BlockSpec(memory_space=pltpu.SMEM)] + [anyspec] * 19 + [vspec] * 2,
        out_specs=[anyspec] * 4,
        scratch_shapes=[
            pltpu.VMEM((NSLOT, 8) + unit, F32), pltpu.VMEM((NSLOT, 8) + unit, F32),
            pltpu.VMEM((NSLOT, 4) + unit, F32), pltpu.VMEM((NSLOT, 2) + unit, F32),
            pltpu.VMEM((NSLOT, 1) + unit, F32)]
        + [pltpu.VMEM((NCH,) + unit, F32)] * 5
        + [pltpu.VMEM((16, 128), F32), pltpu.VMEM((2, DEV, 16, 128), F32), pltpu.VMEM((8, 128), F32),
           pltpu.VMEM((DEV, 16, 128), F32), pltpu.VMEM((16, 128), F32), pltpu.VMEM((16, 128), F32)]
        + slots
        + [dma, dma, dma, dma, dma, dma, dma((2,)), dma((2,)), dma, dma, dma]
        + [dma((NCH,))] * 4 + [dma((NSEND,))]
        + [reg, reg((3,)), reg((3,)), reg((3,))],
        compiler_params=pltpu.CompilerParams(collective_id=0, has_side_effects=True,
                                             vmem_limit_bytes=56 * 1024 * 1024),
        name='lars_comm',
    )(lr, *grads, *weights, *moments, small_g, small_w, small_v)


NBUF = 6
AHEAD = 3


def write_kernel(o_ref, om, os_, oo, oi, o0, of, bm, bs, bo, bi, b0, bf,
                 buf, bbuf, fbuf, fbbuf, in_sem, f_sem, b_sem):
    def view(c, refs):
        m, s, o, i, z = refs
        if c < 18:
            return m.at[c // 9, :, pl.ds(c % 9 * U, U), :]
        if c < 26:
            return s.at[:, pl.ds((c - 18) // 4 * U, U), pl.ds((c - 18) % 4 * CW, CW)]
        if c < 34:
            return o.at[(c - 26) // 4, :, :, pl.ds((c - 26) % 4 * CW, CW)]
        if c < 38:
            return i.at[:, pl.ds((c - 34) * U, U), :]
        return z.at[:, pl.ds((c - 38) * U, U), :]

    def load(i):
        return [pltpu.make_async_copy(o_ref.at[i], buf.at[i % NBUF], in_sem.at[i % NBUF])]

    def stores(i):
        slot = i % NBUF
        if i < FC0:
            pairs = [(buf.at[slot], view(i, (om, os_, oo, oi, o0))), (bbuf.at[slot], view(i, (bm, bs, bo, bi, b0)))]
        else:
            size = 128 if i < NCH - 1 else 104
            have, want = pl.ds(0, size), pl.ds(128 * (i - FC0), size)
            pairs = [(fbuf.at[i % 4, have], of.at[want]), (fbbuf.at[i % 4, have], bf.at[want])]
        return [pltpu.make_async_copy(*pairs[0], f_sem.at[slot]), pltpu.make_async_copy(*pairs[1], b_sem.at[slot])]

    for i in range(AHEAD):
        for d in load(i):
            d.start()
    waited = 0
    for i in range(NCH):
        slot = i % NBUF
        for d in load(i):
            d.wait()
        if i < FC0:
            def cast(p, _):
                bbuf[slot, p] = buf[slot, p].astype(jnp.bfloat16)
                return 0
            lax.fori_loop(0, DEV, cast, 0)
        else:
            while waited <= i - 4:
                for d in stores(waited):
                    d.wait()
                waited += 1
            for p in range(DEV):
                for r in range(4):
                    x = buf[slot, p, :, 128 * r:128 * r + 128]
                    fbuf[i % 4, U * r:U * r + U, 128 * p:128 * p + 128] = x
                    fbbuf[i % 4, U * r:U * r + U, 128 * p:128 * p + 128] = x.astype(jnp.bfloat16)
        for d in stores(i):
            d.start()
        nxt = i + AHEAD
        if nxt < NCH:
            while waited <= nxt - NBUF:
                for d in stores(waited):
                    d.wait()
                waited += 1
            for d in load(nxt):
                d.start()
    while waited < NCH:
        for d in stores(waited):
            d.wait()
        waited += 1


def run_write(o):
    anyspec = pl.BlockSpec(memory_space=pl.ANY)
    shapes = [MID, SHORT, OUT, INN, IN0, (1000, 2048)]
    dma = pltpu.SemaphoreType.DMA
    return pl.pallas_call(
        write_kernel,
        out_shape=[jax.ShapeDtypeStruct(s, F32) for s in shapes]
        + [jax.ShapeDtypeStruct(s, jnp.bfloat16) for s in shapes],
        in_specs=[anyspec],
        out_specs=[anyspec] * 12,
        scratch_shapes=[
            pltpu.VMEM((NBUF, DEV, U, CW), F32), pltpu.VMEM((NBUF, DEV, U, CW), jnp.bfloat16),
            pltpu.VMEM((4, 128, 2048), F32), pltpu.VMEM((4, 128, 2048), jnp.bfloat16),
            dma((NBUF,)), dma((NBUF,)), dma((NBUF,))],
        compiler_params=pltpu.CompilerParams(vmem_limit_bytes=48 * 1024 * 1024),
        name='write_out',
    )(o)


def solution(mesh):
    n_dev = mesh.shape['dp']
    assert n_dev == DEV
    full, lead, cols = P(), P('dp'), P(None, 'dp')
    moment_specs = (lead, lead, cols, cols, cols, lead, lead, lead)
    in_specs = (full,) * 8 + (lead,) * 8 + moment_specs + (full,)
    out_specs = (full,) * 14 + moment_specs

    def body(w_in0, w_short, w_in, w_mid, w_out, w_fc, w_bn, w_bias,
             g_in0, g_short, g_in, g_mid, g_out, g_bn, pooled, dlogits,
             v_in0, v_short, v_in, v_mid, v_out, v_fc, v_bn, v_bias, learn_rate):
        rank = lax.axis_index('dp')
        fc_local = lax.dot_general(jnp.pad(dlogits, ((0, 0), (0, 24))), pooled, (((0,), (0,)), ((), ())),
                                   preferred_element_type=F32)
        bias_local = jnp.sum(dlogits, axis=0, dtype=F32)
        grads = (g_mid.reshape(MID), g_short.reshape(SHORT), g_out.reshape(OUT), g_in.reshape(INN),
                 g_in0.reshape(IN0), fc_local)
        weights = (w_mid.reshape(MID), w_short.reshape(SHORT), w_out.reshape(OUT), w_in.reshape(INN),
                   w_in0.reshape(IN0), w_fc.T)

        def own(x, shape):
            return x.reshape([1 if n == DEV else n for n in shape])
        moments = (own(v_mid, MID), own(v_short, SHORT), own(v_out, OUT), own(v_in, INN), own(v_in0, IN0),
                   jnp.pad(v_fc.reshape(LANES, 1000).T, ((0, 24), (0, 0))))

        def pad_bias(x):
            return jnp.pad(x, ((0, 0), (0, 65)))[:, None, :]
        small_g = jnp.concatenate([g_bn.reshape(DEV, 8, 128),
                                   jnp.pad(pad_bias(jnp.pad(bias_local, (0, 8)).reshape(DEV, 63)),
                                           ((0, 0), (0, 7), (0, 0)))], axis=1)

        def own_small(bn, bias):
            return jnp.concatenate([bn.reshape(8, 128), jnp.pad(bias.reshape(1, 63), ((0, 7), (0, 65)))], axis=0)
        small_w = own_small(lax.dynamic_slice_in_dim(w_bn, rank * 1024, 1024),
                            lax.dynamic_slice_in_dim(jnp.pad(w_bias, (0, 8)), rank * 63, 63))
        small_v = own_small(v_bn, v_bias)
        o, vn, so, sv = run_comm(learn_rate.reshape(1, 1), grads, weights, moments, small_g, small_w, small_v)
        f = run_write(o)
        mid, short, out, inn, in0, fc, mid_b, short_b, out_b, inn_b, in0_b, fc_b = f

        def wide(x, rows):
            return x.reshape(rows, 4, U, CW).transpose(0, 2, 1, 3)
        vn_fc = vn[40:48].reshape(8, U, 4, 128).transpose(0, 2, 1, 3).reshape(1024, 128)[:1000].T
        return (in0.reshape(w_in0.shape), short.reshape(w_short.shape), inn.reshape(w_in.shape),
                mid.reshape(w_mid.shape), out.reshape(w_out.shape), fc.T,
                so[:, :8].reshape(-1), so[:, 8, :63].reshape(-1)[:1000],
                in0_b.reshape(w_in0.shape), short_b.reshape(w_short.shape), inn_b.reshape(w_in.shape),
                mid_b.reshape(w_mid.shape), out_b.reshape(w_out.shape), fc_b.T,
                vn[38:40].reshape(v_in0.shape), wide(vn[18:26], 2).reshape(v_short.shape),
                vn[34:38].reshape(v_in.shape), vn[0:18].reshape(v_mid.shape),
                wide(vn[26:34], 2).reshape(v_out.shape), vn_fc.reshape(v_fc.shape),
                sv[:8].reshape(-1), sv[8, :63])

    return jax.shard_map(body, mesh=mesh, in_specs=in_specs, out_specs=out_specs, check_vma=False)
```

time: 993 us -> 429 us (0.43); the launches traced: 981 us -> 428 us
  Pallas kernels: 0 us -> 382 us
  waiting for transfers between devices: 372 us -> 0 us
  local copies, waits for them, and re-layouts: 263 us -> 30.7 us
  other arithmetic: 233 us -> 4.73 us
  blocking collectives: 81 us -> 0 us
  between operations: 20.7 us -> 1.67 us
    pallas_call x0 -> x2, Pallas kernels: none -> 382 us  [the longest x1 340 us: run_comm(): pl.pallas_call(comm_kernel, out_shape=[jax.ShapeDtypeStruct((NCH, DEV) +...]
    unnamed x12 -> x0, waiting for transfers between devices: 318 us -> none
    unnamed x42 -> x14, local copies, waits for them, and re-layouts: 158 us -> 8.45 us
    all_gather x3 -> x0, other arithmetic: 149 us -> none  [body(): lax.all_gather(w_part - moment_next, 'dp', axis=1, tiled=True)]
    reshape x6 -> x15, local copies, waits for them, and re-layouts: 98.7 us -> 14.9 us  [the longest x2 3.64 us: own(): return x.reshape([1 if n == DEV else n for n in shape])]
    all_gather x6 -> x0, waiting for transfers between devices: 53.7 us -> none  [body(): lax.all_gather(w_part - moment_next, 'dp', axis=1, tiled=True)]
    convert_element_type x6 -> x0, other arithmetic: 34.4 us -> none  [body(): kernels_bf.append(w_full.astype(jnp.bfloat16))]
    unnamed x1 -> x0, blocking collectives: 34.2 us -> none
  transfers between devices with their start and end apart: 9 -> 0, of which waited for: 4 -> 0; matrix products, arithmetic and copies ran while one was open for 45% -> 0% of each run, Pallas kernels for 0% -> 0%
where the time goes in v1:
time: 429 us; the launch traced here: 428 us
  Pallas kernels  382 us (89%)
  local copies, waits for them, and re-layouts  30.7 us (7%)
  matrix products  8.88 us (2%)
  other arithmetic  4.73 us (1%)
    pallas_call x1, Pallas kernels, run_comm(): pl.pallas_call(comm_kernel, out_shape=[jax.ShapeDtypeStruct((NCH, DEV) +...  340 us
    pallas_call x1, Pallas kernels, run_write(): pl.pallas_call(write_kernel, out_shape=[jax.ShapeDtypeStruct(s, F32) for...  42.1 us
    dot_general x1, matrix products, body(): lax.dot_general(jnp.pad(dlogits, ((0, 0), (0, 24))), pooled, (((0,), (0,)...  8.88 us

profile of v1, /device:TPU:1, one launch (start us, length us, event | category | flops | bytes accessed | tf_op | source)
XLA Modules:
  0.0 427.7 jit_solution(7467992440915747179)
XLA Ops:
  0.7 0.0 copy-start
  0.7 0.0 copy-start.3
  1.4 0.8 fusion.2
  2.2 0.0 copy-done
  2.2 1.9 convert_reduce_fusion
  4.1 0.1 reshape.197
  4.2 1.3 select_maximum_fusion.1
  5.5 1.5 select_maximum_fusion.small_g
  7.0 0.0 copy-start.2
  7.0 1.7 reshape.194.v0
  8.7 1.7 copy.66
  10.4 1.9 reshape.191.vs
  12.3 0.0 copy-done.3
  12.3 1.1 copy.64
  13.4 1.4 reshape.195
  14.9 0.2 copy.48
  15.1 0.8 pad.31.vf
  15.9 2.5 copy.63
  18.4 0.0 copy-done.2
  18.4 8.9 %fusion.gf = f32[1024,2048]{1,0:T(8,128)} fusion(bf16[1024,2048]{1,0:T(8,128)(2,1)} %param.39, bf16[1024,1000]{0,1:T(8,128)(2,1)S(1)} %copy-done.2), kind=kOutput, calls=%fused_computation.1 | convolution fusion | flops 4294967296 | bytes 14630912 | tf_op jit(solution)/shard_map/dot_general | solution.py:509
  27.3 339.5 %lars_comm.1 = (f32[48,16,32,512]{3,2,1,0:T(8,128)}, f32[48,32,512]{2,1,0:T(8,128)}, f32[16,16,128]{2,1,0:T(8,128)}, f32[16,128]{1,0:T(8,128)}) custom-call(f32[1,1]{1,0:T(1,128)} %bitcast.74.lr_ref, f32[2,16,288,512]{3,2,1,0:T(8,128)} %bitcast.75, f32[16,64,2048]{2,1,0:T(8,128)} %bitcast.77, f32[2,16,32,2048]{3,2,1,0:T(8,128)} %bitcast.78, ...), custom_call_target="tpu_custom_call" | custom-call | tf_op jit(solution)/shard_map/lars_comm/pallas_call | solution.py:385
  366.8 1.2 slice_bitcast_fusion.4
  368.0 1.3 slice_bitcast_fusion.3
  369.3 0.9 slice_reduce_fusion
  370.1 1.5 slice_bitcast_fusion.2
  371.6 0.7 reshape_squeeze.3
  372.3 0.9 slice.39
  373.2 0.7 copy.56
  373.9 1.0 slice.41
  374.9 1.0 reshape.216
  375.9 1.4 slice.42
  377.3 1.5 slice_bitcast_fusion
  378.8 0.1 copy.65
  378.9 0.3 copy.50
  379.3 1.3 reshape.219
  380.6 2.0 reshape.217
  382.6 0.2 copy.52
  382.8 1.3 reshape.222
  384.1 0.3 copy.49
  384.4 0.9 copy.57
  385.3 0.0 copy-start.1
  385.4 42.1 %write_out.1 = (f32[2,16,288,512]{3,2,1,0:T(8,128)}, f32[16,64,2048]{2,1,0:T(8,128)}, f32[2,16,32,2048]{3,2,1,0:T(8,128)}, f32[16,128,512]{2,1,0:T(8,128)}, f32[...) custom-call(f32[48,16,32,512]{3,2,1,0:T(8,128)} %get-tuple-element.3, ...), custom_call_target="tpu_custom_call" | custom-call | tf_op jit(solution)/shard_map/write_out/pallas_call | solution.py:482
  427.5 0.0 copy-done.1
  (4 shorter events, 0.0 us)
Async XLA Ops:
  0.7 1.5 copy-start
  0.7 11.7 %copy-start.3 = (f32[2,65536]{1,0:T(2,128)S(1)}, f32[2,65536]{1,0:T(2,128)}, u32[]{:S(2)}) copy-start(f32[2,65536]{1,0:T(2,128)} %param.45) | copy-start | bytes 1572868
  7.0 11.4 %copy-start.2 = (bf16[1024,1000]{0,1:T(8,128)(2,1)S(1)}, bf16[1024,1000]{0,1:T(8,128)(2,1)}, u32[]{:S(2)}) copy-start(bf16[1024,1000]{0,1:T(8,128)(2,1)} %param.40) | copy-start | bytes 6144004
  385.3 42.2 %copy-start.1 = (f32[16384]{0:T(1024)S(1)}, f32[16384]{0:T(1024)}, u32[]{:S(2)}) copy-start(f32[16384]{0:T(1024)} %param.31) | copy-start | bytes 196612

commit v2 on v0

v2 whole, which is shorter than its diff:
```python
import functools
import jax
import jax.numpy as jnp
from jax import lax
from jax.experimental import pallas as pl
from jax.experimental.pallas import tpu as pltpu
from jax.sharding import PartitionSpec as P

MOMENTUM = 0.9
TRUST_COEF = 0.001
DECAY = 0.0001

MESH = pl.DeviceIdType.MESH
F32, BF16 = jnp.float32, jnp.bfloat16
DEV = 16
LANES = 128
U, CW = 32, 512
NCH = 48
FC0 = 40
CLASSES, LASTROW = 1000, 992
SUB = 8
TABLE = ((0, 2, 9, 1), (18, 1, 8, 4), (26, 2, 4, 4), (34, 1, 4, 1), (38, 1, 2, 1))
STARTS = (9, 18, 26, 30, 34, 38, FC0)
SPLIT = 26
NSLOT = 15
LAGS = (2, 6, 10, 13)
AG0 = 43
FIRST = 1
AGLAGS = ((2, 5), (4, 10), (8, 16))
AGEND = 20
NSEND = 18
MM0 = 5
SMALL = 16


def tensor_of(c):
    return sum(jnp.where(c >= first, 1, 0) for first in STARTS)


def dshape(first, stack, per, blocks, lead):
    return (stack, lead, per // blocks * U, blocks * CW)


def unit_at(entry, c):
    first, _, per, blocks = entry
    k = (c - first) % per
    return (c - first) // per, k // blocks * U, k % blocks * CW


def aligned(x, size):
    return pl.ds(x if isinstance(x, int) else pl.multiple_of(x, size), size)


def chunk_views(c, refs, fn):
    for entry, ref in zip(TABLE, refs):
        first, stack, per, _ = entry

        @pl.when((c >= first) & (c < first + stack * per))
        def _():
            i, row, col = unit_at(entry, c)
            fn(lambda p: ref.at[i, p, aligned(row, U), aligned(col, CW)])


def comm_kernel(lr_ref, gm, gs, go, gi, g0, x_ref, d_ref, wm, ws, wo, wi, w0, wf, vm, vs, vo, vi, v0, vf,
                g_bn, w_bn, v_bn, w_bias, v_bias,
                o_ref, nm, ns, no, ni, n0, nf, so_ref, sv_ref,
                acc, rd, r1, r2, r3, grad, wbuf, vbuf, xbuf, dbuf, fcg,
                sums, nb, tr, sb, bias, snew, svnew,
                load_sem, ds_sem, dr_sem, s1_sem, p1_sem, s2_sem, p2_sem, s3_sem, p3_sem,
                w_sem, v_sem, x_sem, sm_send, sm_recv, so_send, so_recv, loc_sem, vn_sem, misc_sem,
                nb_send, nb_recv, a1_sem, a2_sem, a3_sem, ad_sem, as_sem,
                cd_sem, c1_sem, c2_sem, c3_sem):
    me = lax.axis_index('dp')
    core = me % 2
    chip = me // 2
    partner = me + 1 - 2 * core
    send_sems = (ds_sem, s1_sem, s2_sem, s3_sem)
    recv_sems = (dr_sem, p1_sem, p2_sem, p3_sem)
    ag_sems = (a1_sem, a2_sem, a3_sem)
    credits = (None, c1_sem, c2_sem, c3_sem)
    others = pl.ds(0, DEV - 1)

    def order(c):
        steps = []
        for i in range(3):
            d = (c + i) % 3
            weight = 1 + d + (d * (d - 1)) // 2
            steps.append(weight * (1 - 2 * ((chip // weight) % 2)))
        return steps

    def remote(src, dst, send, recv, dev):
        return pltpu.make_async_remote_copy(src_ref=src, dst_ref=dst, send_sem=send, recv_sem=recv,
                                            device_id=(dev,), device_id_type=MESH)

    def local(src, dst, sem):
        return pltpu.make_async_copy(src, dst, sem)

    def landed(ref, sem):
        local(ref, ref, sem).wait()

    def drain(n, sem):
        landed(o_ref.at[0, pl.ds(0, n)], sem)

    def signal(sem, dev):
        pl.semaphore_signal(sem, inc=1, device_id=(dev,), device_id_type=MESH)

    def loop(lo, hi, fn):
        def body(i, carry):
            fn(i)
            return carry
        lax.fori_loop(lo, hi, body, 0)

    def each_other(fn):
        loop(1, DEV, lambda d: fn((me + d) % DEV))

    def load_state(c):
        chunk_views(c, (wm, ws, wo, wi, w0), lambda view: local(view(me), wbuf.at[c], w_sem).start())

    def state():
        loop(0, FC0, load_state)
        loop(0, FC0, lambda c: strips(c, (vm, vs, vo, vi, v0), lambda src, dst: local(src, dst, v_sem).start()))
        lane = aligned(me * LANES, LANES)
        for b in range(CLASSES // U):
            dst = wbuf.at[FC0 + b // 4, :, pl.ds(b % 4 * LANES, LANES)]
            local(wf.at[pl.ds(b * U, U), lane], dst, w_sem).start()
        local(wf.at[pl.ds(LASTROW, SUB), lane], wbuf.at[NCH - 1, pl.ds(0, SUB), pl.ds(CW - LANES, LANES)], w_sem).start()
        wbuf[NCH - 1, SUB:, CW - LANES:] = jnp.zeros((U - SUB, LANES), F32)
        for b in range(U):
            dst = vbuf.at[FC0 + b // 4, :, pl.ds(b % 4 * LANES, LANES)]
            local(vf.at[pl.ds(b * U, U)], dst, v_sem).start()

    def strips(c, refs, fn):
        for entry, ref in zip(TABLE, refs):
            first, stack, per, _ = entry

            @pl.when((c >= first) & (c < first + stack * per))
            def _():
                i, row, col = unit_at(entry, c)
                for b in range(CW // LANES):
                    fn(ref.at[aligned(row, U), col // LANES + b, i, 0, :], vbuf.at[c, :, pl.ds(b * LANES, LANES)])

    def state_wait():
        landed(wbuf.at[pl.ds(0, NCH - 1)], w_sem)
        landed(wbuf.at[NCH - 1, :, pl.ds(0, CW - LANES)], w_sem)
        landed(wbuf.at[NCH - 1, pl.ds(0, SUB), pl.ds(CW - LANES, LANES)], w_sem)
        landed(vbuf, v_sem)
        loop(0, NCH, weight_sums)

    def fc_block(b):
        y = jnp.dot(dbuf[...], xbuf[:, aligned(b * 2 * LANES, 2 * LANES)], preferred_element_type=F32)
        for h in range(2):
            part = y[:, h * LANES:(h + 1) * LANES]
            for g in range(CLASSES // U):
                fcg[g // 4, 2 * b + h, :, g % 4 * LANES:(g % 4 + 1) * LANES] = part[g * U:(g + 1) * U]
            fcg[NCH - FC0 - 1, 2 * b + h, 0:SUB, CW - LANES:] = part[LASTROW:]
            fcg[NCH - FC0 - 1, 2 * b + h, SUB:, CW - LANES:] = jnp.zeros((U - SUB, LANES), F32)

    def bias_out():
        line = jnp.dot(dbuf[...], jnp.ones((dbuf.shape[1], LANES), BF16), preferred_element_type=F32)
        square = (LANES, LANES)
        diagonal = lax.broadcasted_iota(jnp.int32, square, 0) == lax.broadcasted_iota(jnp.int32, square, 1)
        for i in range(SUB):
            part = line[i * LANES:min(CLASSES, (i + 1) * LANES)]
            bias[i:i + 1, :] = jnp.sum(jnp.where(diagonal[:part.shape[0]], part, 0.0), axis=0, keepdims=True)
        bias[SUB:, :] = v_bias[...]
        sb[me, SUB:, :] = bias[...]
        each_other(lambda dev: remote(bias, sb.at[me, pl.ds(SUB, 2 * SUB)], sm_send, sm_recv, dev).start())

    def small_update():
        landed(sb.at[0, pl.ds(0, SUB)], misc_sem)
        landed(sb.at[others], sm_recv)
        landed(sb.at[others], sm_send)
        total = jnp.sum(sb[...], axis=0)
        rate = lr_ref[0, 0]
        v_new = MOMENTUM * v_bn[...] + rate * (total[0:SUB] * (1.0 / DEV))
        vb_new = MOMENTUM * total[2 * SUB:] + rate * (total[SUB:2 * SUB] * (1.0 / (DEV * dbuf.shape[1])))
        svnew[0:SUB, :] = v_new
        svnew[SUB:2 * SUB, :] = vb_new
        svnew[2 * SUB:, :] = w_bias[...] - vb_new
        snew[...] = w_bn[aligned(me * SUB, SUB), :] - v_new

    def sent(slot):
        for level in range(4):
            drain(8 >> level, send_sems[level].at[slot])

    def rs_start(c):
        slot = c % NSLOT

        @pl.when(c >= NSLOT)
        def _():
            sent(slot)
            pl.semaphore_wait(cd_sem, 1)
        x1, x2, x3 = order(c)
        pieces = [(q, 2 * (chip + (q // 4) * x1 + ((q // 2) % 2) * x2 + (q % 2) * x3))
                  for q in (4, 5, 6, 7, 0, 1, 2, 3)]

        def to_partner(src, q):
            remote(src, rd.at[slot, q], ds_sem.at[slot], dr_sem.at[slot], partner).start()

        def go_all(view):
            for q, p in pieces:
                to_partner(view(p + 1 - core), q)
                local(view(p + core), acc.at[slot, q], load_sem.at[slot]).start()
        chunk_views(c, (gm, gs, go, gi, g0), go_all)

        @pl.when(c >= FC0)
        def _():
            for q, p in pieces:
                to_partner(fcg.at[c - FC0, p + 1 - core], q)
            for q, p in pieces:
                acc[slot, q] = fcg[c - FC0, p + core]

    def rs_fold(c, level):
        slot, half = c % NSLOT, 4 >> level
        came, going = (rd, r1, r2, r3)[level:level + 2]
        dev = 2 * (chip + order(c)[level]) + core
        if level == 0:
            @pl.when(c < FC0)
            def _():
                drain(8, load_sem.at[slot])
        drain(2 * half, recv_sems[level].at[slot])
        acc[slot, half:2 * half] = acc[slot, half:2 * half] + came[slot, half:2 * half]

        @pl.when(c >= NSLOT)
        def _():
            pl.semaphore_wait(credits[level + 1].at[c % 3], 1)
        remote(acc.at[slot, pl.ds(half, half)], going.at[slot], send_sems[level + 1].at[slot],
               recv_sems[level + 1].at[slot], dev).start()
        acc[slot, 0:half] = acc[slot, 0:half] + came[slot, 0:half]
        give_credit(c, level)

    def give_credit(c, level):
        @pl.when(c + NSLOT < NCH)
        def _():
            if level == 0:
                signal(cd_sem, partner)
            else:
                signal(credits[level].at[c % 3], 2 * (chip + order(c)[level - 1]) + core)

    def fold(x):
        y = jnp.sum(x * x, axis=0, keepdims=True)
        return sum(y[:, i:i + LANES] for i in range(0, CW, LANES))

    def rs_end(c):
        slot = c % NSLOT
        drain(1, recv_sems[3].at[slot])
        scale = jnp.where(c >= FC0, 1.0 / (DEV * dbuf.shape[1]), 1.0 / DEV).astype(F32)
        g = (acc[slot, 0] + r3[slot, 0]) * scale
        grad[c] = g
        t = tensor_of(c)
        sums[pl.ds(t, 1), :] = sums[pl.ds(t, 1), :] + fold(g)
        give_credit(c, 3)

    def weight_sums(c):
        t = pl.ds(SUB + tensor_of(c), 1)
        sums[t, :] = sums[t, :] + fold(wbuf[c])

    def norms_out(n):
        nb[n, me] = sums[...]
        each_other(lambda dev: remote(nb.at[n, me], nb.at[n, me], nb_send.at[n], nb_recv.at[n], dev).start())

    def norms_in(n):
        landed(nb.at[n, others], nb_recv.at[n])
        landed(nb.at[n, others], nb_send.at[n])
        total = jnp.sum(nb[n], axis=0)
        norm = jnp.sqrt(jnp.broadcast_to(jnp.sum(total, axis=1, keepdims=True), (2 * SUB, LANES)))
        g_norm, w_norm = norm[0:SUB], norm[SUB:]
        ratio = jnp.where((w_norm > 0) & (g_norm > 0), TRUST_COEF * w_norm / (g_norm + DECAY * w_norm), 1.0)
        tr[...] = lr_ref[0, 0] * ratio

    def update(a):
        rate = tr[pl.ds(tensor_of(a), 1), :]
        for i in range(0, CW, LANES):
            s = slice(i, i + LANES)
            w = wbuf[a, :, s]
            v = MOMENTUM * vbuf[a, :, s] + rate * (grad[a, :, s] + DECAY * w)
            vbuf[a, :, s] = v
            wbuf[a, :, s] = w - v

    def ag_send(src, a, p, recv, dev):
        remote(src, o_ref.at[a, p], as_sem.at[a % NSEND], recv.at[a], dev).start()

    def ag_pass(a, n):
        x1, x2, x3 = order(a)
        e = [me + 2 * ((q % 2) * x1 + ((q // 2) % 2) * x2 + (q // 4) * x3) for q in range(8)]
        level = n.bit_length() - 1
        held = [wbuf.at[a]] + [o_ref.at[a, p] for p in e[1:n]]
        if n > 1:
            drain(n // 2, ag_sems[level - 1].at[a])
        if n < 8:
            for q in range(n):
                ag_send(held[q], a, e[q], ag_sems[level], e[n])
        for q in range(n // 2, n):
            ag_send(held[q], a, e[q], ad_sem, partner)

    def ag_first(a):
        @pl.when(a >= NSEND)
        def _():
            drain(DEV - 1, as_sem.at[a % NSEND])
        ag_pass(a, 1)
        local(wbuf.at[a], o_ref.at[a, me], loc_sem).start()
        strips(a, (nm, ns, no, ni, n0), lambda dst, src: local(src, dst, vn_sem).start())

    def ag_end(a):
        drain(8, ad_sem.at[a])

    def stage(s, lag, fn, count=NCH):
        c = s - lag

        @pl.when((c >= 0) & (c < count))
        def _():
            fn(c)

    def start_loads():
        local(d_ref, dbuf, misc_sem).start()
        local(x_ref, xbuf, x_sem).start()
        each_other(lambda dev: remote(g_bn.at[dev], sb.at[me, pl.ds(0, SUB)], sm_send, sm_recv, dev).start())
        sums[...] = jnp.zeros_like(sums)
        state()

    def first_products():
        landed(dbuf, misc_sem)
        landed(xbuf, x_sem)
        local(g_bn.at[me], sb.at[me, pl.ds(0, SUB)], misc_sem).start()
        bias_out()

    def small_tensors():
        state_wait()
        small_update()

    def small_back():
        each_other(lambda dev: remote(snew, so_ref.at[me], so_send, so_recv, dev).start())
        local(snew, so_ref.at[me], misc_sem).start()
        local(svnew, sv_ref, x_sem).start()

    def fc_moments():
        for b in range(U):
            local(vbuf.at[FC0 + b // 4, :, pl.ds(b % 4 * LANES, LANES)], nf.at[pl.ds(b * U, U)], vn_sem).start()

    def step(s):
        for at, fn in ((2, start_loads), (MM0, first_products), (SMALL, small_tensors), (SMALL + 1, small_back),
                       (AG0 + NCH + FIRST + 1, fc_moments)):
            pl.when(s == at)(fn)
        for n, at in enumerate((SPLIT, NCH)):
            pl.when(s == at + LAGS[3])(functools.partial(norms_out, n))
            pl.when(s == at + LAGS[3] + 4)(functools.partial(norms_in, n))
        stage(s, LAGS[3], rs_end)
        for level in (2, 1, 0):
            stage(s, LAGS[level], functools.partial(rs_fold, level=level))
        stage(s, 0, rs_start)
        stage(s, AG0 + AGEND, ag_end)
        for n, lag in AGLAGS[::-1]:
            stage(s, AG0 + lag, functools.partial(ag_pass, n=n))
        stage(s, AG0 + FIRST, ag_first)
        stage(s, AG0, update)
        stage(s, MM0, fc_block, DEV // 2)

    barrier = pltpu.get_barrier_semaphore()
    each_other(lambda dev: signal(barrier, dev))
    pl.semaphore_wait(barrier, DEV - 1)
    loop(0, AG0 + NCH + AGEND, step)

    loop(NCH - NSLOT, NCH, lambda c: sent(c % NSLOT))
    loop(NCH - NSEND, NCH, lambda a: drain(DEV - 1, as_sem.at[a % NSEND]))
    landed(snew, misc_sem)
    landed(svnew, x_sem)
    landed(so_ref.at[others], so_recv)
    landed(so_ref.at[others], so_send)
    landed(wbuf, loc_sem)
    landed(vbuf, vn_sem)


def run_comm(lr, grads, pooled, dlogits, weights, moments, small):
    unit = (U, CW)
    anyspec = pl.BlockSpec(memory_space=pl.ANY)
    vspec = pl.BlockSpec(memory_space=pltpu.VMEM)
    dma = pltpu.SemaphoreType.DMA
    reg = pltpu.SemaphoreType.REGULAR
    tile = (SUB, LANES)

    def vmem(*shape, dtype=F32):
        return pltpu.VMEM(shape, dtype)
    return pl.pallas_call(
        comm_kernel,
        out_shape=[jax.ShapeDtypeStruct(s, F32) for s in (
            [(NCH, DEV) + unit] + [v.shape for v in moments] + [(DEV,) + tile, (3 * SUB, LANES)])],
        in_specs=[pl.BlockSpec(memory_space=pltpu.SMEM)] + [anyspec] * 20 + [vspec] * 4,
        out_specs=[anyspec] * 9,
        scratch_shapes=[vmem(NSLOT, n, *unit) for n in (8, 8, 4, 2, 1)] + [vmem(NCH, *unit)] * 3
        + [vmem(*pooled.shape, dtype=BF16), vmem(*dlogits.shape, dtype=BF16),
           vmem(NCH - FC0, DEV, *unit),
           vmem(2 * SUB, LANES), vmem(2, DEV, 2 * SUB, LANES), vmem(*tile),
           vmem(DEV, 3 * SUB, LANES), vmem(2 * SUB, LANES), vmem(*tile), vmem(3 * SUB, LANES)]
        + [dma((NSLOT,))] * 9 + [dma] * 10 + [dma((2,))] * 2 + [dma((NCH,))] * 4 + [dma((NSEND,))]
        + [reg] + [reg((3,))] * 3,
        compiler_params=pltpu.CompilerParams(collective_id=0, has_side_effects=True,
                                             vmem_limit_bytes=60 * 1024 * 1024),
        name='lars_comm',
    )(lr, *grads, pooled, dlogits, *weights, *moments, *small)


NBUF = 6
AHEAD = 3
NFC = 4


def write_kernel(o_ref, nm, ns, no, ni, n0, nf, so_ref, sv_ref, om, os_, oo, oi, o0, of, bm, bs, bo, bi, b0, bf,
                 vm, vs, vo, vi, v0, vf, bn, vbn, vb, wb,
                 buf, bbuf, fbuf, fbbuf, in_sem, f_sem, b_sem, v_sem):
    def view(c, refs):
        entry, ref = [(e, r) for e, r in zip(TABLE, refs) if c >= e[0]][-1]
        i, row, col = unit_at(entry, c)
        return ref.at[i, :, pl.ds(row, U), pl.ds(col, CW)]

    def load(i):
        return [pltpu.make_async_copy(o_ref.at[i], buf.at[i % NBUF], in_sem.at[i % NBUF])]

    def stores(i):
        slot = i % NBUF
        if i < FC0:
            pairs = [(buf.at[slot], view(i, (om, os_, oo, oi, o0))), (bbuf.at[slot], view(i, (bm, bs, bo, bi, b0)))]
        else:
            size = min(LANES, CLASSES - LANES * (i - FC0))
            have, want = pl.ds(0, size), pl.ds(LANES * (i - FC0), size)
            pairs = [(fbuf.at[i % NFC, have], of.at[want]), (fbbuf.at[i % NFC, have], bf.at[want])]
        return [pltpu.make_async_copy(*pairs[0], f_sem.at[slot]), pltpu.make_async_copy(*pairs[1], b_sem.at[slot])]

    done = []

    def settle(upto):
        while len(done) <= upto:
            for d in stores(len(done)):
                d.wait()
            done.append(True)

    for i in range(AHEAD):
        for d in load(i):
            d.start()
    v_outs = [pltpu.make_async_copy(src, dst, v_sem) for src, dst in
              ((nm, vm), (ns, vs), (no, vo), (ni, vi), (n0, v0), (nf.at[pl.ds(0, CLASSES)], vf))]
    bn[...] = so_ref[...]
    vbn[...] = sv_ref[0:SUB]
    vb[...] = sv_ref[SUB:2 * SUB]
    wb[...] = sv_ref[2 * SUB:]
    for i in range(NCH):
        slot = i % NBUF
        for d in load(i):
            d.wait()
        if i < FC0:
            def cast(p, _):
                bbuf[slot, p] = buf[slot, p].astype(BF16)
                return 0
            lax.fori_loop(0, DEV, cast, 0)
        else:
            settle(i - NFC)
            for p in range(DEV):
                for r in range(CW // LANES):
                    x = buf[slot, p, :, LANES * r:LANES * (r + 1)]
                    at = (slice(U * r, U * (r + 1)), slice(LANES * p, LANES * (p + 1)))
                    fbuf[(i % NFC,) + at] = x
                    fbbuf[(i % NFC,) + at] = x.astype(BF16)
        for d in stores(i):
            d.start()
        if i == AHEAD:
            for d in v_outs:
                d.start()
        if i + AHEAD < NCH:
            settle(i + AHEAD - NBUF)
            for d in load(i + AHEAD):
                d.start()
    settle(NCH - 1)
    for d in v_outs:
        d.wait()


def run_write(o, moments_new, so, sv):
    anyspec = pl.BlockSpec(memory_space=pl.ANY)
    vspec = pl.BlockSpec(memory_space=pltpu.VMEM)
    shapes = [dshape(*e, DEV) for e in TABLE] + [(CLASSES, DEV * LANES)]
    moments = [(e[1] * e[2] * LANES, LANES) for e in TABLE] + [(CLASSES, LANES)]
    tile = (SUB, LANES)
    dma = pltpu.SemaphoreType.DMA
    outs = [(s, F32) for s in shapes] + [(s, BF16) for s in shapes] + [(s, F32) for s in moments]
    outs += [((DEV,) + tile, F32)] + [(tile, F32)] * 3
    return pl.pallas_call(
        write_kernel,
        out_shape=[jax.ShapeDtypeStruct(*s) for s in outs],
        in_specs=[anyspec] + [vspec] * 8,
        out_specs=[anyspec] * 18 + [vspec] * 4,
        scratch_shapes=[
            pltpu.VMEM((NBUF, DEV, U, CW), F32), pltpu.VMEM((NBUF, DEV, U, CW), BF16),
            pltpu.VMEM((NFC, LANES, DEV * LANES), F32), pltpu.VMEM((NFC, LANES, DEV * LANES), BF16),
            dma((NBUF,)), dma((NBUF,)), dma((NBUF,)), dma],
        compiler_params=pltpu.CompilerParams(vmem_limit_bytes=48 * 1024 * 1024),
        name='write_out',
    )(o, *moments_new, so, sv)


def solution(mesh):
    n_dev = mesh.shape['dp']
    assert n_dev == DEV
    full, lead, cols = P(), P('dp'), P(None, 'dp')
    moment_specs = (lead, lead, cols, cols, cols, lead, lead, lead)
    in_specs = (full,) * 8 + (lead,) * 8 + moment_specs + (full,)
    out_specs = (full,) * 14 + moment_specs

    def body(w_in0, w_short, w_in, w_mid, w_out, w_fc, w_bn, w_bias,
             g_in0, g_short, g_in, g_mid, g_out, g_bn, pooled, dlogits,
             v_in0, v_short, v_in, v_mid, v_out, v_fc, v_bn, v_bias, learn_rate):
        rank = lax.axis_index('dp')
        width = v_bias.shape[0]
        shapes = [dshape(*e, DEV) for e in TABLE]
        grads = [g.reshape(s) for g, s in zip((g_mid, g_short, g_out, g_in, g_in0), shapes)]
        weights = [w.reshape(s) for w, s in zip((w_mid, w_short, w_out, w_in, w_in0), shapes)] + [w_fc.T]

        def to_rows(v, entry):
            _, stack, _, blocks = entry
            return v.reshape(stack, -1, LANES).transpose(1, 0, 2).reshape(-1, blocks * CW // LANES, stack, 1, LANES)

        def from_rows(v, stack, like):
            return v.reshape(-1, stack, LANES).transpose(1, 0, 2).reshape(like.shape)
        olds = (v_mid, v_short, v_out, v_in, v_in0)
        moments = [to_rows(v, e) for v, e in zip(olds, TABLE)]
        moments.append(jnp.pad(v_fc.reshape(LANES, CLASSES).T, ((0, SUB * LANES - CLASSES), (0, 0))))
        tiles = (-1, SUB, LANES)
        pad = SUB * LANES
        placed = lax.dynamic_update_slice(jnp.zeros((pad,), F32), v_bias, (rank * width,))
        small = [g_bn.reshape(tiles), w_bn.reshape(-1, LANES), v_bn.reshape(SUB, LANES),
                 jnp.pad(w_bias, (0, pad - CLASSES)).reshape(SUB, LANES), placed.reshape(SUB, LANES)]
        o, *made, so, sv = run_comm(learn_rate.reshape(1, 1), grads, pooled, dlogits.T, weights, moments, small)
        mid, short, out, inn, in0, fc, mid_b, short_b, out_b, inn_b, in0_b, fc_b, *rest = run_write(o, [v.reshape(-1, LANES) for v in made], so, sv)
        vm, vs, vo, vi, v0, vf, bn, vbn, vb, wb = rest
        news = [from_rows(v, e[1], old) for v, e, old in zip((vm, vs, vo, vi, v0), TABLE, olds)]
        return (in0.reshape(w_in0.shape), short.reshape(w_short.shape), inn.reshape(w_in.shape),
                mid.reshape(w_mid.shape), out.reshape(w_out.shape), fc.T,
                bn.reshape(w_bn.shape), wb.reshape(-1)[:CLASSES],
                in0_b.reshape(w_in0.shape), short_b.reshape(w_short.shape), inn_b.reshape(w_in.shape),
                mid_b.reshape(w_mid.shape), out_b.reshape(w_out.shape), fc_b.T,
                news[4], news[1], news[3], news[0], news[2], vf.T.reshape(v_fc.shape),
                vbn.reshape(v_bn.shape), lax.dynamic_slice_in_dim(vb.reshape(-1), rank * width, width))

    return jax.shard_map(body, mesh=mesh, in_specs=in_specs, out_specs=out_specs, check_vma=False)
```

time: 993 us -> 403 us (0.41); the launches traced: 981 us -> 402 us
  Pallas kernels: 0 us -> 387 us
  waiting for transfers between devices: 372 us -> 0 us
  local copies, waits for them, and re-layouts: 263 us -> 14.4 us
  other arithmetic: 233 us -> 0 us
  blocking collectives: 81 us -> 0 us
  between operations: 20.7 us -> 1.37 us
  matrix products: 10.8 us -> 0 us
    pallas_call x0 -> x2, Pallas kernels: none -> 387 us  [the longest x1 343 us: run_comm(): pl.pallas_call(comm_kernel, out_shape=[jax.ShapeDtypeStruct(s, F32) for s...]
    unnamed x12 -> x0, waiting for transfers between devices: 318 us -> none
    unnamed x42 -> x18, local copies, waits for them, and re-layouts: 158 us -> 7.79 us
    all_gather x3 -> x0, other arithmetic: 149 us -> none  [body(): lax.all_gather(w_part - moment_next, 'dp', axis=1, tiled=True)]
    reshape x6 -> x4, local copies, waits for them, and re-layouts: 98.7 us -> 4.2 us  [the longest x2 1.64 us: body(): v_fc.reshape(LANES, CLASSES)]
    all_gather x6 -> x0, waiting for transfers between devices: 53.7 us -> none  [body(): lax.all_gather(w_part - moment_next, 'dp', axis=1, tiled=True)]
    convert_element_type x6 -> x0, other arithmetic: 34.4 us -> none  [body(): kernels_bf.append(w_full.astype(jnp.bfloat16))]
    unnamed x1 -> x0, blocking collectives: 34.2 us -> none
  transfers between devices with their start and end apart: 9 -> 0, of which waited for: 4 -> 0; matrix products, arithmetic and copies ran while one was open for 45% -> 0% of each run, Pallas kernels for 0% -> 0%
where the time goes in v2:
time: 403 us; the launch traced here: 402 us
  Pallas kernels  387 us (96%)
  local copies, waits for them, and re-layouts  14.4 us (4%)
    pallas_call x1, Pallas kernels, run_comm(): pl.pallas_call(comm_kernel, out_shape=[jax.ShapeDtypeStruct(s, F32) for s...  343 us
    pallas_call x1, Pallas kernels, run_write(): pl.pallas_call(write_kernel, out_shape=[jax.ShapeDtypeStruct(*s) for s in...  43.4 us

profile of v2, /device:TPU:1, one launch (start us, length us, event | category | flops | bytes accessed | tf_op | source)
XLA Modules:
  0.0 402.3 jit_solution(12603355902127669208)
XLA Ops:
  1.3 1.3 pad_bitcast_fusion.w_bias
  2.6 0.8 dynamic_update_slice.3
  3.4 0.0 copy-start.8
  3.4 1.5 reshape.194
  4.9 0.2 copy.53
  5.1 0.8 pad.8.vf
  5.9 0.0 copy-done.8
  5.9 343.1 %lars_comm.1 = (f32[48,16,32,512]{3,2,1,0:T(8,128)}, f32[288,4,2,1,128]{4,3,2,1,0:T(1,128)}, f32[64,16,1,1,128]{4,3,2,1,0:T(1,128)}, f32[32,16,2,1,128]{4,3,2,1,...) custom-call(f32[1,1]{1,0:T(1,128)} %bitcast.69.lr_ref, ...), custom_call_target="tpu_custom_call" | custom-call | tf_op jit(solution)/shard_map/lars_comm/pallas_call | solution.py:383
  349.1 0.0 copy-start
  349.1 1.3 copy-done
  350.3 0.0 copy-start.1
  350.3 1.0 copy-done.1
  351.4 0.0 copy-start.2
  351.4 1.0 copy-done.2
  352.4 0.0 copy-start.3
  352.4 1.0 copy-done.3
  353.5 0.0 copy-start.4
  353.5 0.9 copy-done.4
  354.4 0.0 copy-start.5
  354.4 0.9 copy-done.5
  355.3 0.0 copy-start.6
  355.3 0.8 copy-done.6
  356.2 0.0 copy-start.7
  356.2 0.7 copy-done.7
  356.9 43.4 %write_out.1 = (f32[2,16,288,512]{3,2,1,0:T(8,128)}, f32[1,16,64,2048]{3,2,1,0:T(8,128)}, f32[2,16,32,2048]{3,2,1,0:T(8,128)}, f32[1,16,128,512]{3,2,1,0:T(8,128...) custom-call(f32[48,16,32,512]{3,2,1,0:T(8,128)} %get-tuple-element.5, ...), custom_call_target="tpu_custom_call" | custom-call | tf_op jit(solution)/shard_map/write_out/pallas_call | solution.py:485
  400.3 0.6 dynamic_slice.3
  400.9 0.2 copy.56
  401.1 1.3 reshape.221
  (1 shorter events, 0.0 us)
Async XLA Ops:
  3.4 2.5 copy-start.8
  349.1 1.3 copy-start
  350.3 1.0 copy-start.1
  351.4 1.0 copy-start.2
  352.4 1.0 copy-start.3
  353.5 0.9 copy-start.4
  354.4 0.9 copy-start.5
  355.3 0.8 copy-start.6
  356.2 0.7 copy-start.7

commit v3 on v2

--- a/solution.py
+++ b/solution.py
@@ -29,8 +29,9 @@
 AGLAGS = ((2, 5), (4, 10), (8, 16))
 AGEND = 20
 NSEND = 18
-MM0 = 5
-SMALL = 16
+LOAD0 = 6
+MM0 = 12
+SMALL = 34
 
 
 def tensor_of(c):
@@ -115,19 +116,21 @@
 
     def load_state(c):
         chunk_views(c, (wm, ws, wo, wi, w0), lambda view: local(view(me), wbuf.at[c], w_sem).start())
-
-    def state():
-        loop(0, FC0, load_state)
-        loop(0, FC0, lambda c: strips(c, (vm, vs, vo, vi, v0), lambda src, dst: local(src, dst, v_sem).start()))
+        strips(c, (vm, vs, vo, vi, v0), lambda src, dst: local(src, dst, v_sem).start())
         lane = aligned(me * LANES, LANES)
-        for b in range(CLASSES // U):
-            dst = wbuf.at[FC0 + b // 4, :, pl.ds(b % 4 * LANES, LANES)]
-            local(wf.at[pl.ds(b * U, U), lane], dst, w_sem).start()
-        local(wf.at[pl.ds(LASTROW, SUB), lane], wbuf.at[NCH - 1, pl.ds(0, SUB), pl.ds(CW - LANES, LANES)], w_sem).start()
-        wbuf[NCH - 1, SUB:, CW - LANES:] = jnp.zeros((U - SUB, LANES), F32)
-        for b in range(U):
-            dst = vbuf.at[FC0 + b // 4, :, pl.ds(b % 4 * LANES, LANES)]
-            local(vf.at[pl.ds(b * U, U)], dst, v_sem).start()
+
+        def classifier(sizes):
+            for i, size in enumerate(sizes):
+                rows = pl.ds(pl.multiple_of((c - FC0) * LANES, LANES) + i * U, size)
+                part = (c, pl.ds(0, size), pl.ds(i * LANES, LANES))
+                local(wf.at[rows, lane], wbuf.at[part], w_sem).start()
+                local(vf.at[rows], vbuf.at[part], v_sem).start()
+        pl.when((c >= FC0) & (c < NCH - 1))(functools.partial(classifier, (U, U, U, U)))
+        pl.when(c == NCH - 1)(functools.partial(classifier, (U, U, U, SUB)))
+
+    def load_two(c):
+        load_state(2 * c)
+        load_state(2 * c + 1)
 
     def strips(c, refs, fn):
         for entry, ref in zip(TABLE, refs):
@@ -140,10 +143,11 @@
                     fn(ref.at[aligned(row, U), col // LANES + b, i, 0, :], vbuf.at[c, :, pl.ds(b * LANES, LANES)])
 
     def state_wait():
-        landed(wbuf.at[pl.ds(0, NCH - 1)], w_sem)
-        landed(wbuf.at[NCH - 1, :, pl.ds(0, CW - LANES)], w_sem)
-        landed(wbuf.at[NCH - 1, pl.ds(0, SUB), pl.ds(CW - LANES, LANES)], w_sem)
-        landed(vbuf, v_sem)
+        for buf, sem in ((wbuf, w_sem), (vbuf, v_sem)):
+            landed(buf.at[pl.ds(0, NCH - 1)], sem)
+            landed(buf.at[NCH - 1, :, pl.ds(0, CW - LANES)], sem)
+            landed(buf.at[NCH - 1, pl.ds(0, SUB), pl.ds(CW - LANES, LANES)], sem)
+            buf[NCH - 1, SUB:, CW - LANES:] = jnp.zeros((U - SUB, LANES), F32)
         loop(0, NCH, weight_sums)
 
     def fc_block(b):
@@ -176,7 +180,11 @@
         vb_new = MOMENTUM * total[2 * SUB:] + rate * (total[SUB:2 * SUB] * (1.0 / (DEV * dbuf.shape[1])))
         svnew[0:SUB, :] = v_new
         svnew[SUB:2 * SUB, :] = vb_new
-        svnew[2 * SUB:, :] = w_bias[...] - vb_new
+        for i in range(SUB):
+            part = w_bias[:, i * LANES:min(CLASSES, (i + 1) * LANES)]
+            row = slice(2 * SUB + i, 2 * SUB + i + 1)
+            svnew[row, :] = jnp.zeros((1, LANES), F32)
+            svnew[row, :part.shape[1]] = part - vb_new[i:i + 1, :part.shape[1]]
         snew[...] = w_bn[aligned(me * SUB, SUB), :] - v_new
 
     def sent(slot):
@@ -311,12 +319,9 @@
         def _():
             fn(c)
 
-    def start_loads():
-        local(d_ref, dbuf, misc_sem).start()
-        local(x_ref, xbuf, x_sem).start()
+    def start_small():
         each_other(lambda dev: remote(g_bn.at[dev], sb.at[me, pl.ds(0, SUB)], sm_send, sm_recv, dev).start())
         sums[...] = jnp.zeros_like(sums)
-        state()
 
     def first_products():
         landed(dbuf, misc_sem)
@@ -334,11 +339,12 @@
         local(svnew, sv_ref, x_sem).start()
 
     def fc_moments():
-        for b in range(U):
+        for b in range(CLASSES // U):
             local(vbuf.at[FC0 + b // 4, :, pl.ds(b % 4 * LANES, LANES)], nf.at[pl.ds(b * U, U)], vn_sem).start()
+        local(vbuf.at[NCH - 1, pl.ds(0, SUB), pl.ds(CW - LANES, LANES)], nf.at[pl.ds(LASTROW, SUB)], vn_sem).start()
 
     def step(s):
-        for at, fn in ((2, start_loads), (MM0, first_products), (SMALL, small_tensors), (SMALL + 1, small_back),
+        for at, fn in ((LOAD0, start_small), (MM0, first_products), (SMALL, small_tensors), (SMALL + 1, small_back),
                        (AG0 + NCH + FIRST + 1, fc_moments)):
             pl.when(s == at)(fn)
         for n, at in enumerate((SPLIT, NCH)):
@@ -354,7 +360,10 @@
         stage(s, AG0 + FIRST, ag_first)
         stage(s, AG0, update)
         stage(s, MM0, fc_block, DEV // 2)
-
+        stage(s, LOAD0, load_two, NCH // 2)
+
+    local(d_ref, dbuf, misc_sem).start()
+    local(x_ref, xbuf, x_sem).start()
     barrier = pltpu.get_barrier_semaphore()
     each_other(lambda dev: signal(barrier, dev))
     pl.semaphore_wait(barrier, DEV - 1)
@@ -367,7 +376,8 @@
     landed(so_ref.at[others], so_recv)
     landed(so_ref.at[others], so_send)
     landed(wbuf, loc_sem)
-    landed(vbuf, vn_sem)
+    landed(vbuf.at[pl.ds(0, FC0)], vn_sem)
+    landed(nf, vn_sem)
 
 
 def run_comm(lr, grads, pooled, dlogits, weights, moments, small):
@@ -399,14 +409,14 @@
     )(lr, *grads, pooled, dlogits, *weights, *moments, *small)
 
 
-NBUF = 6
-AHEAD = 3
+NBUF = 12
+AHEAD = 6
 NFC = 4
 
 
 def write_kernel(o_ref, nm, ns, no, ni, n0, nf, so_ref, sv_ref, om, os_, oo, oi, o0, of, bm, bs, bo, bi, b0, bf,
                  vm, vs, vo, vi, v0, vf, bn, vbn, vb, wb,
-                 buf, bbuf, fbuf, fbbuf, in_sem, f_sem, b_sem, v_sem):
+                 buf, bbuf, fbuf, fbbuf, vbuf, in_sem, f_sem, b_sem, v_sem):
     def view(c, refs):
         entry, ref = [(e, r) for e, r in zip(TABLE, refs) if c >= e[0]][-1]
         i, row, col = unit_at(entry, c)
@@ -436,8 +446,17 @@
     for i in range(AHEAD):
         for d in load(i):
             d.start()
-    v_outs = [pltpu.make_async_copy(src, dst, v_sem) for src, dst in
-              ((nm, vm), (ns, vs), (no, vo), (ni, vi), (n0, v0), (nf.at[pl.ds(0, CLASSES)], vf))]
+    firsts = [e[0] * LANES for e in TABLE] + [FC0 * LANES]
+
+    def moments(refs, back):
+        out = []
+        for first, ref in zip(firsts, refs):
+            pair = (ref, vbuf.at[pl.ds(first, ref.shape[0])])
+            out.append(pltpu.make_async_copy(*(pair[::-1] if back else pair), v_sem))
+        return out
+    v_ins, v_outs = moments((nm, ns, no, ni, n0, nf), False), moments((vm, vs, vo, vi, v0, vf), True)
+    for d in v_ins:
+        d.start()
     bn[...] = so_ref[...]
     vbn[...] = sv_ref[0:SUB]
     vb[...] = sv_ref[SUB:2 * SUB]
@@ -462,6 +481,8 @@
         for d in stores(i):
             d.start()
         if i == AHEAD:
+            for d in v_ins:
+                d.wait()
             for d in v_outs:
                 d.start()
         if i + AHEAD < NCH:
@@ -485,13 +506,14 @@
     return pl.pallas_call(
         write_kernel,
         out_shape=[jax.ShapeDtypeStruct(*s) for s in outs],
-        in_specs=[anyspec] + [vspec] * 8,
+        in_specs=[anyspec] * 7 + [vspec] * 2,
         out_specs=[anyspec] * 18 + [vspec] * 4,
         scratch_shapes=[
             pltpu.VMEM((NBUF, DEV, U, CW), F32), pltpu.VMEM((NBUF, DEV, U, CW), BF16),
             pltpu.VMEM((NFC, LANES, DEV * LANES), F32), pltpu.VMEM((NFC, LANES, DEV * LANES), BF16),
+            pltpu.VMEM((FC0 * LANES + CLASSES, LANES), F32),
             dma((NBUF,)), dma((NBUF,)), dma((NBUF,)), dma],
-        compiler_params=pltpu.CompilerParams(vmem_limit_bytes=48 * 1024 * 1024),
+        compiler_params=pltpu.CompilerParams(vmem_limit_bytes=62 * 1024 * 1024),
         name='write_out',
     )(o, *moments_new, so, sv)
 
@@ -521,12 +543,12 @@
             return v.reshape(-1, stack, LANES).transpose(1, 0, 2).reshape(like.shape)
         olds = (v_mid, v_short, v_out, v_in, v_in0)
         moments = [to_rows(v, e) for v, e in zip(olds, TABLE)]
-        moments.append(jnp.pad(v_fc.reshape(LANES, CLASSES).T, ((0, SUB * LANES - CLASSES), (0, 0))))
+        moments.append(v_fc.reshape(LANES, CLASSES).T)
         tiles = (-1, SUB, LANES)
         pad = SUB * LANES
         placed = lax.dynamic_update_slice(jnp.zeros((pad,), F32), v_bias, (rank * width,))
         small = [g_bn.reshape(tiles), w_bn.reshape(-1, LANES), v_bn.reshape(SUB, LANES),
-                 jnp.pad(w_bias, (0, pad - CLASSES)).reshape(SUB, LANES), placed.reshape(SUB, LANES)]
+                 w_bias.reshape(1, CLASSES), placed.reshape(SUB, LANES)]
         o, *made, so, sv = run_comm(learn_rate.reshape(1, 1), grads, pooled, dlogits.T, weights, moments, small)
         mid, short, out, inn, in0, fc, mid_b, short_b, out_b, inn_b, in0_b, fc_b, *rest = run_write(o, [v.reshape(-1, LANES) for v in made], so, sv)
         vm, vs, vo, vi, v0, vf, bn, vbn, vb, wb = rest

time: 403 us -> 390 us (0.968)
  local copies, waits for them, and re-layouts: 14.4 us -> 7.08 us
  Pallas kernels: 387 us -> 381 us
    unnamed x18 -> x2, local copies, waits for them, and re-layouts: 7.79 us -> 0.01 us
    pallas_call x1, Pallas kernels: 343 us -> 337 us  [run_comm(): pl.pallas_call(comm_kernel, out_shape=[jax.ShapeDtypeStruct(s, F32) for s...]
where the time goes in v3:
time: 390 us
  Pallas kernels  381 us (98%)
  local copies, waits for them, and re-layouts  7.08 us (2%)
    pallas_call x1, Pallas kernels, run_comm(): pl.pallas_call(comm_kernel, out_shape=[jax.ShapeDtypeStruct(s, F32) for s...  337 us
    pallas_call x1, Pallas kernels, run_write(): pl.pallas_call(write_kernel, out_shape=[jax.ShapeDtypeStruct(*s) for s in...  44.5 us

profile of v3, /device:TPU:1, one launch (start us, length us, event | category | flops | bytes accessed | tf_op | source)
XLA Modules:
  0.0 389.7 jit_solution(7115169661315253976)
XLA Ops:
  1.3 0.9 dynamic_update_slice.3
  2.2 0.0 copy-start
  2.2 1.5 reshape.194
  3.6 1.0 copy.53
  4.6 0.0 copy-done
  4.6 336.7 %lars_comm.1 = (f32[48,16,32,512]{3,2,1,0:T(8,128)}, f32[288,4,2,1,128]{4,3,2,1,0:T(1,128)}, f32[64,16,1,1,128]{4,3,2,1,0:T(1,128)}, f32[32,16,2,1,128]{4,3,2,1,...) custom-call(f32[1,1]{1,0:T(1,128)} %bitcast.68.lr_ref, ...), custom_call_target="tpu_custom_call" | custom-call | tf_op jit(solution)/shard_map/lars_comm/pallas_call | solution.py:393
  341.4 44.5 %write_out.1 = (f32[2,16,288,512]{3,2,1,0:T(8,128)}, f32[1,16,64,2048]{3,2,1,0:T(8,128)}, f32[2,16,32,2048]{3,2,1,0:T(8,128)}, f32[1,16,128,512]{3,2,1,0:T(8,128...) custom-call(f32[48,16,32,512]{3,2,1,0:T(8,128)} %get-tuple-element.5, ...), custom_call_target="tpu_custom_call" | custom-call | tf_op jit(solution)/shard_map/write_out/pallas_call | solution.py:506
  385.9 1.3 dynamic_slice.3
  387.1 1.2 copy.56
  388.4 1.3 reshape.221
  (1 shorter events, 0.0 us)
Async XLA Ops:
  2.2 2.5 copy-start

commit v4 on v3

--- a/solution.py
+++ b/solution.py
@@ -16,21 +16,24 @@
 LANES = 128
 U, CW = 32, 512
 NCH = 48
-FC0 = 40
+FC0, FCN = 22, 8
+FCL = FC0 + FCN - 1
 CLASSES, LASTROW = 1000, 992
 SUB = 8
-TABLE = ((0, 2, 9, 1), (18, 1, 8, 4), (26, 2, 4, 4), (34, 1, 4, 1), (38, 1, 2, 1))
-STARTS = (9, 18, 26, 30, 34, 38, FC0)
-SPLIT = 26
+TABLE = ((0, 1, 8, 4), (8, 2, 4, 4), (16, 1, 4, 1), (20, 1, 2, 1), (30, 2, 9, 1))
+STARTS = (8, 12, 16, 20, FC0, 30, 39)
+TAIL0 = 33
+TAILK = (NCH - TAIL0) // 3
+SPLIT = 22
 NSLOT = 15
 LAGS = (2, 6, 10, 13)
-AG0 = 43
+AG0 = 44
 FIRST = 1
 AGLAGS = ((2, 5), (4, 10), (8, 16))
 AGEND = 20
 NSEND = 18
 LOAD0 = 6
-MM0 = 12
+MM0 = 10
 SMALL = 34
 
 
@@ -48,6 +51,24 @@
     return (c - first) // per, k // blocks * U, k % blocks * CW
 
 
+def is_fc(c):
+    return (c >= FC0) & (c <= FCL)
+
+
+def strides(chip, c):
+    steps = []
+    for i in range(3):
+        d = (c + i) % 3
+        weight = 1 + d + (d * (d - 1)) // 2
+        steps.append(weight * (1 - 2 * ((chip // weight) % 2)))
+    return steps
+
+
+def devices(me, steps):
+    x1, x2, x3 = steps
+    return [me + 2 * ((q % 2) * x1 + ((q // 2) % 2) * x2 + (q // 4) * x3) for q in range(8)]
+
+
 def aligned(x, size):
     return pl.ds(x if isinstance(x, int) else pl.multiple_of(x, size), size)
 
@@ -62,9 +83,9 @@
             fn(lambda p: ref.at[i, p, aligned(row, U), aligned(col, CW)])
 
 
-def comm_kernel(lr_ref, gm, gs, go, gi, g0, x_ref, d_ref, wm, ws, wo, wi, w0, wf, vm, vs, vo, vi, v0, vf,
+def comm_kernel(lr_ref, gs, go, gi, g0, gm, x_ref, d_ref, ws, wo, wi, w0, wm, wf, vs, vo, vi, v0, vm, vf,
                 g_bn, w_bn, v_bn, w_bias, v_bias,
-                o_ref, nm, ns, no, ni, n0, nf, so_ref, sv_ref,
+                o_ref, t0, t1, t2, u0, u1, u2, ns, no, ni, n0, nm, nf, so_ref, sv_ref,
                 acc, rd, r1, r2, r3, grad, wbuf, vbuf, xbuf, dbuf, fcg,
                 sums, nb, tr, sb, bias, snew, svnew,
                 load_sem, ds_sem, dr_sem, s1_sem, p1_sem, s2_sem, p2_sem, s3_sem, p3_sem,
@@ -82,12 +103,7 @@
     others = pl.ds(0, DEV - 1)
 
     def order(c):
-        steps = []
-        for i in range(3):
-            d = (c + i) % 3
-            weight = 1 + d + (d * (d - 1)) // 2
-            steps.append(weight * (1 - 2 * ((chip // weight) % 2)))
-        return steps
+        return strides(chip, c)
 
     def remote(src, dst, send, recv, dev):
         return pltpu.make_async_remote_copy(src_ref=src, dst_ref=dst, send_sem=send, recv_sem=recv,
@@ -115,8 +131,8 @@
         loop(1, DEV, lambda d: fn((me + d) % DEV))
 
     def load_state(c):
-        chunk_views(c, (wm, ws, wo, wi, w0), lambda view: local(view(me), wbuf.at[c], w_sem).start())
-        strips(c, (vm, vs, vo, vi, v0), lambda src, dst: local(src, dst, v_sem).start())
+        chunk_views(c, (ws, wo, wi, w0, wm), lambda view: local(view(me), wbuf.at[c], w_sem).start())
+        strips(c, (vs, vo, vi, v0, vm), lambda src, dst: local(src, dst, v_sem).start())
         lane = aligned(me * LANES, LANES)
 
         def classifier(sizes):
@@ -125,8 +141,8 @@
                 part = (c, pl.ds(0, size), pl.ds(i * LANES, LANES))
                 local(wf.at[rows, lane], wbuf.at[part], w_sem).start()
                 local(vf.at[rows], vbuf.at[part], v_sem).start()
-        pl.when((c >= FC0) & (c < NCH - 1))(functools.partial(classifier, (U, U, U, U)))
-        pl.when(c == NCH - 1)(functools.partial(classifier, (U, U, U, SUB)))
+        pl.when((c >= FC0) & (c < FCL))(functools.partial(classifier, (U, U, U, U)))
+        pl.when(c == FCL)(functools.partial(classifier, (U, U, U, SUB)))
 
     def load_two(c):
         load_state(2 * c)
@@ -145,9 +161,9 @@
     def state_wait():
         for buf, sem in ((wbuf, w_sem), (vbuf, v_sem)):
             landed(buf.at[pl.ds(0, NCH - 1)], sem)
-            landed(buf.at[NCH - 1, :, pl.ds(0, CW - LANES)], sem)
-            landed(buf.at[NCH - 1, pl.ds(0, SUB), pl.ds(CW - LANES, LANES)], sem)
-            buf[NCH - 1, SUB:, CW - LANES:] = jnp.zeros((U - SUB, LANES), F32)
+            landed(buf.at[FCL, :, pl.ds(0, CW - LANES)], sem)
+            landed(buf.at[FCL, pl.ds(0, SUB), pl.ds(CW - LANES, LANES)], sem)
+            buf[FCL, SUB:, CW - LANES:] = jnp.zeros((U - SUB, LANES), F32)
         loop(0, NCH, weight_sums)
 
     def fc_block(b):
@@ -156,8 +172,8 @@
             part = y[:, h * LANES:(h + 1) * LANES]
             for g in range(CLASSES // U):
                 fcg[g // 4, 2 * b + h, :, g % 4 * LANES:(g % 4 + 1) * LANES] = part[g * U:(g + 1) * U]
-            fcg[NCH - FC0 - 1, 2 * b + h, 0:SUB, CW - LANES:] = part[LASTROW:]
-            fcg[NCH - FC0 - 1, 2 * b + h, SUB:, CW - LANES:] = jnp.zeros((U - SUB, LANES), F32)
+            fcg[FCN - 1, 2 * b + h, 0:SUB, CW - LANES:] = part[LASTROW:]
+            fcg[FCN - 1, 2 * b + h, SUB:, CW - LANES:] = jnp.zeros((U - SUB, LANES), F32)
 
     def bias_out():
         line = jnp.dot(dbuf[...], jnp.ones((dbuf.shape[1], LANES), BF16), preferred_element_type=F32)
@@ -209,9 +225,9 @@
             for q, p in pieces:
                 to_partner(view(p + 1 - core), q)
                 local(view(p + core), acc.at[slot, q], load_sem.at[slot]).start()
-        chunk_views(c, (gm, gs, go, gi, g0), go_all)
-
-        @pl.when(c >= FC0)
+        chunk_views(c, (gs, go, gi, g0, gm), go_all)
+
+        @pl.when(is_fc(c))
         def _():
             for q, p in pieces:
                 to_partner(fcg.at[c - FC0, p + 1 - core], q)
@@ -223,7 +239,7 @@
         came, going = (rd, r1, r2, r3)[level:level + 2]
         dev = 2 * (chip + order(c)[level]) + core
         if level == 0:
-            @pl.when(c < FC0)
+            @pl.when((c < FC0) | (c > FCL))
             def _():
                 drain(8, load_sem.at[slot])
         drain(2 * half, recv_sems[level].at[slot])
@@ -252,7 +268,7 @@
     def rs_end(c):
         slot = c % NSLOT
         drain(1, recv_sems[3].at[slot])
-        scale = jnp.where(c >= FC0, 1.0 / (DEV * dbuf.shape[1]), 1.0 / DEV).astype(F32)
+        scale = jnp.where(is_fc(c), 1.0 / (DEV * dbuf.shape[1]), 1.0 / DEV).astype(F32)
         g = (acc[slot, 0] + r3[slot, 0]) * scale
         grad[c] = g
         t = tensor_of(c)
@@ -285,32 +301,43 @@
             vbuf[a, :, s] = v
             wbuf[a, :, s] = w - v
 
-    def ag_send(src, a, p, recv, dev):
-        remote(src, o_ref.at[a, p], as_sem.at[a % NSEND], recv.at[a], dev).start()
-
-    def ag_pass(a, n):
-        x1, x2, x3 = order(a)
-        e = [me + 2 * ((q % 2) * x1 + ((q // 2) % 2) * x2 + (q // 4) * x3) for q in range(8)]
+    def ag_send(src, dst, a, recv, dev):
+        remote(src, dst, as_sem.at[a % NSEND], recv.at[a], dev).start()
+
+    def ag_pass(a, n, dst, mirror, last):
+        e = devices(me, order(a))
         level = n.bit_length() - 1
-        held = [wbuf.at[a]] + [o_ref.at[a, p] for p in e[1:n]]
+        held = [wbuf.at[a]] + [dst(e[q], q) for q in range(1, n)]
         if n > 1:
             drain(n // 2, ag_sems[level - 1].at[a])
+        if not last:
+            for q in range(n):
+                ag_send(held[q], dst(e[q], q + n), a, ag_sems[level], e[n])
+        for q in range(n // 2, n):
+            ag_send(held[q], mirror(e[q], q), a, ad_sem, partner)
+        if n == 1:
+            local(wbuf.at[a], dst(me, 0), loc_sem).start()
+
+    def gather(a, n):
+        if n == 1:
+            @pl.when(a >= NSEND)
+            def _():
+                drain(DEV - 1, as_sem.at[a % NSEND])
+            strips(a, (ns, no, ni, n0, nm), lambda dst, src: local(src, dst, vn_sem).start())
+
+        @pl.when(a < TAIL0)
+        def _():
+            ag_pass(a, n, lambda p, q: o_ref.at[a, p], lambda p, q: o_ref.at[a, p], n == 8)
         if n < 8:
-            for q in range(n):
-                ag_send(held[q], a, e[q], ag_sems[level], e[n])
-        for q in range(n // 2, n):
-            ag_send(held[q], a, e[q], ad_sem, partner)
-
-    def ag_first(a):
-        @pl.when(a >= NSEND)
-        def _():
-            drain(DEV - 1, as_sem.at[a % NSEND])
-        ag_pass(a, 1)
-        local(wbuf.at[a], o_ref.at[a, me], loc_sem).start()
-        strips(a, (nm, ns, no, ni, n0), lambda dst, src: local(src, dst, vn_sem).start())
+            for o, (t, u) in enumerate(((t0, u0), (t1, u1), (t2, u2))):
+                @pl.when((a >= TAIL0) & (a % 3 == o))
+                def _():
+                    k = (a - TAIL0) // 3
+                    ag_pass(a, n, lambda p, q: t.at[k, q], lambda p, q: u.at[k, q], n == 4)
 
     def ag_end(a):
-        drain(8, ad_sem.at[a])
+        pl.when(a < TAIL0)(lambda: drain(8, ad_sem.at[a]))
+        pl.when(a >= TAIL0)(lambda: drain(4, ad_sem.at[a]))
 
     def stage(s, lag, fn, count=NCH):
         c = s - lag
@@ -341,11 +368,11 @@
     def fc_moments():
         for b in range(CLASSES // U):
             local(vbuf.at[FC0 + b // 4, :, pl.ds(b % 4 * LANES, LANES)], nf.at[pl.ds(b * U, U)], vn_sem).start()
-        local(vbuf.at[NCH - 1, pl.ds(0, SUB), pl.ds(CW - LANES, LANES)], nf.at[pl.ds(LASTROW, SUB)], vn_sem).start()
+        local(vbuf.at[FCL, pl.ds(0, SUB), pl.ds(CW - LANES, LANES)], nf.at[pl.ds(LASTROW, SUB)], vn_sem).start()
 
     def step(s):
         for at, fn in ((LOAD0, start_small), (MM0, first_products), (SMALL, small_tensors), (SMALL + 1, small_back),
-                       (AG0 + NCH + FIRST + 1, fc_moments)):
+                       (AG0 + FCL + 2, fc_moments)):
             pl.when(s == at)(fn)
         for n, at in enumerate((SPLIT, NCH)):
             pl.when(s == at + LAGS[3])(functools.partial(norms_out, n))
@@ -356,8 +383,8 @@
         stage(s, 0, rs_start)
         stage(s, AG0 + AGEND, ag_end)
         for n, lag in AGLAGS[::-1]:
-            stage(s, AG0 + lag, functools.partial(ag_pass, n=n))
-        stage(s, AG0 + FIRST, ag_first)
+            stage(s, AG0 + lag, functools.partial(gather, n=n))
+        stage(s, AG0 + FIRST, functools.partial(gather, n=1))
         stage(s, AG0, update)
         stage(s, MM0, fc_block, DEV // 2)
         stage(s, LOAD0, load_two, NCH // 2)
@@ -370,13 +397,14 @@
     loop(0, AG0 + NCH + AGEND, step)
 
     loop(NCH - NSLOT, NCH, lambda c: sent(c % NSLOT))
-    loop(NCH - NSEND, NCH, lambda a: drain(DEV - 1, as_sem.at[a % NSEND]))
+    loop(NCH - NSEND, TAIL0, lambda a: drain(DEV - 1, as_sem.at[a % NSEND]))
+    loop(TAIL0, NCH, lambda a: drain(7, as_sem.at[a % NSEND]))
     landed(snew, misc_sem)
     landed(svnew, x_sem)
     landed(so_ref.at[others], so_recv)
     landed(so_ref.at[others], so_send)
     landed(wbuf, loc_sem)
-    landed(vbuf.at[pl.ds(0, FC0)], vn_sem)
+    landed(vbuf.at[pl.ds(0, NCH - FCN)], vn_sem)
     landed(nf, vn_sem)
 
 
@@ -393,12 +421,12 @@
     return pl.pallas_call(
         comm_kernel,
         out_shape=[jax.ShapeDtypeStruct(s, F32) for s in (
-            [(NCH, DEV) + unit] + [v.shape for v in moments] + [(DEV,) + tile, (3 * SUB, LANES)])],
+            [(TAIL0, DEV) + unit] + [(TAILK, 4) + unit] * 6 + [v.shape for v in moments] + [(DEV,) + tile, (3 * SUB, LANES)])],
         in_specs=[pl.BlockSpec(memory_space=pltpu.SMEM)] + [anyspec] * 20 + [vspec] * 4,
-        out_specs=[anyspec] * 9,
+        out_specs=[anyspec] * 15,
         scratch_shapes=[vmem(NSLOT, n, *unit) for n in (8, 8, 4, 2, 1)] + [vmem(NCH, *unit)] * 3
         + [vmem(*pooled.shape, dtype=BF16), vmem(*dlogits.shape, dtype=BF16),
-           vmem(NCH - FC0, DEV, *unit),
+           vmem(FCN, DEV, *unit),
            vmem(2 * SUB, LANES), vmem(2, DEV, 2 * SUB, LANES), vmem(*tile),
            vmem(DEV, 3 * SUB, LANES), vmem(2 * SUB, LANES), vmem(*tile), vmem(3 * SUB, LANES)]
         + [dma((NSLOT,))] * 9 + [dma] * 10 + [dma((2,))] * 2 + [dma((NCH,))] * 4 + [dma((NSEND,))]
@@ -412,10 +440,11 @@
 NBUF = 12
 AHEAD = 6
 NFC = 4
-
-
-def write_kernel(o_ref, nm, ns, no, ni, n0, nf, so_ref, sv_ref, om, os_, oo, oi, o0, of, bm, bs, bo, bi, b0, bf,
-                 vm, vs, vo, vi, v0, vf, bn, vbn, vb, wb,
+WRITE_FLOPS = 10 ** 8
+
+
+def write_kernel(o_ref, ns, no, ni, n0, nm, so_ref, sv_ref, os_, oo, oi, o0, om, of, bs, bo, bi, b0, bm, bf,
+                 vs, vo, vi, v0, vm, bn, vbn,
                  buf, bbuf, fbuf, fbbuf, vbuf, in_sem, f_sem, b_sem, v_sem):
     def view(c, refs):
         entry, ref = [(e, r) for e, r in zip(TABLE, refs) if c >= e[0]][-1]
@@ -427,8 +456,8 @@
 
     def stores(i):
         slot = i % NBUF
-        if i < FC0:
-            pairs = [(buf.at[slot], view(i, (om, os_, oo, oi, o0))), (bbuf.at[slot], view(i, (bm, bs, bo, bi, b0)))]
+        if not FC0 <= i <= FCL:
+            pairs = [(buf.at[slot], view(i, (os_, oo, oi, o0, om))), (bbuf.at[slot], view(i, (bs, bo, bi, b0, bm)))]
         else:
             size = min(LANES, CLASSES - LANES * (i - FC0))
             have, want = pl.ds(0, size), pl.ds(LANES * (i - FC0), size)
@@ -446,7 +475,8 @@
     for i in range(AHEAD):
         for d in load(i):
             d.start()
-    firsts = [e[0] * LANES for e in TABLE] + [FC0 * LANES]
+    sizes = [e[1] * e[2] * LANES for e in TABLE]
+    firsts = [sum(sizes[:n]) for n in range(len(sizes))]
 
     def moments(refs, back):
         out = []
@@ -454,18 +484,16 @@
             pair = (ref, vbuf.at[pl.ds(first, ref.shape[0])])
             out.append(pltpu.make_async_copy(*(pair[::-1] if back else pair), v_sem))
         return out
-    v_ins, v_outs = moments((nm, ns, no, ni, n0, nf), False), moments((vm, vs, vo, vi, v0, vf), True)
+    v_ins, v_outs = moments((ns, no, ni, n0, nm), False), moments((vs, vo, vi, v0, vm), True)
     for d in v_ins:
         d.start()
     bn[...] = so_ref[...]
     vbn[...] = sv_ref[0:SUB]
-    vb[...] = sv_ref[SUB:2 * SUB]
-    wb[...] = sv_ref[2 * SUB:]
-    for i in range(NCH):
+    for i in range(TAIL0):
         slot = i % NBUF
         for d in load(i):
             d.wait()
-        if i < FC0:
+        if not FC0 <= i <= FCL:
             def cast(p, _):
                 bbuf[slot, p] = buf[slot, p].astype(BF16)
                 return 0
@@ -485,11 +513,11 @@
                 d.wait()
             for d in v_outs:
                 d.start()
-        if i + AHEAD < NCH:
+        if i + AHEAD < TAIL0:
             settle(i + AHEAD - NBUF)
             for d in load(i + AHEAD):
                 d.start()
-    settle(NCH - 1)
+    settle(TAIL0 - 1)
     for d in v_outs:
         d.wait()
 
@@ -498,24 +526,98 @@
     anyspec = pl.BlockSpec(memory_space=pl.ANY)
     vspec = pl.BlockSpec(memory_space=pltpu.VMEM)
     shapes = [dshape(*e, DEV) for e in TABLE] + [(CLASSES, DEV * LANES)]
-    moments = [(e[1] * e[2] * LANES, LANES) for e in TABLE] + [(CLASSES, LANES)]
+    moments = [(e[1] * e[2] * LANES, LANES) for e in TABLE]
     tile = (SUB, LANES)
     dma = pltpu.SemaphoreType.DMA
     outs = [(s, F32) for s in shapes] + [(s, BF16) for s in shapes] + [(s, F32) for s in moments]
-    outs += [((DEV,) + tile, F32)] + [(tile, F32)] * 3
+    outs += [((DEV,) + tile, F32), (tile, F32)]
     return pl.pallas_call(
         write_kernel,
         out_shape=[jax.ShapeDtypeStruct(*s) for s in outs],
-        in_specs=[anyspec] * 7 + [vspec] * 2,
-        out_specs=[anyspec] * 18 + [vspec] * 4,
+        in_specs=[anyspec] * 6 + [vspec] * 2,
+        out_specs=[anyspec] * 17 + [vspec] * 2,
         scratch_shapes=[
             pltpu.VMEM((NBUF, DEV, U, CW), F32), pltpu.VMEM((NBUF, DEV, U, CW), BF16),
             pltpu.VMEM((NFC, LANES, DEV * LANES), F32), pltpu.VMEM((NFC, LANES, DEV * LANES), BF16),
-            pltpu.VMEM((FC0 * LANES + CLASSES, LANES), F32),
+            pltpu.VMEM(((NCH - FCN) * LANES, LANES), F32),
             dma((NBUF,)), dma((NBUF,)), dma((NBUF,)), dma],
         compiler_params=pltpu.CompilerParams(vmem_limit_bytes=62 * 1024 * 1024),
+        cost_estimate=pl.CostEstimate(flops=WRITE_FLOPS, bytes_accessed=TAIL0 * 160 * U * CW, transcendentals=0),
         name='write_out',
     )(o, *moments_new, so, sv)
+
+
+TBUF = 6
+
+
+def tail_kernel(groups, *refs):
+    count = 3 * len(groups)
+    srcs, (_, _, om, bm, buf, bbuf, in_sem, f_sem, b_sem) = refs[:count], refs[count:]
+    me = lax.axis_index('dp')
+    mate = 1 - 2 * (me % 2)
+    entry = TABLE[-1]
+    size = 4 * len(groups)
+
+    def load(n):
+        k, o = n // 3, n % 3
+        return [pltpu.make_async_copy(srcs[3 * j + o].at[k], buf.at[n % TBUF, pl.ds(4 * j, 4)], in_sem.at[n % TBUF])
+                for j in range(len(groups))]
+
+    def store(n):
+        slot = n % TBUF
+        e = devices(me, strides(me // 2, n % 3))
+        i, row, _ = unit_at(entry, TAIL0 + n)
+        for j, (base, other) in enumerate(groups):
+            for q in range(4):
+                p = e[base + q] + mate * other
+                pltpu.make_async_copy(buf.at[slot, 4 * j + q], om.at[i, p, pl.ds(row, U)], f_sem.at[slot]).start()
+                pltpu.make_async_copy(bbuf.at[slot, 4 * j + q], bm.at[i, p, pl.ds(row, U)], b_sem.at[slot]).start()
+
+    def settled(n):
+        for ref, sem in ((buf, f_sem), (bbuf, b_sem)):
+            pltpu.make_async_copy(ref.at[n % TBUF], ref.at[n % TBUF], sem.at[n % TBUF]).wait()
+
+    total, ahead = NCH - TAIL0, TBUF // 2
+    for n in range(ahead):
+        for d in load(n):
+            d.start()
+    for n in range(total):
+        slot = n % TBUF
+        for d in load(n):
+            d.wait()
+
+        def cast(p, _):
+            bbuf[slot, p] = buf[slot, p].astype(BF16)
+            return 0
+        lax.fori_loop(0, size, cast, 0)
+        store(n)
+        nxt = n + ahead
+        if nxt < total:
+            if nxt >= TBUF:
+                settled(nxt - TBUF)
+            for d in load(nxt):
+                d.start()
+    for n in range(max(0, total - TBUF), total):
+        settled(n)
+
+
+def run_tail(groups, srcs, full, half, name):
+    anyspec = pl.BlockSpec(memory_space=pl.ANY)
+    dma = pltpu.SemaphoreType.DMA
+    size = 4 * len(groups)
+    count = len(srcs)
+    return pl.pallas_call(
+        functools.partial(tail_kernel, groups),
+        out_shape=[jax.ShapeDtypeStruct(x.shape, x.dtype) for x in (full, half)],
+        in_specs=[anyspec] * (count + 2),
+        out_specs=[anyspec] * 2,
+        input_output_aliases={count: 0, count + 1: 1},
+        scratch_shapes=[pltpu.VMEM((TBUF, size, U, CW), F32), pltpu.VMEM((TBUF, size, U, CW), BF16),
+                        dma((TBUF,)), dma((TBUF,)), dma((TBUF,))],
+        compiler_params=pltpu.CompilerParams(vmem_limit_bytes=62 * 1024 * 1024),
+        cost_estimate=pl.CostEstimate(flops=WRITE_FLOPS // 3, bytes_accessed=15 * size * 10 * U * CW, transcendentals=0),
+        name=name,
+    )(*srcs, full, half)
 
 
 def solution(mesh):
@@ -532,8 +634,8 @@
         rank = lax.axis_index('dp')
         width = v_bias.shape[0]
         shapes = [dshape(*e, DEV) for e in TABLE]
-        grads = [g.reshape(s) for g, s in zip((g_mid, g_short, g_out, g_in, g_in0), shapes)]
-        weights = [w.reshape(s) for w, s in zip((w_mid, w_short, w_out, w_in, w_in0), shapes)] + [w_fc.T]
+        grads = [g.reshape(s) for g, s in zip((g_short, g_out, g_in, g_in0, g_mid), shapes)]
+        weights = [w.reshape(s) for w, s in zip((w_short, w_out, w_in, w_in0, w_mid), shapes)] + [w_fc.T]
 
         def to_rows(v, entry):
             _, stack, _, blocks = entry
@@ -541,7 +643,7 @@
 
         def from_rows(v, stack, like):
             return v.reshape(-1, stack, LANES).transpose(1, 0, 2).reshape(like.shape)
-        olds = (v_mid, v_short, v_out, v_in, v_in0)
+        olds = (v_short, v_out, v_in, v_in0, v_mid)
         moments = [to_rows(v, e) for v, e in zip(olds, TABLE)]
         moments.append(v_fc.reshape(LANES, CLASSES).T)
         tiles = (-1, SUB, LANES)
@@ -549,16 +651,27 @@
         placed = lax.dynamic_update_slice(jnp.zeros((pad,), F32), v_bias, (rank * width,))
         small = [g_bn.reshape(tiles), w_bn.reshape(-1, LANES), v_bn.reshape(SUB, LANES),
                  w_bias.reshape(1, CLASSES), placed.reshape(SUB, LANES)]
-        o, *made, so, sv = run_comm(learn_rate.reshape(1, 1), grads, pooled, dlogits.T, weights, moments, small)
-        mid, short, out, inn, in0, fc, mid_b, short_b, out_b, inn_b, in0_b, fc_b, *rest = run_write(o, [v.reshape(-1, LANES) for v in made], so, sv)
-        vm, vs, vo, vi, v0, vf, bn, vbn, vb, wb = rest
-        news = [from_rows(v, e[1], old) for v, e, old in zip((vm, vs, vo, vi, v0), TABLE, olds)]
+        o, t0, t1, t2, u0, u1, u2, *made, nf, so, sv = run_comm(
+            learn_rate.reshape(1, 1), grads, pooled, dlogits.T, weights, moments, small)
+        ts, us = (t0, t1, t2), (u0, u1, u2)
+
+        def across(x, weight):
+            return lax.ppermute(x, 'dp', [(i, i ^ weight) for i in range(DEV)])
+        rs = [across(t, 2 << (n + 2) % 3) for n, t in enumerate(ts)]
+        outs = run_write(o, [v.reshape(-1, LANES) for v in made], so, sv)
+        short, out, inn, in0, mid, fc, short_b, out_b, inn_b, in0_b, mid_b, fc_b, vs, vo, vi, v0, vm, bn, vbn = outs
+        *held, vbn = lax.optimization_barrier((*rs, vbn))
+        mates = [across(r, 1) for r in held]
+        mid, mid_b = run_tail(((0, False), (0, True), (4, False)), [*ts, *us, *rs], mid, mid_b, 'write_tail')
+        mid, mid_b = run_tail(((4, True),), mates, mid, mid_b, 'write_last')
+        news = [from_rows(v, e[1], old) for v, e, old in zip((vs, vo, vi, v0, vm), TABLE, olds)]
+        vb, wb = sv[SUB:2 * SUB], sv[2 * SUB:]
         return (in0.reshape(w_in0.shape), short.reshape(w_short.shape), inn.reshape(w_in.shape),
                 mid.reshape(w_mid.shape), out.reshape(w_out.shape), fc.T,
                 bn.reshape(w_bn.shape), wb.reshape(-1)[:CLASSES],
                 in0_b.reshape(w_in0.shape), short_b.reshape(w_short.shape), inn_b.reshape(w_in.shape),
                 mid_b.reshape(w_mid.shape), out_b.reshape(w_out.shape), fc_b.T,
-                news[4], news[1], news[3], news[0], news[2], vf.T.reshape(v_fc.shape),
+                news[3], news[0], news[2], news[4], news[1], nf.T.reshape(v_fc.shape),
                 vbn.reshape(v_bn.shape), lax.dynamic_slice_in_dim(vb.reshape(-1), rank * width, width))
 
     return jax.shard_map(body, mesh=mesh, in_specs=in_specs, out_specs=out_specs, check_vma=False)

time: 390 us -> 373 us (0.956)
  Pallas kernels: 381 us -> 361 us
    pallas_call x1, Pallas kernels: 337 us -> 311 us  [run_comm(): pl.pallas_call(comm_kernel, out_shape=[jax.ShapeDtypeStruct(s, F32) for s...]
    pallas_call x0 -> x2, Pallas kernels: none -> 18.3 us  [run_tail(): pl.pallas_call(functools.partial(tail_kernel, groups), out_shape=[jax.Sha...]
    pallas_call x1, Pallas kernels: 44.5 us -> 31.7 us  [run_write(): pl.pallas_call(write_kernel, out_shape=[jax.ShapeDtypeStruct(*s) for s in...]
  transfers between devices with their start and end apart: 0 -> 6, of which waited for: 0 -> 0; matrix products, arithmetic and copies ran while one was open for 0% -> 1% of each run, Pallas kernels for 0% -> 12%
where the time goes in v4:
time: 373 us; the launch traced here: 372 us
  Pallas kernels  361 us (97%)
  local copies, waits for them, and re-layouts  6.55 us (2%)
    pallas_call x1, Pallas kernels, run_comm(): pl.pallas_call(comm_kernel, out_shape=[jax.ShapeDtypeStruct(s, F32) for s...  311 us
    pallas_call x1, Pallas kernels, run_write(): pl.pallas_call(write_kernel, out_shape=[jax.ShapeDtypeStruct(*s) for s in...  31.7 us
    pallas_call x2, Pallas kernels, run_tail(): pl.pallas_call(functools.partial(tail_kernel, groups), out_shape=[jax.Sha...  18.3 us
  transfers between devices with their start and end apart: 6, of which 0 were waited for; matrix products, arithmetic and copies ran while one was open for 1% of the time, Pallas kernels for 12%

profile of v4, /device:TPU:1, one launch (start us, length us, event | category | flops | bytes accessed | tf_op | source)
XLA Modules:
  0.0 372.1 jit_solution(4752057681617408720)
XLA Ops:
  0.7 1.4 reshape.194
  2.1 1.0 copy.57
  3.8 0.9 dynamic_update_slice.3
  4.6 0.0 copy-start.3
  4.6 0.6 copy-done.3
  5.2 311.2 %lars_comm.1 = (f32[33,16,32,512]{3,2,1,0:T(8,128)}, f32[5,4,32,512]{3,2,1,0:T(8,128)}, f32[5,4,32,512]{3,2,1,0:T(8,128)}, f32[5,4,32,512]{3,2,1,0:T(8,128)}, f3...) custom-call(f32[1,1]{1,0:T(1,128)} %bitcast.70.lr_ref, ...), custom_call_target="tpu_custom_call" | custom-call | tf_op jit(solution)/shard_map/lars_comm/pallas_call | solution.py:421
  316.5 0.2 collective-permute-start
  316.7 0.4 collective-permute-start.1
  317.1 1.1 collective-permute-start.2
  318.2 0.0 copy-start.2
  318.2 0.0 copy-start.1
  318.2 31.7 %write_out.1 = (f32[1,16,64,2048]{3,2,1,0:T(8,128)}, f32[2,16,32,2048]{3,2,1,0:T(8,128)}, f32[1,16,128,512]{3,2,1,0:T(8,128)}, f32[1,16,64,512]{3,2,1,0:T(8,128)...) custom-call(f32[33,16,32,512]{3,2,1,0:T(8,128)} %get-tuple-element.6, ...), custom_call_target="tpu_custom_call" | custom-call | flops 100000000 | bytes 86507520 | tf_op jit(solution)/shard_map/write_out/pallas_call | solution.py:534
  349.9 0.0 collective-permute-done.refs_6_
  349.9 0.0 copy-start
  349.9 0.0 collective-permute-done.1.refs_7_
  349.9 0.0 collective-permute-done.2.refs_8_
  350.0 0.6 collective-permute-start.3
  350.5 0.1 collective-permute-start.4
  350.6 0.5 collective-permute-start.5
  351.0 0.0 copy-done.2
  351.0 0.6 slice_bitcast_fusion
  351.6 0.6 dynamic_slice.3
  352.2 0.0 copy-done.1
  352.2 0.2 copy.60
  352.4 1.3 reshape.221
  353.7 0.0 copy-done
  353.7 11.2 %write_tail.1 = (f32[2,16,288,512]{3,2,1,0:T(8,128)}, bf16[2,16,288,512]{3,2,1,0:T(8,128)(2,1)}) custom-call(f32[5,4,32,512]{3,2,1,0:T(8,128)} %get-tuple-element.75.refs_0_, f32[5,4,32,512]{3,2,1,0:T(8,128)} %get-tuple-element.76.refs_1_, f32[5,4,32,512]{3,2,1,0:T(8,128)} %get-tuple-element.77.refs_2_, ...), custom_call_target="tpu_custom_call", output_to_operand_aliasing={{0}: (9, {}), {1}: (10, {})} | custom-call | flops 33333332 | bytes 29491200 | tf_op jit(solution)/shard_map/write_tail/pallas_call | solution.py:609
  364.9 0.0 collective-permute-done.3.refs_0_
  364.9 0.0 collective-permute-done.4.refs_1_
  364.9 0.0 collective-permute-done.5.refs_2_
  364.9 7.1 %write_last.1 = (f32[2,16,288,512]{3,2,1,0:T(8,128)}, bf16[2,16,288,512]{3,2,1,0:T(8,128)(2,1)}) custom-call(f32[5,4,32,512]{3,2,1,0:T(8,128)} %collective-permute-done.3.refs_0_, f32[5,4,32,512]{3,2,1,0:T(8,128)} %collective-permute-done.4.refs_1_, f32[5,4,32,512]{3,2,1,0:T(8,128)} %collective-permute-done.5.refs_2_, ...), custom_call_target="tpu_custom_call", output_to_operand_aliasing={{0}: (3, {}), {1}: (4, {})} | custom-call | flops 33333332 | bytes 9830400 | tf_op jit(solution)/shard_map/write_last/pallas_call | solution.py:609
  (1 shorter events, 0.0 us)
Async XLA Ops:
  4.6 0.6 copy-start.3
  316.5 33.4 %collective-permute-start = (f32[5,4,32,512]{3,2,1,0:T(8,128)}, f32[5,4,32,512]{3,2,1,0:T(8,128)S(1)}, u32[]{:S(2)}, u32[]{:S(2)}) collective-permute-start(f32[5,4,32,512]{3,2,1,0:T(8,128)} %get-tuple-element.75.refs_0_), channel_id=1, source_target_pairs={{0,8},{1,9},{2,10},{3,11},{4,12},{5,13},{6,14},{7,15},{8,0},{9,1},... | collective-permute-start | bytes 3932168 | tf_op jit(solution)/shard_map/ppermute | solution.py:659
  316.7 33.2 %collective-permute-start.1 = (f32[5,4,32,512]{3,2,1,0:T(8,128)}, f32[5,4,32,512]{3,2,1,0:T(8,128)}, u32[]{:S(2)}, u32[]{:S(2)}) collective-permute-start(f32[5,4,32,512]{3,2,1,0:T(8,128)} %get-tuple-element.76.refs_1_), channel_id=1, source_target_pairs={{0,2},{1,3},{2,0},{3,1},{4,6},{5,7},{6,4},{7,5},{8,10},{9,11},{10,... | collective-permute-start | bytes 3932168 | tf_op jit(solution)/shard_map/ppermute | solution.py:659
  317.1 32.9 %collective-permute-start.2 = (f32[5,4,32,512]{3,2,1,0:T(8,128)}, f32[5,4,32,512]{3,2,1,0:T(8,128)}, u32[]{:S(2)}, u32[]{:S(2)}) collective-permute-start(f32[5,4,32,512]{3,2,1,0:T(8,128)} %get-tuple-element.77.refs_2_), channel_id=1, source_target_pairs={{0,4},{1,5},{2,6},{3,7},{4,0},{5,1},{6,2},{7,3},{8,12},{9,13},{10,... | collective-permute-start | bytes 3932168 | tf_op jit(solution)/shard_map/ppermute | solution.py:659
  318.2 32.9 %copy-start.2 = (f32[24,128]{1,0:T(8,128)S(1)}, f32[24,128]{1,0:T(8,128)}, u32[]{:S(2)}) copy-start(f32[24,128]{1,0:T(8,128)} %get-tuple-element.71.sv_ref) | copy-start | bytes 36868
  318.2 34.0 %copy-start.1 = (f32[1000,128]{1,0:T(8,128)S(1)}, f32[1000,128]{1,0:T(8,128)}, u32[]{:S(2)}) copy-start(f32[1000,128]{1,0:T(8,128)} %get-tuple-element.104) | copy-start | bytes 1536004
  349.9 3.8 %copy-start = (f32[5,4,32,512]{3,2,1,0:T(8,128)}, f32[5,4,32,512]{3,2,1,0:T(8,128)S(1)}, u32[]{:S(2)}) copy-start(f32[5,4,32,512]{3,2,1,0:T(8,128)S(1)} %collective-permute-done.refs_6_) | copy-start | bytes 3932164
  350.0 15.0 %collective-permute-start.3 = (f32[5,4,32,512]{3,2,1,0:T(8,128)S(1)}, f32[5,4,32,512]{3,2,1,0:T(8,128)}, u32[]{:S(2)}, u32[]{:S(2)}) collective-permute-start(f32[5,4,32,512]{3,2,1,0:T(8,128)S(1)} %collective-permute-done.refs_6_), channel_id=1, source_target_pairs={{0,1},{1,0},{2,3},{3,2},{4,5},{5,4},{6,7},{7,6},{8,9},{9,8},{10,11... | collective-permute-start | bytes 3932168 | tf_op jit(solution)/shard_map/ppermute | solution.py:659
  350.5 14.4 %collective-permute-start.4 = (f32[5,4,32,512]{3,2,1,0:T(8,128)}, f32[5,4,32,512]{3,2,1,0:T(8,128)}, u32[]{:S(2)}, u32[]{:S(2)}) collective-permute-start(f32[5,4,32,512]{3,2,1,0:T(8,128)} %collective-permute-done.1.refs_7_), channel_id=1, source_target_pairs={{0,1},{1,0},{2,3},{3,2},{4,5},{5,4},{6,7},{7,6},{8,9},{9,8},{10,11... | collective-permute-start | bytes 3932168 | tf_op jit(solution)/shard_map/ppermute | solution.py:659
  350.6 14.4 %collective-permute-start.5 = (f32[5,4,32,512]{3,2,1,0:T(8,128)}, f32[5,4,32,512]{3,2,1,0:T(8,128)}, u32[]{:S(2)}, u32[]{:S(2)}) collective-permute-start(f32[5,4,32,512]{3,2,1,0:T(8,128)} %collective-permute-done.2.refs_8_), channel_id=1, source_target_pairs={{0,1},{1,0},{2,3},{3,2},{4,5},{5,4},{6,7},{7,6},{8,9},{9,8},{10,11... | collective-permute-start | bytes 3932168 | tf_op jit(solution)/shard_map/ppermute | solution.py:659

commit v5 on v4

--- a/solution.py
+++ b/solution.py
@@ -10,30 +10,32 @@
 TRUST_COEF = 0.001
 DECAY = 0.0001
 
+
 MESH = pl.DeviceIdType.MESH
 F32, BF16 = jnp.float32, jnp.bfloat16
 DEV = 16
 LANES = 128
 U, CW = 32, 512
 NCH = 48
-FC0, FCN = 22, 8
+FC0, FCN = 16, 8
 FCL = FC0 + FCN - 1
 CLASSES, LASTROW = 1000, 992
 SUB = 8
-TABLE = ((0, 1, 8, 4), (8, 2, 4, 4), (16, 1, 4, 1), (20, 1, 2, 1), (30, 2, 9, 1))
-STARTS = (8, 12, 16, 20, FC0, 30, 39)
-TAIL0 = 33
-TAILK = (NCH - TAIL0) // 3
-SPLIT = 22
+TABLE = ((0, 1, 8, 4), (8, 2, 4, 4), (24, 1, 4, 1), (28, 1, 2, 1), (30, 2, 9, 1))
+STARTS = (8, 12, FC0, 24, 28, 30, 39)
+TAIL0 = 24
+GROUP = 12
+TAILK = GROUP // 3
+SPLIT = 24
 NSLOT = 15
-LAGS = (2, 6, 10, 13)
-AG0 = 44
+LAGS = (3, 6, 9, 12)
+AG0 = 45
 FIRST = 1
-AGLAGS = ((2, 5), (4, 10), (8, 16))
-AGEND = 20
+AGLAGS = ((2, 6), (4, 12), (8, 18))
+AGEND = 21
 NSEND = 18
 LOAD0 = 6
-MM0 = 10
+MM0 = 6
 SMALL = 34
 
 
@@ -85,7 +87,7 @@
 
 def comm_kernel(lr_ref, gs, go, gi, g0, gm, x_ref, d_ref, ws, wo, wi, w0, wm, wf, vs, vo, vi, v0, vm, vf,
                 g_bn, w_bn, v_bn, w_bias, v_bias,
-                o_ref, t0, t1, t2, u0, u1, u2, ns, no, ni, n0, nm, nf, so_ref, sv_ref,
+                o_ref, t0, t1, t2, t3, t4, t5, u0, u1, u2, u3, u4, u5, ns, no, ni, n0, nm, nf, so_ref, sv_ref,
                 acc, rd, r1, r2, r3, grad, wbuf, vbuf, xbuf, dbuf, fcg,
                 sums, nb, tr, sb, bias, snew, svnew,
                 load_sem, ds_sem, dr_sem, s1_sem, p1_sem, s2_sem, p2_sem, s3_sem, p3_sem,
@@ -125,6 +127,7 @@
         def body(i, carry):
             fn(i)
             return carry
+
         lax.fori_loop(lo, hi, body, 0)
 
     def each_other(fn):
@@ -141,6 +144,7 @@
                 part = (c, pl.ds(0, size), pl.ds(i * LANES, LANES))
                 local(wf.at[rows, lane], wbuf.at[part], w_sem).start()
                 local(vf.at[rows], vbuf.at[part], v_sem).start()
+
         pl.when((c >= FC0) & (c < FCL))(functools.partial(classifier, (U, U, U, U)))
         pl.when(c == FCL)(functools.partial(classifier, (U, U, U, SUB)))
 
@@ -214,6 +218,7 @@
         def _():
             sent(slot)
             pl.semaphore_wait(cd_sem, 1)
+
         x1, x2, x3 = order(c)
         pieces = [(q, 2 * (chip + (q // 4) * x1 + ((q // 2) % 2) * x2 + (q % 2) * x3))
                   for q in (4, 5, 6, 7, 0, 1, 2, 3)]
@@ -225,6 +230,7 @@
             for q, p in pieces:
                 to_partner(view(p + 1 - core), q)
                 local(view(p + core), acc.at[slot, q], load_sem.at[slot]).start()
+
         chunk_views(c, (gs, go, gi, g0, gm), go_all)
 
         @pl.when(is_fc(c))
@@ -248,6 +254,7 @@
         @pl.when(c >= NSLOT)
         def _():
             pl.semaphore_wait(credits[level + 1].at[c % 3], 1)
+
         remote(acc.at[slot, pl.ds(half, half)], going.at[slot], send_sems[level + 1].at[slot],
                recv_sems[level + 1].at[slot], dev).start()
         acc[slot, 0:half] = acc[slot, 0:half] + came[slot, 0:half]
@@ -322,17 +329,22 @@
         if n == 1:
             @pl.when(a >= NSEND)
             def _():
-                drain(DEV - 1, as_sem.at[a % NSEND])
+                pl.when(a - NSEND < TAIL0)(lambda: drain(DEV - 1, as_sem.at[a % NSEND]))
+                pl.when(a - NSEND >= TAIL0)(lambda: drain(7, as_sem.at[a % NSEND]))
+
             strips(a, (ns, no, ni, n0, nm), lambda dst, src: local(src, dst, vn_sem).start())
 
         @pl.when(a < TAIL0)
         def _():
             ag_pass(a, n, lambda p, q: o_ref.at[a, p], lambda p, q: o_ref.at[a, p], n == 8)
+
         if n < 8:
-            for o, (t, u) in enumerate(((t0, u0), (t1, u1), (t2, u2))):
-                @pl.when((a >= TAIL0) & (a % 3 == o))
+            for j, (t, u) in enumerate(((t0, u0), (t1, u1), (t2, u2), (t3, u3), (t4, u4), (t5, u5))):
+                first = TAIL0 + j // 3 * GROUP
+
+                @pl.when((a >= first) & (a < first + GROUP) & (a % 3 == j % 3))
                 def _():
-                    k = (a - TAIL0) // 3
+                    k = (a - first) // 3
                     ag_pass(a, n, lambda p, q: t.at[k, q], lambda p, q: u.at[k, q], n == 4)
 
     def ag_end(a):
@@ -397,8 +409,7 @@
     loop(0, AG0 + NCH + AGEND, step)
 
     loop(NCH - NSLOT, NCH, lambda c: sent(c % NSLOT))
-    loop(NCH - NSEND, TAIL0, lambda a: drain(DEV - 1, as_sem.at[a % NSEND]))
-    loop(TAIL0, NCH, lambda a: drain(7, as_sem.at[a % NSEND]))
+    loop(NCH - NSEND, NCH, lambda a: drain(7, as_sem.at[a % NSEND]))
     landed(snew, misc_sem)
     landed(svnew, x_sem)
     landed(so_ref.at[others], so_recv)
@@ -418,12 +429,13 @@
 
     def vmem(*shape, dtype=F32):
         return pltpu.VMEM(shape, dtype)
+
     return pl.pallas_call(
         comm_kernel,
         out_shape=[jax.ShapeDtypeStruct(s, F32) for s in (
-            [(TAIL0, DEV) + unit] + [(TAILK, 4) + unit] * 6 + [v.shape for v in moments] + [(DEV,) + tile, (3 * SUB, LANES)])],
+            [(TAIL0, DEV) + unit] + [(TAILK, 4) + unit] * 12 + [v.shape for v in moments] + [(DEV,) + tile, (3 * SUB, LANES)])],
         in_specs=[pl.BlockSpec(memory_space=pltpu.SMEM)] + [anyspec] * 20 + [vspec] * 4,
-        out_specs=[anyspec] * 15,
+        out_specs=[anyspec] * 21,
         scratch_shapes=[vmem(NSLOT, n, *unit) for n in (8, 8, 4, 2, 1)] + [vmem(NCH, *unit)] * 3
         + [vmem(*pooled.shape, dtype=BF16), vmem(*dlogits.shape, dtype=BF16),
            vmem(FCN, DEV, *unit),
@@ -443,7 +455,7 @@
 WRITE_FLOPS = 10 ** 8
 
 
-def write_kernel(o_ref, ns, no, ni, n0, nm, so_ref, sv_ref, os_, oo, oi, o0, om, of, bs, bo, bi, b0, bm, bf,
+def write_kernel(o_ref, ns, no, ni, n0, nm, so_ref, sv_ref, os_, oo, of, bs, bo, bf,
                  vs, vo, vi, v0, vm, bn, vbn,
                  buf, bbuf, fbuf, fbbuf, vbuf, in_sem, f_sem, b_sem, v_sem):
     def view(c, refs):
@@ -457,7 +469,7 @@
     def stores(i):
         slot = i % NBUF
         if not FC0 <= i <= FCL:
-            pairs = [(buf.at[slot], view(i, (os_, oo, oi, o0, om))), (bbuf.at[slot], view(i, (bs, bo, bi, b0, bm)))]
+            pairs = [(buf.at[slot], view(i, (os_, oo))), (bbuf.at[slot], view(i, (bs, bo)))]
         else:
             size = min(LANES, CLASSES - LANES * (i - FC0))
             have, want = pl.ds(0, size), pl.ds(LANES * (i - FC0), size)
@@ -484,6 +496,7 @@
             pair = (ref, vbuf.at[pl.ds(first, ref.shape[0])])
             out.append(pltpu.make_async_copy(*(pair[::-1] if back else pair), v_sem))
         return out
+
     v_ins, v_outs = moments((ns, no, ni, n0, nm), False), moments((vs, vo, vi, v0, vm), True)
     for d in v_ins:
         d.start()
@@ -497,6 +510,7 @@
             def cast(p, _):
                 bbuf[slot, p] = buf[slot, p].astype(BF16)
                 return 0
+
             lax.fori_loop(0, DEV, cast, 0)
         else:
             settle(i - NFC)
@@ -525,7 +539,7 @@
 def run_write(o, moments_new, so, sv):
     anyspec = pl.BlockSpec(memory_space=pl.ANY)
     vspec = pl.BlockSpec(memory_space=pltpu.VMEM)
-    shapes = [dshape(*e, DEV) for e in TABLE] + [(CLASSES, DEV * LANES)]
+    shapes = [dshape(*e, DEV) for e in TABLE[:2]] + [(CLASSES, DEV * LANES)]
     moments = [(e[1] * e[2] * LANES, LANES) for e in TABLE]
     tile = (SUB, LANES)
     dma = pltpu.SemaphoreType.DMA
@@ -535,7 +549,7 @@
         write_kernel,
         out_shape=[jax.ShapeDtypeStruct(*s) for s in outs],
         in_specs=[anyspec] * 6 + [vspec] * 2,
-        out_specs=[anyspec] * 17 + [vspec] * 2,
+        out_specs=[anyspec] * 11 + [vspec] * 2,
         scratch_shapes=[
             pltpu.VMEM((NBUF, DEV, U, CW), F32), pltpu.VMEM((NBUF, DEV, U, CW), BF16),
             pltpu.VMEM((NFC, LANES, DEV * LANES), F32), pltpu.VMEM((NFC, LANES, DEV * LANES), BF16),
@@ -547,77 +561,94 @@
     )(o, *moments_new, so, sv)
 
 
-TBUF = 6
-
-
-def tail_kernel(groups, *refs):
-    count = 3 * len(groups)
-    srcs, (_, _, om, bm, buf, bbuf, in_sem, f_sem, b_sem) = refs[:count], refs[count:]
+TBUF, TAHEAD = 16, 10
+
+
+def tail_kernel(jobs, size, count, aliased, *refs):
+    srcs, refs = refs[:count], refs[count + 7 * aliased:]
+    fulls, halves, (token, buf, bbuf, in_sem, f_sem, b_sem) = refs[:3], refs[3:6], refs[6:]
     me = lax.axis_index('dp')
     mate = 1 - 2 * (me % 2)
-    entry = TABLE[-1]
-    size = 4 * len(groups)
+    ring = buf.shape[0]
+    token[...] = jnp.zeros_like(token)
 
     def load(n):
-        k, o = n // 3, n % 3
-        return [pltpu.make_async_copy(srcs[3 * j + o].at[k], buf.at[n % TBUF, pl.ds(4 * j, 4)], in_sem.at[n % TBUF])
-                for j in range(len(groups))]
+        return [pltpu.make_async_copy(srcs[src].at[k], buf.at[n % ring, pl.ds(4 * j, 4)], in_sem.at[n % ring])
+                for j, (src, k, _, _) in enumerate(jobs[n][1])]
 
     def store(n):
-        slot = n % TBUF
-        e = devices(me, strides(me // 2, n % 3))
-        i, row, _ = unit_at(entry, TAIL0 + n)
-        for j, (base, other) in enumerate(groups):
+        slot = n % ring
+        c, parts = jobs[n]
+        e = devices(me, strides(me // 2, c % 3))
+        entry, full, half = [x for x in zip(TABLE[2:], fulls, halves) if c >= x[0][0]][-1]
+        i, row, _ = unit_at(entry, c)
+        for j, (_, _, base, other) in enumerate(parts):
             for q in range(4):
                 p = e[base + q] + mate * other
-                pltpu.make_async_copy(buf.at[slot, 4 * j + q], om.at[i, p, pl.ds(row, U)], f_sem.at[slot]).start()
-                pltpu.make_async_copy(bbuf.at[slot, 4 * j + q], bm.at[i, p, pl.ds(row, U)], b_sem.at[slot]).start()
+                at = (i, p, pl.ds(row, U))
+                pltpu.make_async_copy(buf.at[slot, 4 * j + q], full.at[at], f_sem.at[slot]).start()
+                pltpu.make_async_copy(bbuf.at[slot, 4 * j + q], half.at[at], b_sem.at[slot]).start()
 
     def settled(n):
         for ref, sem in ((buf, f_sem), (bbuf, b_sem)):
-            pltpu.make_async_copy(ref.at[n % TBUF], ref.at[n % TBUF], sem.at[n % TBUF]).wait()
-
-    total, ahead = NCH - TAIL0, TBUF // 2
+            pltpu.make_async_copy(ref.at[n % ring], ref.at[n % ring], sem.at[n % ring]).wait()
+
+    total = len(jobs)
+    ahead = ring if ring == total else TAHEAD
     for n in range(ahead):
         for d in load(n):
             d.start()
     for n in range(total):
-        slot = n % TBUF
+        slot = n % ring
         for d in load(n):
             d.wait()
 
         def cast(p, _):
             bbuf[slot, p] = buf[slot, p].astype(BF16)
             return 0
+
         lax.fori_loop(0, size, cast, 0)
         store(n)
         nxt = n + ahead
         if nxt < total:
-            if nxt >= TBUF:
-                settled(nxt - TBUF)
+            if nxt >= ring:
+                settled(nxt - ring)
             for d in load(nxt):
                 d.start()
-    for n in range(max(0, total - TBUF), total):
+    for n in range(max(0, total - ring), total):
         settled(n)
 
 
-def run_tail(groups, srcs, full, half, name):
+def run_tail(groups, sets, arrays):
     anyspec = pl.BlockSpec(memory_space=pl.ANY)
     dma = pltpu.SemaphoreType.DMA
-    size = 4 * len(groups)
+    size = 4 * len(sets)
+    srcs, jobs = [], []
+    for g in groups:
+        base = len(srcs)
+        for arrs, _, _ in sets:
+            srcs += arrs[3 * g:3 * g + 3]
+        for n in range(GROUP):
+            jobs.append((TAIL0 + g * GROUP + n, [(base + 3 * j + n % 3, n // 3, first, other)
+                                                 for j, (_, first, other) in enumerate(sets)]))
+    ring = min(len(jobs), TBUF)
     count = len(srcs)
+    given = list(arrays or [])[:6]
+    tokens = list(arrays or [])[6:]
+    shapes = [dshape(*e, DEV) for e in TABLE[2:]]
+    outs = [jax.ShapeDtypeStruct(s, t) for t in (F32, BF16) for s in shapes]
     return pl.pallas_call(
-        functools.partial(tail_kernel, groups),
-        out_shape=[jax.ShapeDtypeStruct(x.shape, x.dtype) for x in (full, half)],
-        in_specs=[anyspec] * (count + 2),
-        out_specs=[anyspec] * 2,
-        input_output_aliases={count: 0, count + 1: 1},
-        scratch_shapes=[pltpu.VMEM((TBUF, size, U, CW), F32), pltpu.VMEM((TBUF, size, U, CW), BF16),
-                        dma((TBUF,)), dma((TBUF,)), dma((TBUF,))],
+        functools.partial(tail_kernel, jobs, size, count, len(given) > 0),
+        out_shape=outs + [jax.ShapeDtypeStruct((SUB, LANES), F32)],
+        in_specs=[anyspec] * (count + len(given) + len(tokens)),
+        out_specs=[anyspec] * 6 + [pl.BlockSpec(memory_space=pltpu.VMEM)],
+        input_output_aliases={count + n: n for n in range(len(given))},
+        scratch_shapes=[pltpu.VMEM((ring, size, U, CW), F32), pltpu.VMEM((ring, size, U, CW), BF16),
+                        dma((ring,)), dma((ring,)), dma((ring,))],
         compiler_params=pltpu.CompilerParams(vmem_limit_bytes=62 * 1024 * 1024),
-        cost_estimate=pl.CostEstimate(flops=WRITE_FLOPS // 3, bytes_accessed=15 * size * 10 * U * CW, transcendentals=0),
-        name=name,
-    )(*srcs, full, half)
+        cost_estimate=pl.CostEstimate(flops=WRITE_FLOPS // 3, bytes_accessed=len(jobs) * size * 10 * U * CW,
+                                      transcendentals=0),
+    )(*srcs, *given, *tokens)
 
 
 def solution(mesh):
@@ -643,6 +674,7 @@
 
         def from_rows(v, stack, like):
             return v.reshape(-1, stack, LANES).transpose(1, 0, 2).reshape(like.shape)
+
         olds = (v_short, v_out, v_in, v_in0, v_mid)
         moments = [to_rows(v, e) for v, e in zip(olds, TABLE)]
         moments.append(v_fc.reshape(LANES, CLASSES).T)
@@ -651,19 +683,29 @@
         placed = lax.dynamic_update_slice(jnp.zeros((pad,), F32), v_bias, (rank * width,))
         small = [g_bn.reshape(tiles), w_bn.reshape(-1, LANES), v_bn.reshape(SUB, LANES),
                  w_bias.reshape(1, CLASSES), placed.reshape(SUB, LANES)]
-        o, t0, t1, t2, u0, u1, u2, *made, nf, so, sv = run_comm(
+        o, *made, nf, so, sv = run_comm(
             learn_rate.reshape(1, 1), grads, pooled, dlogits.T, weights, moments, small)
-        ts, us = (t0, t1, t2), (u0, u1, u2)
+        ts, us, made = made[:6], made[6:12], made[12:]
 
         def across(x, weight):
             return lax.ppermute(x, 'dp', [(i, i ^ weight) for i in range(DEV)])
-        rs = [across(t, 2 << (n + 2) % 3) for n, t in enumerate(ts)]
+
+        def to_mates(arrs, token):
+            *held, token = lax.optimization_barrier((*arrs, token))
+            return [across(r, 1) for r in held], token
+
+        rs = []
+        for n, t in enumerate(ts):
+            rs.append(across(t, 2 << (n + 2) % 3))
         outs = run_write(o, [v.reshape(-1, LANES) for v in made], so, sv)
-        short, out, inn, in0, mid, fc, short_b, out_b, inn_b, in0_b, mid_b, fc_b, vs, vo, vi, v0, vm, bn, vbn = outs
-        *held, vbn = lax.optimization_barrier((*rs, vbn))
-        mates = [across(r, 1) for r in held]
-        mid, mid_b = run_tail(((0, False), (0, True), (4, False)), [*ts, *us, *rs], mid, mid_b, 'write_tail')
-        mid, mid_b = run_tail(((4, True),), mates, mid, mid_b, 'write_last')
+        short, out, fc, short_b, out_b, fc_b, vs, vo, vi, v0, vm, bn, vbn = outs
+        mates, vbn = to_mates(rs[:3], vbn)
+        tail = run_tail((0, 1), [(ts, 0, False), (us, 0, True)], None)
+        *tail, token = run_tail((0,), [(rs, 4, False), (mates, 4, True)], tail)
+        last, token = to_mates(rs[3:], token)
+        tail = run_tail((1,), [(rs, 4, False)], (*tail, token))
+        *tail, _ = run_tail((1,), [(mates + last, 4, True)], tail)
+        inn, in0, mid, inn_b, in0_b, mid_b = tail
         news = [from_rows(v, e[1], old) for v, e, old in zip((vs, vo, vi, v0, vm), TABLE, olds)]
         vb, wb = sv[SUB:2 * SUB], sv[2 * SUB:]
         return (in0.reshape(w_in0.shape), short.reshape(w_short.shape), inn.reshape(w_in.shape),

time: 373 us -> 365 us (0.979)
  Pallas kernels: 361 us -> 342 us
  waiting for transfers between devices: 0.02 us -> 5.56 us
  starting transfers between devices: 2.76 us -> 7.18 us
    pallas_call x1, Pallas kernels: 311 us -> 291 us  [run_comm(): pl.pallas_call(comm_kernel, out_shape=[jax.ShapeDtypeStruct(s, F32) for s...]
    pallas_call x2 -> x4, Pallas kernels: 18.3 us -> 26.6 us  [run_tail(): pl.pallas_call(functools.partial(tail_kernel, jobs, size, count, len(give...]
    pallas_call x1, Pallas kernels: 31.7 us -> 24.4 us  [run_write(): pl.pallas_call(write_kernel, out_shape=[jax.ShapeDtypeStruct(*s) for s in...]
    ppermute x6 -> x12, waiting for transfers between devices: 0.02 us -> 5.56 us  [across(): return lax.ppermute(x, 'dp', [(i, i ^ weight) for i in range(DEV)])]
    ppermute x6 -> x12, starting transfers between devices: 2.76 us -> 7.18 us  [across(): return lax.ppermute(x, 'dp', [(i, i ^ weight) for i in range(DEV)])]
  transfers between devices with their start and end apart: 6 -> 12, of which waited for: 0 -> 3; matrix products, arithmetic and copies ran while one was open for 1% -> 1% of each run, Pallas kernels for 12% -> 13%
where the time goes in v5:
time: 365 us
  Pallas kernels  342 us (94%)
  local copies, waits for them, and re-layouts  7.9 us (2%)
  starting transfers between devices  7.18 us (2%)
  waiting for transfers between devices  5.56 us (2%)
    pallas_call x1, Pallas kernels, run_comm(): pl.pallas_call(comm_kernel, out_shape=[jax.ShapeDtypeStruct(s, F32) for s...  291 us
    pallas_call x4, Pallas kernels, run_tail(): pl.pallas_call(functools.partial(tail_kernel, jobs, size, count, len(give...  26.6 us
    pallas_call x1, Pallas kernels, run_write(): pl.pallas_call(write_kernel, out_shape=[jax.ShapeDtypeStruct(*s) for s in...  24.4 us
  transfers between devices with their start and end apart: 12, of which 3 were waited for; matrix products, arithmetic and copies ran while one was open for 1% of the time, Pallas kernels for 13%

profile of v5, /device:TPU:1, one launch (start us, length us, event | category | flops | bytes accessed | tf_op | source)
XLA Modules:
  0.0 364.5 jit_solution(10418838139946460554)
XLA Ops:
  1.3 1.4 reshape.194
  2.8 1.0 copy.71
  3.8 0.8 dynamic_update_slice.3
  4.6 0.0 copy-start.5
  4.6 0.6 copy-done.5
  5.2 291.4 %lars_comm.1 = (f32[24,16,32,512]{3,2,1,0:T(8,128)}, f32[4,4,32,512]{3,2,1,0:T(8,128)}, f32[4,4,32,512]{3,2,1,0:T(8,128)}, f32[4,4,32,512]{3,2,1,0:T(8,128)}, f3...) custom-call(f32[1,1]{1,0:T(1,128)} %bitcast.70.lr_ref, ...), custom_call_target="tpu_custom_call" | custom-call | tf_op jit(solution)/shard_map/lars_comm/pallas_call | solution.py:433
  296.6 1.2 collective-permute-start.3
  297.8 0.5 collective-permute-start.4
  298.3 0.5 collective-permute-start.5
  298.8 0.0 copy-start
  298.8 24.4 %write_out.1 = (f32[1,16,64,2048]{3,2,1,0:T(8,128)}, f32[2,16,32,2048]{3,2,1,0:T(8,128)}, f32[1000,2048]{1,0:T(8,128)}, bf16[1,16,64,2048]{3,2,1,0:T(8,128)(2,1)...) custom-call(f32[24,16,32,512]{3,2,1,0:T(8,128)} %get-tuple-element.9, ...), custom_call_target="tpu_custom_call" | custom-call | flops 100000000 | bytes 62914560 | tf_op jit(solution)/shard_map/write_out/pallas_call | solution.py:548
  323.2 0.0 collective-permute-done.3.refs_0_
  323.2 0.0 collective-permute-done.4.refs_1_
  323.2 0.0 collective-permute-done.5.refs_2_
  323.2 1.0 collective-permute-start.6
  324.2 0.0 collective-permute-start.7
  324.2 0.5 collective-permute-start.8
  324.7 0.3 collective-permute-start
  325.0 1.0 collective-permute-start.1
  326.0 0.7 collective-permute-done.6.refs_3_
  326.7 0.0 copy-done
  326.7 0.5 collective-permute-start.2
  327.2 0.4 copy-done.1
  327.7 12.1 %shard_map.408 = (f32[1,16,128,512]{3,2,1,0:T(8,128)}, f32[1,16,64,512]{3,2,1,0:T(8,128)}, f32[2,16,288,512]{3,2,1,0:T(8,128)}, bf16[1,16,128,512]{3,2,1,0:T(8,1...) custom-call(f32[4,4,32,512]{3,2,1,0:T(8,128)} %get-tuple-element.94.refs_0_, ...), custom_call_target="tpu_custom_call" | custom-call | flops 33333332 | bytes 31457280 | tf_op jit(solution)/shard_map/pallas_call | solution.py:640
  339.8 0.0 collective-permute-done.7.refs_4_
  339.8 0.0 collective-permute-done.8.refs_5_
  339.8 0.0 copy-start.4
  339.8 0.0 copy-start.3
  339.8 6.5 %shard_map.409 = (f32[1,16,128,512]{3,2,1,0:T(8,128)}, f32[1,16,64,512]{3,2,1,0:T(8,128)}, f32[2,16,288,512]{3,2,1,0:T(8,128)}, bf16[1,16,128,512]{3,2,1,0:T(8,1...) custom-call(f32[4,4,32,512]{3,2,1,0:T(8,128)} %collective-permute-do, ...), custom_call_target="tpu_custom_call", output_to_operand_aliasing={{0}: (6, {}), {1}: (7, {}), {2}: (8, {}), {3}: (9, {}), {4}... | custom-call | flops 33333332 | bytes 15728640 | tf_op jit(solution)/shard_map/pallas_call | solution.py:640
  346.3 3.4 collective-permute-done.refs_0_
  349.7 0.0 collective-permute-done.1.refs_1_
  349.7 1.4 collective-permute-done.2.refs_2_
  351.1 1.2 collective-permute-start.9
  352.4 0.0 collective-permute-start.10
  352.4 0.5 collective-permute-start.11
  352.9 0.0 copy-done.4
  352.9 0.6 slice_bitcast_fusion
  353.5 0.6 dynamic_slice.3
  354.1 0.0 copy-done.3
  354.1 0.2 copy.74
  354.3 1.3 reshape.221
  355.5 4.0 %shard_map.410 = (f32[1,16,128,512]{3,2,1,0:T(8,128)}, f32[1,16,64,512]{3,2,1,0:T(8,128)}, f32[2,16,288,512]{3,2,1,0:T(8,128)}, bf16[1,16,128,512]{3,2,1,0:T(8,1...) custom-call(f32[4,4,32,512]{3,2,1,0:T(8,128)} %collective-permute-do, ...), custom_call_target="tpu_custom_call", output_to_operand_aliasing={{0}: (3, {}), {1}: (4, {}), {2}: (5, {}), {3}: (6, {}), {4}... | custom-call | flops 33333332 | bytes 7864320 | tf_op jit(solution)/shard_map/pallas_call | solution.py:640
  359.6 0.0 collective-permute-done.9.refs_0_
  359.6 0.0 copy-start.2
  359.6 0.0 collective-permute-done.10.refs_1_
  359.6 0.0 collective-permute-done.11.refs_2_
  359.6 0.9 copy-done.2
  360.5 4.0 %shard_map.411 = (f32[1,16,128,512]{3,2,1,0:T(8,128)}, f32[1,16,64,512]{3,2,1,0:T(8,128)}, f32[2,16,288,512]{3,2,1,0:T(8,128)}, bf16[1,16,128,512]{3,2,1,0:T(8,1...) custom-call(f32[4,4,32,512]{3,2,1,0:T(8,128)} %copy-done.2, ...), custom_call_target="tpu_custom_call", output_to_operand_aliasing={{0}: (3, {}), {1}: (4, {}), {2}: (5, {}), {3}: (6, {}), {4}... | custom-call | flops 33333332 | bytes 7864320 | tf_op jit(solution)/shard_map/pallas_call | solution.py:640
  (2 shorter events, 0.0 us)
Async XLA Ops:
  4.6 0.6 copy-start.5
  296.6 26.6 %collective-permute-start.3 = (f32[4,4,32,512]{3,2,1,0:T(8,128)}, f32[4,4,32,512]{3,2,1,0:T(8,128)}, u32[]{:S(2)}, u32[]{:S(2)}) collective-permute-start(f32[4,4,32,512]{3,2,1,0:T(8,128)} %get-tuple-element.94.refs_0_), channel_id=1, source_target_pairs={{0,8},{1,9},{2,10},{3,11},{4,12},{5,13},{6,14},{7,15},{8,0},{9,1},... | collective-permute-start | bytes 3145736 | tf_op jit(solution)/shard_map/ppermute | solution.py:691
  297.8 25.4 %collective-permute-start.4 = (f32[4,4,32,512]{3,2,1,0:T(8,128)}, f32[4,4,32,512]{3,2,1,0:T(8,128)}, u32[]{:S(2)}, u32[]{:S(2)}) collective-permute-start(f32[4,4,32,512]{3,2,1,0:T(8,128)} %get-tuple-element.95.refs_1_), channel_id=1, source_target_pairs={{0,2},{1,3},{2,0},{3,1},{4,6},{5,7},{6,4},{7,5},{8,10},{9,11},{10,... | collective-permute-start | bytes 3145736 | tf_op jit(solution)/shard_map/ppermute | solution.py:691
  298.3 24.9 %collective-permute-start.5 = (f32[4,4,32,512]{3,2,1,0:T(8,128)}, f32[4,4,32,512]{3,2,1,0:T(8,128)}, u32[]{:S(2)}, u32[]{:S(2)}) collective-permute-start(f32[4,4,32,512]{3,2,1,0:T(8,128)} %get-tuple-element.96.refs_2_), channel_id=1, source_target_pairs={{0,4},{1,5},{2,6},{3,7},{4,0},{5,1},{6,2},{7,3},{8,12},{9,13},{10,... | collective-permute-start | bytes 3145736 | tf_op jit(solution)/shard_map/ppermute | solution.py:691
  298.8 27.9 %copy-start = (f32[4,4,32,512]{3,2,1,0:T(8,128)S(1)}, f32[4,4,32,512]{3,2,1,0:T(8,128)}, u32[]{:S(2)}) copy-start(f32[4,4,32,512]{3,2,1,0:T(8,128)} %get-tuple-element.93.refs_8_) | copy-start | bytes 3145732
  323.2 3.5 collective-permute-start.6
  324.2 15.6 %collective-permute-start.7 = (f32[4,4,32,512]{3,2,1,0:T(8,128)}, f32[4,4,32,512]{3,2,1,0:T(8,128)}, u32[]{:S(2)}, u32[]{:S(2)}) collective-permute-start(f32[4,4,32,512]{3,2,1,0:T(8,128)} %collective-permute-done.4.refs_1_), channel_id=1, source_target_pairs={{0,1},{1,0},{2,3},{3,2},{4,5},{5,4},{6,7},{7,6},{8,9},{9,8},{10,11... | collective-permute-start | bytes 3145736 | tf_op jit(solution)/shard_map/ppermute | solution.py:691
  324.2 15.6 %collective-permute-start.8 = (f32[4,4,32,512]{3,2,1,0:T(8,128)}, f32[4,4,32,512]{3,2,1,0:T(8,128)}, u32[]{:S(2)}, u32[]{:S(2)}) collective-permute-start(f32[4,4,32,512]{3,2,1,0:T(8,128)} %collective-permute-done.5.refs_2_), channel_id=1, source_target_pairs={{0,1},{1,0},{2,3},{3,2},{4,5},{5,4},{6,7},{7,6},{8,9},{9,8},{10,11... | collective-permute-start | bytes 3145736 | tf_op jit(solution)/shard_map/ppermute | solution.py:691
  324.7 25.0 %collective-permute-start = (f32[4,4,32,512]{3,2,1,0:T(8,128)}, f32[4,4,32,512]{3,2,1,0:T(8,128)}, u32[]{:S(2)}, u32[]{:S(2)}) collective-permute-start(f32[4,4,32,512]{3,2,1,0:T(8,128)} %get-tuple-element.91.refs_6_), channel_id=1, source_target_pairs={{0,8},{1,9},{2,10},{3,11},{4,12},{5,13},{6,14},{7,15},{8,0},{9,1},... | collective-permute-start | bytes 3145736 | tf_op jit(solution)/shard_map/ppermute | solution.py:691
  325.0 24.7 %collective-permute-start.1 = (f32[4,4,32,512]{3,2,1,0:T(8,128)}, f32[4,4,32,512]{3,2,1,0:T(8,128)}, u32[]{:S(2)}, u32[]{:S(2)}) collective-permute-start(f32[4,4,32,512]{3,2,1,0:T(8,128)} %get-tuple-element.92.refs_7_), channel_id=1, source_target_pairs={{0,2},{1,3},{2,0},{3,1},{4,6},{5,7},{6,4},{7,5},{8,10},{9,11},{10,... | collective-permute-start | bytes 3145736 | tf_op jit(solution)/shard_map/ppermute | solution.py:691
  326.7 1.0 copy-start.1
  326.7 24.5 %collective-permute-start.2 = (f32[4,4,32,512]{3,2,1,0:T(8,128)S(1)}, f32[4,4,32,512]{3,2,1,0:T(8,128)}, u32[]{:S(2)}, u32[]{:S(2)}) collective-permute-start(f32[4,4,32,512]{3,2,1,0:T(8,128)S(1)} %copy-done), channel_id=1, source_target_pairs={{0,4},{1,5},{2,6},{3,7},{4,0},{5,1},{6,2},{7,3},{8,12},{9,13},{10,... | collective-permute-start | bytes 3145736 | tf_op jit(solution)/shard_map/ppermute | solution.py:691
  339.8 13.1 %copy-start.4 = (f32[24,128]{1,0:T(8,128)S(1)}, f32[24,128]{1,0:T(8,128)}, u32[]{:S(2)}) copy-start(f32[24,128]{1,0:T(8,128)} %get-tuple-element.104.sv_ref) | copy-start | bytes 36868
  339.8 14.3 %copy-start.3 = (f32[1000,128]{1,0:T(8,128)S(1)}, f32[1000,128]{1,0:T(8,128)}, u32[]{:S(2)}) copy-start(f32[1000,128]{1,0:T(8,128)} %get-tuple-element.158) | copy-start | bytes 1536004
  351.1 8.4 %collective-permute-start.9 = (f32[4,4,32,512]{3,2,1,0:T(8,128)}, f32[4,4,32,512]{3,2,1,0:T(8,128)S(1)}, u32[]{:S(2)}, u32[]{:S(2)}) collective-permute-start(f32[4,4,32,512]{3,2,1,0:T(8,128)} %collective-permute-done.refs_0_), channel_id=1, source_target_pairs={{0,1},{1,0},{2,3},{3,2},{4,5},{5,4},{6,7},{7,6},{8,9},{9,8},{10,11... | collective-permute-start | bytes 3145736 | tf_op jit(solution)/shard_map/ppermute | solution.py:691
  352.4 7.2 %collective-permute-start.10 = (f32[4,4,32,512]{3,2,1,0:T(8,128)}, f32[4,4,32,512]{3,2,1,0:T(8,128)}, u32[]{:S(2)}, u32[]{:S(2)}) collective-permute-start(f32[4,4,32,512]{3,2,1,0:T(8,128)} %collective-permute-done.1.refs_1_), channel_id=1, source_target_pairs={{0,1},{1,0},{2,3},{3,2},{4,5},{5,4},{6,7},{7,6},{8,9},{9,8},{10,11... | collective-permute-start | bytes 3145736 | tf_op jit(solution)/shard_map/ppermute | solution.py:691
  352.4 7.2 %collective-permute-start.11 = (f32[4,4,32,512]{3,2,1,0:T(8,128)}, f32[4,4,32,512]{3,2,1,0:T(8,128)}, u32[]{:S(2)}, u32[]{:S(2)}) collective-permute-start(f32[4,4,32,512]{3,2,1,0:T(8,128)} %collective-permute-done.2.refs_2_), channel_id=1, source_target_pairs={{0,1},{1,0},{2,3},{3,2},{4,5},{5,4},{6,7},{7,6},{8,9},{9,8},{10,11... | collective-permute-start | bytes 3145736 | tf_op jit(solution)/shard_map/ppermute | solution.py:691
  359.6 1.0 copy-start.2

commit v6 on v5

--- a/solution.py
+++ b/solution.py
@@ -28,8 +28,8 @@
 TAILK = GROUP // 3
 SPLIT = 24
 NSLOT = 15
-LAGS = (3, 6, 9, 12)
-AG0 = 45
+LAGS = (2, 5, 8, 11)
+AG0 = 41
 FIRST = 1
 AGLAGS = ((2, 6), (4, 12), (8, 18))
 AGEND = 21
@@ -389,10 +389,10 @@
         for n, at in enumerate((SPLIT, NCH)):
             pl.when(s == at + LAGS[3])(functools.partial(norms_out, n))
             pl.when(s == at + LAGS[3] + 4)(functools.partial(norms_in, n))
+        stage(s, 0, rs_start)
+        for level in range(3):
+            stage(s, LAGS[level], functools.partial(rs_fold, level=level))
         stage(s, LAGS[3], rs_end)
-        for level in (2, 1, 0):
-            stage(s, LAGS[level], functools.partial(rs_fold, level=level))
-        stage(s, 0, rs_start)
         stage(s, AG0 + AGEND, ag_end)
         for n, lag in AGLAGS[::-1]:
             stage(s, AG0 + lag, functools.partial(gather, n=n))
@@ -453,6 +453,7 @@
 AHEAD = 6
 NFC = 4
 WRITE_FLOPS = 10 ** 8
+VMEM = 67043328
 
 
 def write_kernel(o_ref, ns, no, ni, n0, nm, so_ref, sv_ref, os_, oo, of, bs, bo, bf,
@@ -555,7 +556,7 @@
             pltpu.VMEM((NFC, LANES, DEV * LANES), F32), pltpu.VMEM((NFC, LANES, DEV * LANES), BF16),
             pltpu.VMEM(((NCH - FCN) * LANES, LANES), F32),
             dma((NBUF,)), dma((NBUF,)), dma((NBUF,)), dma],
-        compiler_params=pltpu.CompilerParams(vmem_limit_bytes=62 * 1024 * 1024),
+        compiler_params=pltpu.CompilerParams(vmem_limit_bytes=VMEM),
         cost_estimate=pl.CostEstimate(flops=WRITE_FLOPS, bytes_accessed=TAIL0 * 160 * U * CW, transcendentals=0),
         name='write_out',
     )(o, *moments_new, so, sv)
@@ -645,7 +646,7 @@
         input_output_aliases={count + n: n for n in range(len(given))},
         scratch_shapes=[pltpu.VMEM((ring, size, U, CW), F32), pltpu.VMEM((ring, size, U, CW), BF16),
                         dma((ring,)), dma((ring,)), dma((ring,))],
-        compiler_params=pltpu.CompilerParams(vmem_limit_bytes=62 * 1024 * 1024),
+        compiler_params=pltpu.CompilerParams(vmem_limit_bytes=VMEM),
         cost_estimate=pl.CostEstimate(flops=WRITE_FLOPS // 3, bytes_accessed=len(jobs) * size * 10 * U * CW,
                                       transcendentals=0),
     )(*srcs, *given, *tokens)

time: 365 us -> 368 us (level)
  transfers between devices with their start and end apart: 12 -> 12, of which waited for: 3 -> 4; matrix products, arithmetic and copies ran while one was open for 1% -> 1% of each run, Pallas kernels for 13% -> 13%
where the time goes in v6:
time: 368 us; the launch traced here: 367 us
  Pallas kernels  343 us (93%)
  local copies, waits for them, and re-layouts  8.22 us (2%)
  waiting for transfers between devices  7.67 us (2%)
  starting transfers between devices  7.02 us (2%)
    pallas_call x1, Pallas kernels, run_comm(): pl.pallas_call(comm_kernel, out_shape=[jax.ShapeDtypeStruct(s, F32) for s...  292 us
    pallas_call x4, Pallas kernels, run_tail(): pl.pallas_call(functools.partial(tail_kernel, jobs, size, count, len(give...  26.5 us
    pallas_call x1, Pallas kernels, run_write(): pl.pallas_call(write_kernel, out_shape=[jax.ShapeDtypeStruct(*s) for s in...  24.3 us
    ppermute x12, waiting for transfers between devices, across(): return lax.ppermute(x, 'dp', [(i, i ^ weight) for i in range(DEV)])  7.67 us
  transfers between devices with their start and end apart: 12, of which 4 were waited for; matrix products, arithmetic and copies ran while one was open for 1% of the time, Pallas kernels for 13%

profile of v6, /device:TPU:1, one launch (start us, length us, event | category | flops | bytes accessed | tf_op | source)
XLA Modules:
  0.0 367.4 jit_solution(1687495367666757370)
XLA Ops:
  1.3 1.4 reshape.194
  2.8 1.0 copy.71
  3.8 0.8 dynamic_update_slice.3
  4.6 0.0 copy-start
  4.6 0.6 copy-done
  5.2 292.2 %lars_comm.1 = (f32[24,16,32,512]{3,2,1,0:T(8,128)}, f32[4,4,32,512]{3,2,1,0:T(8,128)}, f32[4,4,32,512]{3,2,1,0:T(8,128)}, f32[4,4,32,512]{3,2,1,0:T(8,128)}, f3...) custom-call(f32[1,1]{1,0:T(1,128)} %bitcast.70.lr_ref, ...), custom_call_target="tpu_custom_call" | custom-call | tf_op jit(solution)/shard_map/lars_comm/pallas_call | solution.py:433
  297.4 1.5 collective-permute-start.3
  298.9 1.2 collective-permute-start.4
  300.1 0.3 collective-permute-start.5
  300.4 24.3 %write_out.1 = (f32[1,16,64,2048]{3,2,1,0:T(8,128)}, f32[2,16,32,2048]{3,2,1,0:T(8,128)}, f32[1000,2048]{1,0:T(8,128)}, bf16[1,16,64,2048]{3,2,1,0:T(8,128)(2,1)...) custom-call(f32[24,16,32,512]{3,2,1,0:T(8,128)} %get-tuple-element.9, ...), custom_call_target="tpu_custom_call" | custom-call | flops 100000000 | bytes 62914560 | tf_op jit(solution)/shard_map/write_out/pallas_call | solution.py:549
  324.7 0.0 collective-permute-done.3.refs_0_
  324.7 0.0 collective-permute-done.4.refs_1_
  324.7 0.2 collective-permute-done.5.refs_2_
  324.9 1.0 collective-permute-start.6
  326.0 0.0 collective-permute-start.7
  326.0 0.5 collective-permute-start.8
  326.5 0.3 collective-permute-start
  326.8 0.0 collective-permute-start.1
  326.8 1.8 collective-permute-done.6.refs_3_
  328.6 0.4 collective-permute-start.2
  329.0 12.1 %shard_map.408 = (f32[1,16,128,512]{3,2,1,0:T(8,128)}, f32[1,16,64,512]{3,2,1,0:T(8,128)}, f32[2,16,288,512]{3,2,1,0:T(8,128)}, bf16[1,16,128,512]{3,2,1,0:T(8,1...) custom-call(f32[4,4,32,512]{3,2,1,0:T(8,128)} %get-tuple-element.94.refs_0_, ...), custom_call_target="tpu_custom_call" | custom-call | flops 33333332 | bytes 31457280 | tf_op jit(solution)/shard_map/pallas_call | solution.py:641
  341.1 0.0 collective-permute-done.7.refs_4_
  341.1 0.0 collective-permute-done.8.refs_5_
  341.1 6.4 %shard_map.409 = (f32[1,16,128,512]{3,2,1,0:T(8,128)}, f32[1,16,64,512]{3,2,1,0:T(8,128)}, f32[2,16,288,512]{3,2,1,0:T(8,128)}, bf16[1,16,128,512]{3,2,1,0:T(8,1...) custom-call(f32[4,4,32,512]{3,2,1,0:T(8,128)} %collective-permute-do, ...), custom_call_target="tpu_custom_call", output_to_operand_aliasing={{0}: (6, {}), {1}: (7, {}), {2}: (8, {}), {3}: (9, {}), {4}... | custom-call | flops 33333332 | bytes 15728640 | tf_op jit(solution)/shard_map/pallas_call | solution.py:641
  347.6 3.9 %collective-permute-done.refs_0_ = f32[4,4,32,512]{3,2,1,0:T(8,128)} collective-permute-done((f32[4,4,32,512]{3,2,1,0:T(8,128)}, f32[4,4,32,512]{3,2,1,0:T(8,128)}, u32[]{:S(2)}, u32[]{:S(2)}) %collective-permute-start) | collective-permute-done | bytes 1048608 | tf_op jit(solution)/shard_map/ppermute | solution.py:692
  351.5 0.0 collective-permute-done.1.refs_1_
  351.5 1.7 collective-permute-done.2.refs_2_
  353.3 1.2 collective-permute-start.9
  354.5 0.0 collective-permute-start.10
  354.5 0.5 collective-permute-start.11
  355.0 1.3 slice_bitcast_fusion
  356.3 0.6 dynamic_slice.3
  356.9 1.2 copy.74
  358.1 1.3 reshape.221
  359.4 4.0 %shard_map.410 = (f32[1,16,128,512]{3,2,1,0:T(8,128)}, f32[1,16,64,512]{3,2,1,0:T(8,128)}, f32[2,16,288,512]{3,2,1,0:T(8,128)}, bf16[1,16,128,512]{3,2,1,0:T(8,1...) custom-call(f32[4,4,32,512]{3,2,1,0:T(8,128)} %collective-permute-do, ...), custom_call_target="tpu_custom_call", output_to_operand_aliasing={{0}: (3, {}), {1}: (4, {}), {2}: (5, {}), {3}: (6, {}), {4}... | custom-call | flops 33333332 | bytes 7864320 | tf_op jit(solution)/shard_map/pallas_call | solution.py:641
  363.4 0.0 collective-permute-done.9.refs_0_
  363.4 0.0 collective-permute-done.10.refs_1_
  363.4 0.0 collective-permute-done.11.refs_2_
  363.4 4.0 %shard_map.411 = (f32[1,16,128,512]{3,2,1,0:T(8,128)}, f32[1,16,64,512]{3,2,1,0:T(8,128)}, f32[2,16,288,512]{3,2,1,0:T(8,128)}, bf16[1,16,128,512]{3,2,1,0:T(8,1...) custom-call(f32[4,4,32,512]{3,2,1,0:T(8,128)} %collective-permute-do, ...), custom_call_target="tpu_custom_call", output_to_operand_aliasing={{0}: (3, {}), {1}: (4, {}), {2}: (5, {}), {3}: (6, {}), {4}... | custom-call | flops 33333332 | bytes 7864320 | tf_op jit(solution)/shard_map/pallas_call | solution.py:641
  (1 shorter events, 0.0 us)
Async XLA Ops:
  4.6 0.6 copy-start
  297.4 27.3 %collective-permute-start.3 = (f32[4,4,32,512]{3,2,1,0:T(8,128)}, f32[4,4,32,512]{3,2,1,0:T(8,128)}, u32[]{:S(2)}, u32[]{:S(2)}) collective-permute-start(f32[4,4,32,512]{3,2,1,0:T(8,128)} %get-tuple-element.94.refs_0_), channel_id=1, source_target_pairs={{0,8},{1,9},{2,10},{3,11},{4,12},{5,13},{6,14},{7,15},{8,0},{9,1},... | collective-permute-start | bytes 3145736 | tf_op jit(solution)/shard_map/ppermute | solution.py:692
  298.9 25.8 %collective-permute-start.4 = (f32[4,4,32,512]{3,2,1,0:T(8,128)}, f32[4,4,32,512]{3,2,1,0:T(8,128)}, u32[]{:S(2)}, u32[]{:S(2)}) collective-permute-start(f32[4,4,32,512]{3,2,1,0:T(8,128)} %get-tuple-element.95.refs_1_), channel_id=1, source_target_pairs={{0,2},{1,3},{2,0},{3,1},{4,6},{5,7},{6,4},{7,5},{8,10},{9,11},{10,... | collective-permute-start | bytes 3145736 | tf_op jit(solution)/shard_map/ppermute | solution.py:692
  300.1 24.8 %collective-permute-start.5 = (f32[4,4,32,512]{3,2,1,0:T(8,128)}, f32[4,4,32,512]{3,2,1,0:T(8,128)}, u32[]{:S(2)}, u32[]{:S(2)}) collective-permute-start(f32[4,4,32,512]{3,2,1,0:T(8,128)} %get-tuple-element.96.refs_2_), channel_id=1, source_target_pairs={{0,4},{1,5},{2,6},{3,7},{4,0},{5,1},{6,2},{7,3},{8,12},{9,13},{10,... | collective-permute-start | bytes 3145736 | tf_op jit(solution)/shard_map/ppermute | solution.py:692
  324.9 3.7 collective-permute-start.6
  326.0 15.2 %collective-permute-start.7 = (f32[4,4,32,512]{3,2,1,0:T(8,128)}, f32[4,4,32,512]{3,2,1,0:T(8,128)}, u32[]{:S(2)}, u32[]{:S(2)}) collective-permute-start(f32[4,4,32,512]{3,2,1,0:T(8,128)} %collective-permute-done.4.refs_1_), channel_id=1, source_target_pairs={{0,1},{1,0},{2,3},{3,2},{4,5},{5,4},{6,7},{7,6},{8,9},{9,8},{10,11... | collective-permute-start | bytes 3145736 | tf_op jit(solution)/shard_map/ppermute | solution.py:692
  326.0 15.2 %collective-permute-start.8 = (f32[4,4,32,512]{3,2,1,0:T(8,128)}, f32[4,4,32,512]{3,2,1,0:T(8,128)}, u32[]{:S(2)}, u32[]{:S(2)}) collective-permute-start(f32[4,4,32,512]{3,2,1,0:T(8,128)} %collective-permute-done.5.refs_2_), channel_id=1, source_target_pairs={{0,1},{1,0},{2,3},{3,2},{4,5},{5,4},{6,7},{7,6},{8,9},{9,8},{10,11... | collective-permute-start | bytes 3145736 | tf_op jit(solution)/shard_map/ppermute | solution.py:692
  326.5 25.0 %collective-permute-start = (f32[4,4,32,512]{3,2,1,0:T(8,128)}, f32[4,4,32,512]{3,2,1,0:T(8,128)}, u32[]{:S(2)}, u32[]{:S(2)}) collective-permute-start(f32[4,4,32,512]{3,2,1,0:T(8,128)} %get-tuple-element.91.refs_6_), channel_id=1, source_target_pairs={{0,8},{1,9},{2,10},{3,11},{4,12},{5,13},{6,14},{7,15},{8,0},{9,1},... | collective-permute-start | bytes 3145736 | tf_op jit(solution)/shard_map/ppermute | solution.py:692
  326.8 24.7 %collective-permute-start.1 = (f32[4,4,32,512]{3,2,1,0:T(8,128)}, f32[4,4,32,512]{3,2,1,0:T(8,128)}, u32[]{:S(2)}, u32[]{:S(2)}) collective-permute-start(f32[4,4,32,512]{3,2,1,0:T(8,128)} %get-tuple-element.92.refs_7_), channel_id=1, source_target_pairs={{0,2},{1,3},{2,0},{3,1},{4,6},{5,7},{6,4},{7,5},{8,10},{9,11},{10,... | collective-permute-start | bytes 3145736 | tf_op jit(solution)/shard_map/ppermute | solution.py:692
  328.6 24.7 %collective-permute-start.2 = (f32[4,4,32,512]{3,2,1,0:T(8,128)}, f32[4,4,32,512]{3,2,1,0:T(8,128)}, u32[]{:S(2)}, u32[]{:S(2)}) collective-permute-start(f32[4,4,32,512]{3,2,1,0:T(8,128)} %get-tuple-element.93.refs_8_), channel_id=1, source_target_pairs={{0,4},{1,5},{2,6},{3,7},{4,0},{5,1},{6,2},{7,3},{8,12},{9,13},{10,... | collective-permute-start | bytes 3145736 | tf_op jit(solution)/shard_map/ppermute | solution.py:692
  353.3 10.1 %collective-permute-start.9 = (f32[4,4,32,512]{3,2,1,0:T(8,128)}, f32[4,4,32,512]{3,2,1,0:T(8,128)}, u32[]{:S(2)}, u32[]{:S(2)}) collective-permute-start(f32[4,4,32,512]{3,2,1,0:T(8,128)} %collective-permute-done.refs_0_), channel_id=1, source_target_pairs={{0,1},{1,0},{2,3},{3,2},{4,5},{5,4},{6,7},{7,6},{8,9},{9,8},{10,11... | collective-permute-start | bytes 3145736 | tf_op jit(solution)/shard_map/ppermute | solution.py:692
  354.5 8.9 %collective-permute-start.10 = (f32[4,4,32,512]{3,2,1,0:T(8,128)}, f32[4,4,32,512]{3,2,1,0:T(8,128)}, u32[]{:S(2)}, u32[]{:S(2)}) collective-permute-start(f32[4,4,32,512]{3,2,1,0:T(8,128)} %collective-permute-done.1.refs_1_), channel_id=1, source_target_pairs={{0,1},{1,0},{2,3},{3,2},{4,5},{5,4},{6,7},{7,6},{8,9},{9,8},{10,11... | collective-permute-start | bytes 3145736 | tf_op jit(solution)/shard_map/ppermute | solution.py:692
  354.5 8.9 %collective-permute-start.11 = (f32[4,4,32,512]{3,2,1,0:T(8,128)}, f32[4,4,32,512]{3,2,1,0:T(8,128)}, u32[]{:S(2)}, u32[]{:S(2)}) collective-permute-start(f32[4,4,32,512]{3,2,1,0:T(8,128)} %collective-permute-done.2.refs_2_), channel_id=1, source_target_pairs={{0,1},{1,0},{2,3},{3,2},{4,5},{5,4},{6,7},{7,6},{8,9},{9,8},{10,11... | collective-permute-start | bytes 3145736 | tf_op jit(solution)/shard_map/ppermute | solution.py:692

commit v7 on v5

--- a/solution.py
+++ b/solution.py
@@ -28,7 +28,7 @@
 TAILK = GROUP // 3
 SPLIT = 24
 NSLOT = 15
-LAGS = (3, 6, 9, 12)
+LAGS = (3, 9, 12, 14)
 AG0 = 45
 FIRST = 1
 AGLAGS = ((2, 6), (4, 12), (8, 18))
@@ -186,7 +186,13 @@
         for i in range(SUB):
             part = line[i * LANES:min(CLASSES, (i + 1) * LANES)]
             bias[i:i + 1, :] = jnp.sum(jnp.where(diagonal[:part.shape[0]], part, 0.0), axis=0, keepdims=True)
-        bias[SUB:, :] = v_bias[...]
+        width = v_bias.shape[1]
+        spread = (width, SUB * LANES)
+        chosen = (lax.broadcasted_iota(jnp.int32, spread, 0) + me * width == lax.broadcasted_iota(jnp.int32, spread, 1))
+        placed = jnp.dot(jnp.broadcast_to(v_bias[...], (SUB, width)), jnp.where(chosen, 1.0, 0.0),
+                         precision=lax.Precision.HIGHEST, preferred_element_type=F32)
+        for i in range(SUB):
+            bias[SUB + i:SUB + i + 1, :] = placed[0:1, i * LANES:(i + 1) * LANES]
         sb[me, SUB:, :] = bias[...]
         each_other(lambda dev: remote(bias, sb.at[me, pl.ds(SUB, 2 * SUB)], sm_send, sm_recv, dev).start())
 
@@ -453,10 +459,11 @@
 AHEAD = 6
 NFC = 4
 WRITE_FLOPS = 10 ** 8
+VMEM = 67043328
 
 
 def write_kernel(o_ref, ns, no, ni, n0, nm, so_ref, sv_ref, os_, oo, of, bs, bo, bf,
-                 vs, vo, vi, v0, vm, bn, vbn,
+                 vs, vo, vi, v0, vm, bn, vbn, wb,
                  buf, bbuf, fbuf, fbbuf, vbuf, in_sem, f_sem, b_sem, v_sem):
     def view(c, refs):
         entry, ref = [(e, r) for e, r in zip(TABLE, refs) if c >= e[0]][-1]
@@ -502,6 +509,9 @@
         d.start()
     bn[...] = so_ref[...]
     vbn[...] = sv_ref[0:SUB]
+    for i in range(SUB):
+        lanes = slice(i * LANES, min(CLASSES, (i + 1) * LANES))
+        wb[:, lanes] = sv_ref[2 * SUB + i:2 * SUB + i + 1, :lanes.stop - lanes.start]
     for i in range(TAIL0):
         slot = i % NBUF
         for d in load(i):
@@ -544,18 +554,18 @@
     tile = (SUB, LANES)
     dma = pltpu.SemaphoreType.DMA
     outs = [(s, F32) for s in shapes] + [(s, BF16) for s in shapes] + [(s, F32) for s in moments]
-    outs += [((DEV,) + tile, F32), (tile, F32)]
+    outs += [((DEV,) + tile, F32), (tile, F32), ((1, CLASSES), F32)]
     return pl.pallas_call(
         write_kernel,
         out_shape=[jax.ShapeDtypeStruct(*s) for s in outs],
         in_specs=[anyspec] * 6 + [vspec] * 2,
-        out_specs=[anyspec] * 11 + [vspec] * 2,
+        out_specs=[anyspec] * 11 + [vspec] * 3,
         scratch_shapes=[
             pltpu.VMEM((NBUF, DEV, U, CW), F32), pltpu.VMEM((NBUF, DEV, U, CW), BF16),
             pltpu.VMEM((NFC, LANES, DEV * LANES), F32), pltpu.VMEM((NFC, LANES, DEV * LANES), BF16),
             pltpu.VMEM(((NCH - FCN) * LANES, LANES), F32),
             dma((NBUF,)), dma((NBUF,)), dma((NBUF,)), dma],
-        compiler_params=pltpu.CompilerParams(vmem_limit_bytes=62 * 1024 * 1024),
+        compiler_params=pltpu.CompilerParams(vmem_limit_bytes=VMEM),
         cost_estimate=pl.CostEstimate(flops=WRITE_FLOPS, bytes_accessed=TAIL0 * 160 * U * CW, transcendentals=0),
         name='write_out',
     )(o, *moments_new, so, sv)
@@ -645,7 +655,7 @@
         input_output_aliases={count + n: n for n in range(len(given))},
         scratch_shapes=[pltpu.VMEM((ring, size, U, CW), F32), pltpu.VMEM((ring, size, U, CW), BF16),
                         dma((ring,)), dma((ring,)), dma((ring,))],
-        compiler_params=pltpu.CompilerParams(vmem_limit_bytes=62 * 1024 * 1024),
+        compiler_params=pltpu.CompilerParams(vmem_limit_bytes=VMEM),
         cost_estimate=pl.CostEstimate(flops=WRITE_FLOPS // 3, bytes_accessed=len(jobs) * size * 10 * U * CW,
                                       transcendentals=0),
     )(*srcs, *given, *tokens)
@@ -679,10 +689,8 @@
         moments = [to_rows(v, e) for v, e in zip(olds, TABLE)]
         moments.append(v_fc.reshape(LANES, CLASSES).T)
         tiles = (-1, SUB, LANES)
-        pad = SUB * LANES
-        placed = lax.dynamic_update_slice(jnp.zeros((pad,), F32), v_bias, (rank * width,))
         small = [g_bn.reshape(tiles), w_bn.reshape(-1, LANES), v_bn.reshape(SUB, LANES),
-                 w_bias.reshape(1, CLASSES), placed.reshape(SUB, LANES)]
+                 w_bias.reshape(1, CLASSES), v_bias.reshape(1, width)]
         o, *made, nf, so, sv = run_comm(
             learn_rate.reshape(1, 1), grads, pooled, dlogits.T, weights, moments, small)
         ts, us, made = made[:6], made[6:12], made[12:]
@@ -698,7 +706,7 @@
         for n, t in enumerate(ts):
             rs.append(across(t, 2 << (n + 2) % 3))
         outs = run_write(o, [v.reshape(-1, LANES) for v in made], so, sv)
-        short, out, fc, short_b, out_b, fc_b, vs, vo, vi, v0, vm, bn, vbn = outs
+        short, out, fc, short_b, out_b, fc_b, vs, vo, vi, v0, vm, bn, vbn, wb = outs
         mates, vbn = to_mates(rs[:3], vbn)
         tail = run_tail((0, 1), [(ts, 0, False), (us, 0, True)], None)
         *tail, token = run_tail((0,), [(rs, 4, False), (mates, 4, True)], tail)
@@ -707,10 +715,10 @@
         *tail, _ = run_tail((1,), [(mates + last, 4, True)], tail)
         inn, in0, mid, inn_b, in0_b, mid_b = tail
         news = [from_rows(v, e[1], old) for v, e, old in zip((vs, vo, vi, v0, vm), TABLE, olds)]
-        vb, wb = sv[SUB:2 * SUB], sv[2 * SUB:]
+        vb = sv[SUB:2 * SUB]
         return (in0.reshape(w_in0.shape), short.reshape(w_short.shape), inn.reshape(w_in.shape),
                 mid.reshape(w_mid.shape), out.reshape(w_out.shape), fc.T,
-                bn.reshape(w_bn.shape), wb.reshape(-1)[:CLASSES],
+                bn.reshape(w_bn.shape), wb.reshape(w_bias.shape),
                 in0_b.reshape(w_in0.shape), short_b.reshape(w_short.shape), inn_b.reshape(w_in.shape),
                 mid_b.reshape(w_mid.shape), out_b.reshape(w_out.shape), fc_b.T,
                 news[3], news[0], news[2], news[4], news[1], nf.T.reshape(v_fc.shape),

time: 365 us -> 364 us (level)
  transfers between devices with their start and end apart: 12 -> 12, of which waited for: 3 -> 4; matrix products, arithmetic and copies ran while one was open for 1% -> 1% of each run, Pallas kernels for 13% -> 13%
where the time goes in v7:
time: 364 us
  Pallas kernels  343 us (94%)
  starting transfers between devices  7.29 us (2%)
  local copies, waits for them, and re-layouts  6.21 us (2%)
  waiting for transfers between devices  6.08 us (2%)
    pallas_call x1, Pallas kernels, run_comm(): pl.pallas_call(comm_kernel, out_shape=[jax.ShapeDtypeStruct(s, F32) for s...  292 us
    pallas_call x4, Pallas kernels, run_tail(): pl.pallas_call(functools.partial(tail_kernel, jobs, size, count, len(give...  26.5 us
    pallas_call x1, Pallas kernels, run_write(): pl.pallas_call(write_kernel, out_shape=[jax.ShapeDtypeStruct(*s) for s in...  24.7 us
    ppermute x12, starting transfers between devices, across(): return lax.ppermute(x, 'dp', [(i, i ^ weight) for i in range(DEV)])  7.29 us
  transfers between devices with their start and end apart: 12, of which 4 were waited for; matrix products, arithmetic and copies ran while one was open for 1% of the time, Pallas kernels for 13%

profile of v7, /device:TPU:1, one launch (start us, length us, event | category | flops | bytes accessed | tf_op | source)
XLA Modules:
  0.0 363.8 jit_solution(3020665867260778845)
XLA Ops:
  1.3 1.4 reshape.194
  2.8 1.0 copy.71
  3.7 291.5 %lars_comm.1 = (f32[24,16,32,512]{3,2,1,0:T(8,128)}, f32[4,4,32,512]{3,2,1,0:T(8,128)}, f32[4,4,32,512]{3,2,1,0:T(8,128)}, f32[4,4,32,512]{3,2,1,0:T(8,128)}, f3...) custom-call(f32[1,1]{1,0:T(1,128)} %bitcast.68.lr_ref, ...), custom_call_target="tpu_custom_call" | custom-call | tf_op jit(solution)/shard_map/lars_comm/pallas_call | solution.py:439
  295.3 1.1 collective-permute-start.3
  296.4 0.5 collective-permute-start.4
  296.9 0.7 collective-permute-start.5
  297.6 24.7 %write_out.1 = (f32[1,16,64,2048]{3,2,1,0:T(8,128)}, f32[2,16,32,2048]{3,2,1,0:T(8,128)}, f32[1000,2048]{1,0:T(8,128)}, bf16[1,16,64,2048]{3,2,1,0:T(8,128)(2,1)...) custom-call(f32[24,16,32,512]{3,2,1,0:T(8,128)} %get-tuple-element.9, ...), custom_call_target="tpu_custom_call" | custom-call | flops 100000000 | bytes 62914560 | tf_op jit(solution)/shard_map/write_out/pallas_call | solution.py:558
  322.4 0.0 collective-permute-done.3.refs_0_
  322.4 0.0 collective-permute-done.4.refs_1_
  322.4 0.0 collective-permute-done.5.refs_2_
  322.4 0.5 collective-permute-start.6
  322.9 0.1 collective-permute-start.7
  323.0 0.5 collective-permute-start.8
  323.4 0.6 collective-permute-start
  324.0 0.9 collective-permute-start.1
  324.9 0.7 collective-permute-done.6.refs_3_
  325.6 0.7 collective-permute-start.2
  326.3 12.1 %shard_map.408 = (f32[1,16,128,512]{3,2,1,0:T(8,128)}, f32[1,16,64,512]{3,2,1,0:T(8,128)}, f32[2,16,288,512]{3,2,1,0:T(8,128)}, bf16[1,16,128,512]{3,2,1,0:T(8,1...) custom-call(f32[4,4,32,512]{3,2,1,0:T(8,128)} %get-tuple-element.95.refs_0_, ...), custom_call_target="tpu_custom_call" | custom-call | flops 33333332 | bytes 31457280 | tf_op jit(solution)/shard_map/pallas_call | solution.py:650
  338.4 0.0 collective-permute-done.7.refs_4_
  338.4 0.0 collective-permute-done.8.refs_5_
  338.4 6.4 %shard_map.409 = (f32[1,16,128,512]{3,2,1,0:T(8,128)}, f32[1,16,64,512]{3,2,1,0:T(8,128)}, f32[2,16,288,512]{3,2,1,0:T(8,128)}, bf16[1,16,128,512]{3,2,1,0:T(8,1...) custom-call(f32[4,4,32,512]{3,2,1,0:T(8,128)} %collective-permute-do, ...), custom_call_target="tpu_custom_call", output_to_operand_aliasing={{0}: (6, {}), {1}: (7, {}), {2}: (8, {}), {3}: (9, {}), {4}... | custom-call | flops 33333332 | bytes 15728640 | tf_op jit(solution)/shard_map/pallas_call | solution.py:650
  344.8 3.6 collective-permute-done.refs_0_
  348.4 0.3 collective-permute-done.1.refs_1_
  348.8 1.5 collective-permute-done.2.refs_2_
  350.2 1.2 collective-permute-start.9
  351.4 0.0 collective-permute-start.10
  351.4 0.5 collective-permute-start.11
  352.0 1.2 copy.74
  353.2 1.3 reshape.221
  354.5 0.7 slice_bitcast_fusion
  355.2 0.6 dynamic_slice.3
  355.7 4.0 %shard_map.410 = (f32[1,16,128,512]{3,2,1,0:T(8,128)}, f32[1,16,64,512]{3,2,1,0:T(8,128)}, f32[2,16,288,512]{3,2,1,0:T(8,128)}, bf16[1,16,128,512]{3,2,1,0:T(8,1...) custom-call(f32[4,4,32,512]{3,2,1,0:T(8,128)} %collective-permute-do, ...), custom_call_target="tpu_custom_call", output_to_operand_aliasing={{0}: (3, {}), {1}: (4, {}), {2}: (5, {}), {3}: (6, {}), {4}... | custom-call | flops 33333332 | bytes 7864320 | tf_op jit(solution)/shard_map/pallas_call | solution.py:650
  359.8 0.0 collective-permute-done.9.refs_0_
  359.8 0.0 collective-permute-done.10.refs_1_
  359.8 0.0 collective-permute-done.11.refs_2_
  359.8 4.0 %shard_map.411 = (f32[1,16,128,512]{3,2,1,0:T(8,128)}, f32[1,16,64,512]{3,2,1,0:T(8,128)}, f32[2,16,288,512]{3,2,1,0:T(8,128)}, bf16[1,16,128,512]{3,2,1,0:T(8,1...) custom-call(f32[4,4,32,512]{3,2,1,0:T(8,128)} %collective-permute-do, ...), custom_call_target="tpu_custom_call", output_to_operand_aliasing={{0}: (3, {}), {1}: (4, {}), {2}: (5, {}), {3}: (6, {}), {4}... | custom-call | flops 33333332 | bytes 7864320 | tf_op jit(solution)/shard_map/pallas_call | solution.py:650
Async XLA Ops:
  295.3 27.1 %collective-permute-start.3 = (f32[4,4,32,512]{3,2,1,0:T(8,128)}, f32[4,4,32,512]{3,2,1,0:T(8,128)}, u32[]{:S(2)}, u32[]{:S(2)}) collective-permute-start(f32[4,4,32,512]{3,2,1,0:T(8,128)} %get-tuple-element.95.refs_0_), channel_id=1, source_target_pairs={{0,8},{1,9},{2,10},{3,11},{4,12},{5,13},{6,14},{7,15},{8,0},{9,1},... | collective-permute-start | bytes 3145736 | tf_op jit(solution)/shard_map/ppermute | solution.py:699
  296.4 26.0 %collective-permute-start.4 = (f32[4,4,32,512]{3,2,1,0:T(8,128)}, f32[4,4,32,512]{3,2,1,0:T(8,128)}, u32[]{:S(2)}, u32[]{:S(2)}) collective-permute-start(f32[4,4,32,512]{3,2,1,0:T(8,128)} %get-tuple-element.96.refs_1_), channel_id=1, source_target_pairs={{0,2},{1,3},{2,0},{3,1},{4,6},{5,7},{6,4},{7,5},{8,10},{9,11},{10,... | collective-permute-start | bytes 3145736 | tf_op jit(solution)/shard_map/ppermute | solution.py:699
  296.9 25.5 %collective-permute-start.5 = (f32[4,4,32,512]{3,2,1,0:T(8,128)}, f32[4,4,32,512]{3,2,1,0:T(8,128)}, u32[]{:S(2)}, u32[]{:S(2)}) collective-permute-start(f32[4,4,32,512]{3,2,1,0:T(8,128)} %get-tuple-element.97.refs_2_), channel_id=1, source_target_pairs={{0,4},{1,5},{2,6},{3,7},{4,0},{5,1},{6,2},{7,3},{8,12},{9,13},{10,... | collective-permute-start | bytes 3145736 | tf_op jit(solution)/shard_map/ppermute | solution.py:699
  322.4 3.1 collective-permute-start.6
  322.9 15.4 %collective-permute-start.7 = (f32[4,4,32,512]{3,2,1,0:T(8,128)}, f32[4,4,32,512]{3,2,1,0:T(8,128)}, u32[]{:S(2)}, u32[]{:S(2)}) collective-permute-start(f32[4,4,32,512]{3,2,1,0:T(8,128)} %collective-permute-done.4.refs_1_), channel_id=1, source_target_pairs={{0,1},{1,0},{2,3},{3,2},{4,5},{5,4},{6,7},{7,6},{8,9},{9,8},{10,11... | collective-permute-start | bytes 3145736 | tf_op jit(solution)/shard_map/ppermute | solution.py:699
  323.0 15.4 %collective-permute-start.8 = (f32[4,4,32,512]{3,2,1,0:T(8,128)}, f32[4,4,32,512]{3,2,1,0:T(8,128)}, u32[]{:S(2)}, u32[]{:S(2)}) collective-permute-start(f32[4,4,32,512]{3,2,1,0:T(8,128)} %collective-permute-done.5.refs_2_), channel_id=1, source_target_pairs={{0,1},{1,0},{2,3},{3,2},{4,5},{5,4},{6,7},{7,6},{8,9},{9,8},{10,11... | collective-permute-start | bytes 3145736 | tf_op jit(solution)/shard_map/ppermute | solution.py:699
  323.4 25.0 %collective-permute-start = (f32[4,4,32,512]{3,2,1,0:T(8,128)}, f32[4,4,32,512]{3,2,1,0:T(8,128)}, u32[]{:S(2)}, u32[]{:S(2)}) collective-permute-start(f32[4,4,32,512]{3,2,1,0:T(8,128)} %get-tuple-element.92.refs_6_), channel_id=1, source_target_pairs={{0,8},{1,9},{2,10},{3,11},{4,12},{5,13},{6,14},{7,15},{8,0},{9,1},... | collective-permute-start | bytes 3145736 | tf_op jit(solution)/shard_map/ppermute | solution.py:699
  324.0 24.7 %collective-permute-start.1 = (f32[4,4,32,512]{3,2,1,0:T(8,128)}, f32[4,4,32,512]{3,2,1,0:T(8,128)}, u32[]{:S(2)}, u32[]{:S(2)}) collective-permute-start(f32[4,4,32,512]{3,2,1,0:T(8,128)} %get-tuple-element.93.refs_7_), channel_id=1, source_target_pairs={{0,2},{1,3},{2,0},{3,1},{4,6},{5,7},{6,4},{7,5},{8,10},{9,11},{10,... | collective-permute-start | bytes 3145736 | tf_op jit(solution)/shard_map/ppermute | solution.py:699
  325.6 24.7 %collective-permute-start.2 = (f32[4,4,32,512]{3,2,1,0:T(8,128)}, f32[4,4,32,512]{3,2,1,0:T(8,128)}, u32[]{:S(2)}, u32[]{:S(2)}) collective-permute-start(f32[4,4,32,512]{3,2,1,0:T(8,128)} %get-tuple-element.94.refs_8_), channel_id=1, source_target_pairs={{0,4},{1,5},{2,6},{3,7},{4,0},{5,1},{6,2},{7,3},{8,12},{9,13},{10,... | collective-permute-start | bytes 3145736 | tf_op jit(solution)/shard_map/ppermute | solution.py:699
  350.2 9.5 %collective-permute-start.9 = (f32[4,4,32,512]{3,2,1,0:T(8,128)}, f32[4,4,32,512]{3,2,1,0:T(8,128)}, u32[]{:S(2)}, u32[]{:S(2)}) collective-permute-start(f32[4,4,32,512]{3,2,1,0:T(8,128)} %collective-permute-done.refs_0_), channel_id=1, source_target_pairs={{0,1},{1,0},{2,3},{3,2},{4,5},{5,4},{6,7},{7,6},{8,9},{9,8},{10,11... | collective-permute-start | bytes 3145736 | tf_op jit(solution)/shard_map/ppermute | solution.py:699
  351.4 8.3 %collective-permute-start.10 = (f32[4,4,32,512]{3,2,1,0:T(8,128)}, f32[4,4,32,512]{3,2,1,0:T(8,128)}, u32[]{:S(2)}, u32[]{:S(2)}) collective-permute-start(f32[4,4,32,512]{3,2,1,0:T(8,128)} %collective-permute-done.1.refs_1_), channel_id=1, source_target_pairs={{0,1},{1,0},{2,3},{3,2},{4,5},{5,4},{6,7},{7,6},{8,9},{9,8},{10,11... | collective-permute-start | bytes 3145736 | tf_op jit(solution)/shard_map/ppermute | solution.py:699
  351.4 8.3 %collective-permute-start.11 = (f32[4,4,32,512]{3,2,1,0:T(8,128)}, f32[4,4,32,512]{3,2,1,0:T(8,128)}, u32[]{:S(2)}, u32[]{:S(2)}) collective-permute-start(f32[4,4,32,512]{3,2,1,0:T(8,128)} %collective-permute-done.2.refs_2_), channel_id=1, source_target_pairs={{0,1},{1,0},{2,3},{3,2},{4,5},{5,4},{6,7},{7,6},{8,9},{9,8},{10,11... | collective-permute-start | bytes 3145736 | tf_op jit(solution)/shard_map/ppermute | solution.py:699

commit v8 on v7

--- a/solution.py
+++ b/solution.py
@@ -462,9 +462,9 @@
 VMEM = 67043328
 
 
-def write_kernel(o_ref, ns, no, ni, n0, nm, so_ref, sv_ref, os_, oo, of, bs, bo, bf,
-                 vs, vo, vi, v0, vm, bn, vbn, wb,
-                 buf, bbuf, fbuf, fbbuf, vbuf, in_sem, f_sem, b_sem, v_sem):
+def write_kernel(o_ref, ns, no, ni, n0, nm, nf, so_ref, sv_ref, os_, oo, of, bs, bo, bf,
+                 vs, vo, vi, v0, vm, vf, bn, vbn, wb, vb,
+                 buf, bbuf, fbuf, fbbuf, vbuf, nbuf, across, line, flat, in_sem, f_sem, b_sem, v_sem, n_sem):
     def view(c, refs):
         entry, ref = [(e, r) for e, r in zip(TABLE, refs) if c >= e[0]][-1]
         i, row, col = unit_at(entry, c)
@@ -507,6 +507,38 @@
     v_ins, v_outs = moments((ns, no, ni, n0, nm), False), moments((vs, vo, vi, v0, vm), True)
     for d in v_ins:
         d.start()
+    nf_in = pltpu.make_async_copy(nf, nbuf.at[pl.ds(0, CLASSES)], n_sem)
+    nf_in.start()
+    nf_out = pltpu.make_async_copy(flat, vf, n_sem)
+
+    def flatten_fc():
+        period = 2 * SUB
+        rows_per = CLASSES * period // LANES
+        nbuf[CLASSES:, :] = jnp.zeros((SUB * LANES - CLASSES, LANES), F32)
+        across[SUB] = jnp.zeros((LANES, LANES), F32)
+        for b in range(SUB):
+            across[b] = nbuf[b * LANES:(b + 1) * LANES, :].T
+        live = {}
+        for r in range(period):
+            first, shift = divmod(CLASSES * r, LANES)
+            x = [across[b, pl.ds(r, SUB, stride=period), :] for b in range(SUB + 1)]
+            y = pltpu.roll(jnp.concatenate(x, axis=1), shift, 1)
+            for b in range(SUB + 1):
+                part = y[:, b * LANES:(b + 1) * LANES]
+                if first + b < rows_per:
+                    live[first + b] = live[first + b] + part if first + b in live else part
+            after = CLASSES * (r + 1) // LANES
+            for row in [k for k in live if k < after]:
+                flat[pl.ds(row, SUB, stride=rows_per), :] = live.pop(row)
+
+    width = vb.shape[1]
+    for i in range(SUB):
+        line[:, i * LANES:(i + 1) * LANES] = jnp.broadcast_to(sv_ref[SUB + i:SUB + i + 1, :], (SUB, LANES))
+    spread = (SUB * LANES, width)
+    chosen = (lax.broadcasted_iota(jnp.int32, spread, 1) + lax.axis_index('dp') * width
+              == lax.broadcasted_iota(jnp.int32, spread, 0))
+    own = jnp.dot(line[...], jnp.where(chosen, 1.0, 0.0), precision=lax.Precision.HIGHEST, preferred_element_type=F32)
+    vb[...] = own[0:1]
     bn[...] = so_ref[...]
     vbn[...] = sv_ref[0:SUB]
     for i in range(SUB):
@@ -537,34 +569,39 @@
                 d.wait()
             for d in v_outs:
                 d.start()
+            nf_in.wait()
+            flatten_fc()
+            nf_out.start()
         if i + AHEAD < TAIL0:
             settle(i + AHEAD - NBUF)
             for d in load(i + AHEAD):
                 d.start()
     settle(TAIL0 - 1)
+    nf_out.wait()
     for d in v_outs:
         d.wait()
 
 
-def run_write(o, moments_new, so, sv):
+def run_write(o, moments_new, so, sv, width):
     anyspec = pl.BlockSpec(memory_space=pl.ANY)
     vspec = pl.BlockSpec(memory_space=pltpu.VMEM)
     shapes = [dshape(*e, DEV) for e in TABLE[:2]] + [(CLASSES, DEV * LANES)]
-    moments = [(e[1] * e[2] * LANES, LANES) for e in TABLE]
+    moments = [(e[1] * e[2] * LANES, LANES) for e in TABLE] + [(CLASSES, LANES)]
     tile = (SUB, LANES)
     dma = pltpu.SemaphoreType.DMA
     outs = [(s, F32) for s in shapes] + [(s, BF16) for s in shapes] + [(s, F32) for s in moments]
-    outs += [((DEV,) + tile, F32), (tile, F32), ((1, CLASSES), F32)]
+    outs += [((DEV,) + tile, F32), (tile, F32), ((1, CLASSES), F32), ((1, width), F32)]
     return pl.pallas_call(
         write_kernel,
         out_shape=[jax.ShapeDtypeStruct(*s) for s in outs],
-        in_specs=[anyspec] * 6 + [vspec] * 2,
-        out_specs=[anyspec] * 11 + [vspec] * 3,
+        in_specs=[anyspec] * 7 + [vspec] * 2,
+        out_specs=[anyspec] * 12 + [vspec] * 4,
         scratch_shapes=[
             pltpu.VMEM((NBUF, DEV, U, CW), F32), pltpu.VMEM((NBUF, DEV, U, CW), BF16),
             pltpu.VMEM((NFC, LANES, DEV * LANES), F32), pltpu.VMEM((NFC, LANES, DEV * LANES), BF16),
-            pltpu.VMEM(((NCH - FCN) * LANES, LANES), F32),
-            dma((NBUF,)), dma((NBUF,)), dma((NBUF,)), dma],
+            pltpu.VMEM(((NCH - FCN) * LANES, LANES), F32), pltpu.VMEM((SUB * LANES, LANES), F32),
+            pltpu.VMEM((SUB + 1, LANES, LANES), F32), pltpu.VMEM((SUB, SUB * LANES), F32),
+            pltpu.VMEM((CLASSES, LANES), F32), dma((NBUF,)), dma((NBUF,)), dma((NBUF,)), dma, dma],
         compiler_params=pltpu.CompilerParams(vmem_limit_bytes=VMEM),
         cost_estimate=pl.CostEstimate(flops=WRITE_FLOPS, bytes_accessed=TAIL0 * 160 * U * CW, transcendentals=0),
         name='write_out',
@@ -672,7 +709,6 @@
     def body(w_in0, w_short, w_in, w_mid, w_out, w_fc, w_bn, w_bias,
              g_in0, g_short, g_in, g_mid, g_out, g_bn, pooled, dlogits,
              v_in0, v_short, v_in, v_mid, v_out, v_fc, v_bn, v_bias, learn_rate):
-        rank = lax.axis_index('dp')
         width = v_bias.shape[0]
         shapes = [dshape(*e, DEV) for e in TABLE]
         grads = [g.reshape(s) for g, s in zip((g_short, g_out, g_in, g_in0, g_mid), shapes)]
@@ -691,7 +727,7 @@
         tiles = (-1, SUB, LANES)
         small = [g_bn.reshape(tiles), w_bn.reshape(-1, LANES), v_bn.reshape(SUB, LANES),
                  w_bias.reshape(1, CLASSES), v_bias.reshape(1, width)]
-        o, *made, nf, so, sv = run_comm(
+        o, *made, so, sv = run_comm(
             learn_rate.reshape(1, 1), grads, pooled, dlogits.T, weights, moments, small)
         ts, us, made = made[:6], made[6:12], made[12:]
 
@@ -705,8 +741,8 @@
         rs = []
         for n, t in enumerate(ts):
             rs.append(across(t, 2 << (n + 2) % 3))
-        outs = run_write(o, [v.reshape(-1, LANES) for v in made], so, sv)
-        short, out, fc, short_b, out_b, fc_b, vs, vo, vi, v0, vm, bn, vbn, wb = outs
+        outs = run_write(o, [v.reshape(-1, LANES) for v in made], so, sv, width)
+        short, out, fc, short_b, out_b, fc_b, vs, vo, vi, v0, vm, vf, bn, vbn, wb, vb = outs
         mates, vbn = to_mates(rs[:3], vbn)
         tail = run_tail((0, 1), [(ts, 0, False), (us, 0, True)], None)
         *tail, token = run_tail((0,), [(rs, 4, False), (mates, 4, True)], tail)
@@ -715,13 +751,12 @@
         *tail, _ = run_tail((1,), [(mates + last, 4, True)], tail)
         inn, in0, mid, inn_b, in0_b, mid_b = tail
         news = [from_rows(v, e[1], old) for v, e, old in zip((vs, vo, vi, v0, vm), TABLE, olds)]
-        vb = sv[SUB:2 * SUB]
         return (in0.reshape(w_in0.shape), short.reshape(w_short.shape), inn.reshape(w_in.shape),
                 mid.reshape(w_mid.shape), out.reshape(w_out.shape), fc.T,
                 bn.reshape(w_bn.shape), wb.reshape(w_bias.shape),
                 in0_b.reshape(w_in0.shape), short_b.reshape(w_short.shape), inn_b.reshape(w_in.shape),
                 mid_b.reshape(w_mid.shape), out_b.reshape(w_out.shape), fc_b.T,
-                news[3], news[0], news[2], news[4], news[1], nf.T.reshape(v_fc.shape),
-                vbn.reshape(v_bn.shape), lax.dynamic_slice_in_dim(vb.reshape(-1), rank * width, width))
+                news[3], news[0], news[2], news[4], news[1], vf.reshape(v_fc.shape),
+                vbn.reshape(v_bn.shape), vb.reshape(v_bias.shape))
 
     return jax.shard_map(body, mesh=mesh, in_specs=in_specs, out_specs=out_specs, check_vma=False)

time: 364 us -> 362 us (level)
  local copies, waits for them, and re-layouts: 6.21 us -> 2.44 us
  transfers between devices with their start and end apart: 12 -> 12, of which waited for: 4 -> 5; matrix products, arithmetic and copies ran while one was open for 1% -> 0% of each run, Pallas kernels for 13% -> 13%
where the time goes in v8:
time: 362 us; the launch traced here: 361 us
  Pallas kernels  343 us (95%)
  starting transfers between devices  7.29 us (2%)
  waiting for transfers between devices  7.14 us (2%)
    pallas_call x1, Pallas kernels, run_comm(): pl.pallas_call(comm_kernel, out_shape=[jax.ShapeDtypeStruct(s, F32) for s...  292 us
    pallas_call x4, Pallas kernels, run_tail(): pl.pallas_call(functools.partial(tail_kernel, jobs, size, count, len(give...  26.5 us
    pallas_call x1, Pallas kernels, run_write(): pl.pallas_call(write_kernel, out_shape=[jax.ShapeDtypeStruct(*s) for s in...  25 us
    ppermute x12, starting transfers between devices, across(): return lax.ppermute(x, 'dp', [(i, i ^ weight) for i in range(DEV)])  7.29 us
  transfers between devices with their start and end apart: 12, of which 5 were waited for; matrix products, arithmetic and copies ran while one was open for 0% of the time, Pallas kernels for 13%

profile of v8, /device:TPU:1, one launch (start us, length us, event | category | flops | bytes accessed | tf_op | source)
XLA Modules:
  0.0 361.3 jit_solution(15221378500111265909)
XLA Ops:
  1.3 1.4 reshape.194
  2.8 1.0 copy.71
  3.7 291.5 %lars_comm.1 = (f32[24,16,32,512]{3,2,1,0:T(8,128)}, f32[4,4,32,512]{3,2,1,0:T(8,128)}, f32[4,4,32,512]{3,2,1,0:T(8,128)}, f32[4,4,32,512]{3,2,1,0:T(8,128)}, f3...) custom-call(f32[1,1]{1,0:T(1,128)} %bitcast.67.lr_ref, ...), custom_call_target="tpu_custom_call" | custom-call | tf_op jit(solution)/shard_map/lars_comm/pallas_call | solution.py:439
  295.3 1.1 collective-permute-start.3
  296.4 0.5 collective-permute-start.4
  296.9 0.7 collective-permute-start.5
  297.6 25.0 %write_out.1 = (f32[1,16,64,2048]{3,2,1,0:T(8,128)}, f32[2,16,32,2048]{3,2,1,0:T(8,128)}, f32[1000,2048]{1,0:T(8,128)}, bf16[1,16,64,2048]{3,2,1,0:T(8,128)(2,1)...) custom-call(f32[24,16,32,512]{3,2,1,0:T(8,128)} %get-tuple-element.1, ...), custom_call_target="tpu_custom_call" | custom-call | flops 100000000 | bytes 62914560 | tf_op jit(solution)/shard_map/write_out/pallas_call | solution.py:594
  322.6 0.0 collective-permute-done.3.refs_0_
  322.6 0.0 collective-permute-done.4.refs_1_
  322.7 0.0 collective-permute-done.5.refs_2_
  322.7 0.5 collective-permute-start.6
  323.2 0.1 collective-permute-start.7
  323.2 0.5 collective-permute-start.8
  323.7 0.5 collective-permute-start
  324.2 0.9 collective-permute-start.1
  325.1 0.7 collective-permute-done.6.refs_3_
  325.8 0.7 collective-permute-start.2
  326.5 12.1 %shard_map.408 = (f32[1,16,128,512]{3,2,1,0:T(8,128)}, f32[1,16,64,512]{3,2,1,0:T(8,128)}, f32[2,16,288,512]{3,2,1,0:T(8,128)}, bf16[1,16,128,512]{3,2,1,0:T(8,1...) custom-call(f32[4,4,32,512]{3,2,1,0:T(8,128)} %get-tuple-element.97.refs_0_, ...), custom_call_target="tpu_custom_call" | custom-call | flops 33333332 | bytes 31457280 | tf_op jit(solution)/shard_map/pallas_call | solution.py:687
  338.6 0.0 collective-permute-done.7.refs_4_
  338.6 0.0 collective-permute-done.8.refs_5_
  338.6 6.5 %shard_map.409 = (f32[1,16,128,512]{3,2,1,0:T(8,128)}, f32[1,16,64,512]{3,2,1,0:T(8,128)}, f32[2,16,288,512]{3,2,1,0:T(8,128)}, bf16[1,16,128,512]{3,2,1,0:T(8,1...) custom-call(f32[4,4,32,512]{3,2,1,0:T(8,128)} %collective-permute-do, ...), custom_call_target="tpu_custom_call", output_to_operand_aliasing={{0}: (6, {}), {1}: (7, {}), {2}: (8, {}), {3}: (9, {}), {4}... | custom-call | flops 33333332 | bytes 15728640 | tf_op jit(solution)/shard_map/pallas_call | solution.py:687
  345.1 3.6 collective-permute-done.refs_0_
  348.7 0.2 collective-permute-done.1.refs_1_
  348.9 1.6 collective-permute-done.2.refs_2_
  350.5 1.2 collective-permute-start.9
  351.7 0.0 collective-permute-start.10
  351.7 0.5 collective-permute-start.11
  352.2 4.0 %shard_map.410 = (f32[1,16,128,512]{3,2,1,0:T(8,128)}, f32[1,16,64,512]{3,2,1,0:T(8,128)}, f32[2,16,288,512]{3,2,1,0:T(8,128)}, bf16[1,16,128,512]{3,2,1,0:T(8,1...) custom-call(f32[4,4,32,512]{3,2,1,0:T(8,128)} %collective-permute-do, ...), custom_call_target="tpu_custom_call", output_to_operand_aliasing={{0}: (3, {}), {1}: (4, {}), {2}: (5, {}), {3}: (6, {}), {4}... | custom-call | flops 33333332 | bytes 7864320 | tf_op jit(solution)/shard_map/pallas_call | solution.py:687
  356.2 0.0 collective-permute-done.9.refs_0_
  356.2 0.0 collective-permute-done.10.refs_1_
  356.3 1.1 collective-permute-done.11.refs_2_
  357.3 4.0 %shard_map.411 = (f32[1,16,128,512]{3,2,1,0:T(8,128)}, f32[1,16,64,512]{3,2,1,0:T(8,128)}, f32[2,16,288,512]{3,2,1,0:T(8,128)}, bf16[1,16,128,512]{3,2,1,0:T(8,1...) custom-call(f32[4,4,32,512]{3,2,1,0:T(8,128)} %collective-permute-do, ...), custom_call_target="tpu_custom_call", output_to_operand_aliasing={{0}: (3, {}), {1}: (4, {}), {2}: (5, {}), {3}: (6, {}), {4}... | custom-call | flops 33333332 | bytes 7864320 | tf_op jit(solution)/shard_map/pallas_call | solution.py:687
Async XLA Ops:
  295.3 27.4 %collective-permute-start.3 = (f32[4,4,32,512]{3,2,1,0:T(8,128)}, f32[4,4,32,512]{3,2,1,0:T(8,128)}, u32[]{:S(2)}, u32[]{:S(2)}) collective-permute-start(f32[4,4,32,512]{3,2,1,0:T(8,128)} %get-tuple-element.97.refs_0_), channel_id=1, source_target_pairs={{0,8},{1,9},{2,10},{3,11},{4,12},{5,13},{6,14},{7,15},{8,0},{9,1},... | collective-permute-start | bytes 3145736 | tf_op jit(solution)/shard_map/ppermute | solution.py:735
  296.4 26.2 %collective-permute-start.4 = (f32[4,4,32,512]{3,2,1,0:T(8,128)}, f32[4,4,32,512]{3,2,1,0:T(8,128)}, u32[]{:S(2)}, u32[]{:S(2)}) collective-permute-start(f32[4,4,32,512]{3,2,1,0:T(8,128)} %get-tuple-element.98.refs_1_), channel_id=1, source_target_pairs={{0,2},{1,3},{2,0},{3,1},{4,6},{5,7},{6,4},{7,5},{8,10},{9,11},{10,... | collective-permute-start | bytes 3145736 | tf_op jit(solution)/shard_map/ppermute | solution.py:735
  296.9 25.8 %collective-permute-start.5 = (f32[4,4,32,512]{3,2,1,0:T(8,128)}, f32[4,4,32,512]{3,2,1,0:T(8,128)}, u32[]{:S(2)}, u32[]{:S(2)}) collective-permute-start(f32[4,4,32,512]{3,2,1,0:T(8,128)} %get-tuple-element.99.refs_2_), channel_id=1, source_target_pairs={{0,4},{1,5},{2,6},{3,7},{4,0},{5,1},{6,2},{7,3},{8,12},{9,13},{10,... | collective-permute-start | bytes 3145736 | tf_op jit(solution)/shard_map/ppermute | solution.py:735
  322.7 3.1 collective-permute-start.6
  323.2 15.4 %collective-permute-start.7 = (f32[4,4,32,512]{3,2,1,0:T(8,128)}, f32[4,4,32,512]{3,2,1,0:T(8,128)}, u32[]{:S(2)}, u32[]{:S(2)}) collective-permute-start(f32[4,4,32,512]{3,2,1,0:T(8,128)} %collective-permute-done.4.refs_1_), channel_id=1, source_target_pairs={{0,1},{1,0},{2,3},{3,2},{4,5},{5,4},{6,7},{7,6},{8,9},{9,8},{10,11... | collective-permute-start | bytes 3145736 | tf_op jit(solution)/shard_map/ppermute | solution.py:735
  323.2 15.4 %collective-permute-start.8 = (f32[4,4,32,512]{3,2,1,0:T(8,128)}, f32[4,4,32,512]{3,2,1,0:T(8,128)}, u32[]{:S(2)}, u32[]{:S(2)}) collective-permute-start(f32[4,4,32,512]{3,2,1,0:T(8,128)} %collective-permute-done.5.refs_2_), channel_id=1, source_target_pairs={{0,1},{1,0},{2,3},{3,2},{4,5},{5,4},{6,7},{7,6},{8,9},{9,8},{10,11... | collective-permute-start | bytes 3145736 | tf_op jit(solution)/shard_map/ppermute | solution.py:735
  323.7 25.0 %collective-permute-start = (f32[4,4,32,512]{3,2,1,0:T(8,128)}, f32[4,4,32,512]{3,2,1,0:T(8,128)}, u32[]{:S(2)}, u32[]{:S(2)}) collective-permute-start(f32[4,4,32,512]{3,2,1,0:T(8,128)} %get-tuple-element.94.refs_6_), channel_id=1, source_target_pairs={{0,8},{1,9},{2,10},{3,11},{4,12},{5,13},{6,14},{7,15},{8,0},{9,1},... | collective-permute-start | bytes 3145736 | tf_op jit(solution)/shard_map/ppermute | solution.py:735
  324.2 24.7 %collective-permute-start.1 = (f32[4,4,32,512]{3,2,1,0:T(8,128)}, f32[4,4,32,512]{3,2,1,0:T(8,128)}, u32[]{:S(2)}, u32[]{:S(2)}) collective-permute-start(f32[4,4,32,512]{3,2,1,0:T(8,128)} %get-tuple-element.95.refs_7_), channel_id=1, source_target_pairs={{0,2},{1,3},{2,0},{3,1},{4,6},{5,7},{6,4},{7,5},{8,10},{9,11},{10,... | collective-permute-start | bytes 3145736 | tf_op jit(solution)/shard_map/ppermute | solution.py:735
  325.8 24.7 %collective-permute-start.2 = (f32[4,4,32,512]{3,2,1,0:T(8,128)}, f32[4,4,32,512]{3,2,1,0:T(8,128)}, u32[]{:S(2)}, u32[]{:S(2)}) collective-permute-start(f32[4,4,32,512]{3,2,1,0:T(8,128)} %get-tuple-element.96.refs_8_), channel_id=1, source_target_pairs={{0,4},{1,5},{2,6},{3,7},{4,0},{5,1},{6,2},{7,3},{8,12},{9,13},{10,... | collective-permute-start | bytes 3145736 | tf_op jit(solution)/shard_map/ppermute | solution.py:735
  350.5 5.8 %collective-permute-start.9 = (f32[4,4,32,512]{3,2,1,0:T(8,128)}, f32[4,4,32,512]{3,2,1,0:T(8,128)}, u32[]{:S(2)}, u32[]{:S(2)}) collective-permute-start(f32[4,4,32,512]{3,2,1,0:T(8,128)} %collective-permute-done.refs_0_), channel_id=1, source_target_pairs={{0,1},{1,0},{2,3},{3,2},{4,5},{5,4},{6,7},{7,6},{8,9},{9,8},{10,11... | collective-permute-start | bytes 3145736 | tf_op jit(solution)/shard_map/ppermute | solution.py:735
  351.7 4.5 %collective-permute-start.10 = (f32[4,4,32,512]{3,2,1,0:T(8,128)}, f32[4,4,32,512]{3,2,1,0:T(8,128)}, u32[]{:S(2)}, u32[]{:S(2)}) collective-permute-start(f32[4,4,32,512]{3,2,1,0:T(8,128)} %collective-permute-done.1.refs_1_), channel_id=1, source_target_pairs={{0,1},{1,0},{2,3},{3,2},{4,5},{5,4},{6,7},{7,6},{8,9},{9,8},{10,11... | collective-permute-start | bytes 3145736 | tf_op jit(solution)/shard_map/ppermute | solution.py:735
  351.7 5.6 %collective-permute-start.11 = (f32[4,4,32,512]{3,2,1,0:T(8,128)}, f32[4,4,32,512]{3,2,1,0:T(8,128)}, u32[]{:S(2)}, u32[]{:S(2)}) collective-permute-start(f32[4,4,32,512]{3,2,1,0:T(8,128)} %collective-permute-done.2.refs_2_), channel_id=1, source_target_pairs={{0,1},{1,0},{2,3},{3,2},{4,5},{5,4},{6,7},{7,6},{8,9},{9,8},{10,11... | collective-permute-start | bytes 3145736 | tf_op jit(solution)/shard_map/ppermute | solution.py:735
